TPU v7x, 32 devices: a whole 2x2x4 slice. The times are simulated.
32 devices in a mesh: dp: 8 (over y, x, core), head: 4 (over z).
Axes of the slice: x: 2, y: 2, z: 4, core: 2. Of those that a mesh axis runs over, the one named last changes fastest.
Arguments:
- tokens: bfloat16 [32768, 768], P(('dp', 'head')), may hold values from -6 to 6
- span_mask: int32 [32768], P(('dp', 'head')), may hold values from 0 to 1, as said below
- valid_mask: int32 [32768], P(('dp', 'head')), may hold values from 0 to 1, as said below
- mask_embedding: bfloat16 [768], replicated, may hold values from -6 to 6
- qkv_weight: bfloat16 [768, 3, 768], P(None, None, 'head'), may hold values from -0.3125 to 0.3125
- query_bias: bfloat16 [768], P('head'), may hold values from -3 to 3
- value_bias: bfloat16 [768], P('head'), may hold values from -3 to 3
- out_weight: bfloat16 [768, 768], replicated, may hold values from -0.875 to 0.875
- out_bias: float32 [768], replicated, may hold values from -3 to 3
- norm1_gain: float32 [768], replicated, may hold values from 0.5 to 1.5
- norm1_bias: float32 [768], replicated, may hold values from -3 to 3
- up_weight: bfloat16 [768, 3072], replicated, may hold values from -0.21875 to 0.21875
- up_bias: float32 [3072], replicated, may hold values from -3 to 3
- down_weight: bfloat16 [3072, 768], replicated, may hold values from -0.109375 to 0.109375
- down_bias: float32 [768], replicated, may hold values from -3 to 3
- norm2_gain: float32 [768], replicated, may hold values from 0.5 to 1.5
- norm2_bias: float32 [768], replicated, may hold values from -3 to 3
- out_grad: bfloat16 [32768, 768], P(('dp', 'head')), may hold values from -6 to 6
Outputs:
- output: bfloat16 [32768, 768], P(('dp', 'head'))
- tokens_grad: float32 [32768, 768], P(('dp', 'head'))
- mask_embedding_grad: float32 [768], replicated
- qkv_weight_grad: float32 [768, 3, 768], P(None, None, 'head')
- query_bias_grad: float32 [768], P('head')
- value_bias_grad: float32 [768], P('head')
- out_weight_grad: float32 [768, 768], replicated
- out_bias_grad: float32 [768], replicated
- norm1_gain_grad: float32 [768], replicated
- norm1_bias_grad: float32 [768], replicated
- up_weight_grad: float32 [768, 3072], replicated
- up_bias_grad: float32 [3072], replicated
- down_weight_grad: float32 [3072, 768], replicated
- down_bias_grad: float32 [768], replicated
- norm2_gain_grad: float32 [768], replicated
- norm2_bias_grad: float32 [768], replicated
- stream_rms: float32 [3], replicated
Inputs may be any that keep to these rules, and one draw needn't show every extreme that they name: `span_mask`: 1 marks a token inside a masked span; spans lie within one row of 512 tokens. `valid_mask`: 1 marks a token whose output gradient counts.
All inputs are finite; a program needn't handle non-finite values.
Results may differ from a plain program's by a relative error of at most 0.017.
Values may be sent and summed in bfloat16 or wider, within the bound.
A program may use at most 192 MiB of HBM per device.

v0:
```python
import math

import jax
import jax.numpy as jnp
from jax import lax
from jax.sharding import PartitionSpec as P

HEAD_DIM = 64
LEN = 512


eps_norm = 1e-12


def contract_rows(left, right):
    return lax.dot_general(
        left, right, (((0,), (0,)), ((), ())), preferred_element_type=jnp.float32
    )


def contract_last(left, right):
    return lax.dot_general(
        left, right, (((1,), (1,)), ((), ())), preferred_element_type=jnp.float32
    )


def norm_forward(hidden, gain, bias):
    center = hidden - jnp.mean(hidden, axis=-1, keepdims=True)
    inverse = lax.rsqrt(jnp.mean(center * center, axis=-1, keepdims=True) + eps_norm)
    normal = center * inverse
    return (normal * gain + bias, normal, inverse)


def norm_backward(upstream, normal, inverse, gain):
    gain_grad = jnp.sum(upstream * normal, axis=0)
    bias_grad = jnp.sum(upstream, axis=0)
    scaled = upstream * gain
    hidden_grad = inverse * (
        scaled
        - jnp.mean(scaled, axis=-1, keepdims=True)
        - normal * jnp.mean(scaled * normal, axis=-1, keepdims=True)
    )
    return (hidden_grad, gain_grad, bias_grad)


def gelu_exact(values):
    return 0.5 * values * (1.0 + jax.scipy.special.erf(values / math.sqrt(2.0)))


def gelu_slope(values):
    return 0.5 * (1.0 + jax.scipy.special.erf(values / math.sqrt(2.0))) + values * jnp.exp(
        -0.5 * values * values
    ) / math.sqrt(2.0 * math.pi)


def project(rows, weight, first_bias, third_bias):
    columns = weight.shape[2]
    projected = jnp.dot(
        rows, weight.reshape(weight.shape[0], 3 * columns), preferred_element_type=jnp.float32
    )
    queries = (projected[:, :columns] + first_bias).astype(jnp.bfloat16)
    key_low = projected[:, columns : 2 * columns].astype(jnp.bfloat16)
    values = (projected[:, 2 * columns :] + third_bias).astype(jnp.bfloat16)
    return (queries, key_low, values)


def attend_forward(queries, key_low, values):
    scaling = 1.0 / math.sqrt(HEAD_DIM)

    def single(blocks):
        query_block, key_block, value_block = blocks
        scores = (
            jnp.einsum("qhd,khd->hqk", query_block, key_block, preferred_element_type=jnp.float32)
            * scaling
        )
        highest = jnp.max(scores, axis=-1, keepdims=True)
        exponent = jnp.exp(scores - highest)
        totals = jnp.sum(exponent, axis=-1, keepdims=True)
        probabilities = (exponent / totals).astype(jnp.bfloat16)
        context = jnp.einsum(
            "hqk,khd->qhd", probabilities, value_block, preferred_element_type=jnp.float32
        )
        return (context.astype(jnp.bfloat16), (highest + jnp.log(totals))[..., 0])

    return lax.map(single, (queries, key_low, values))


def attend_backward(queries, key_low, values, logsum, context_grad):
    scaling = 1.0 / math.sqrt(HEAD_DIM)

    def single(blocks):
        query_block, key_block, value_block, lse_block, grad_block = blocks
        scores = (
            jnp.einsum("qhd,khd->hqk", query_block, key_block, preferred_element_type=jnp.float32)
            * scaling
        )
        probabilities = jnp.exp(scores - lse_block[..., None])
        prob_grad = jnp.einsum(
            "qhd,khd->hqk", grad_block, value_block, preferred_element_type=jnp.float32
        )
        correction = jnp.sum(probabilities * prob_grad, axis=-1, keepdims=True)
        score_grad = (probabilities * (prob_grad - correction)).astype(jnp.bfloat16)
        grad_query = (
            jnp.einsum("hqk,khd->qhd", score_grad, key_block, preferred_element_type=jnp.float32)
            * scaling
        )
        grad_key = (
            jnp.einsum("hqk,qhd->khd", score_grad, query_block, preferred_element_type=jnp.float32)
            * scaling
        )
        grad_value = jnp.einsum(
            "hqk,qhd->khd",
            probabilities.astype(jnp.bfloat16),
            grad_block,
            preferred_element_type=jnp.float32,
        )
        return (
            grad_query.astype(jnp.bfloat16),
            grad_key.astype(jnp.bfloat16),
            grad_value.astype(jnp.bfloat16),
        )

    return lax.map(single, (queries, key_low, values, logsum, context_grad))


def body(
    tokens,
    span_mask,
    valid_mask,
    mask_embedding,
    qkv_weight,
    query_bias,
    value_bias,
    out_weight,
    out_bias,
    norm1_gain,
    norm1_bias,
    up_weight,
    up_bias,
    down_weight,
    down_bias,
    norm2_gain,
    norm2_bias,
    out_grad,
):
    features = tokens.shape[1]
    masked = (span_mask == 1)[:, None]
    inputs = jnp.where(masked, mask_embedding[None, :], tokens)
    inputs_wide = inputs.astype(jnp.float32)
    validity = valid_mask.astype(jnp.float32)[:, None]
    gathered = lax.all_gather(inputs, "head", axis=0, tiled=True)
    weight, first_bias, third_bias = (qkv_weight, query_bias, value_bias)
    columns = weight.shape[2]
    row_total = gathered.shape[0]
    blocked = (row_total // LEN, LEN, columns // HEAD_DIM, HEAD_DIM)
    queries, key_low, values = project(gathered, weight, first_bias, third_bias)
    queries = queries.reshape(blocked)
    key_low = key_low.reshape(blocked)
    values = values.reshape(blocked)
    context, logsum = attend_forward(queries, key_low, values)
    context = context.reshape(row_total, columns)
    context = lax.all_to_all(context, "head", split_axis=0, concat_axis=1, tiled=True)
    attended = jnp.dot(context, out_weight, preferred_element_type=jnp.float32) + out_bias
    normed, normal_first, inverse_first = norm_forward(
        inputs_wide + attended, norm1_gain, norm1_bias
    )
    normed_low = normed.astype(jnp.bfloat16)
    preact = jnp.dot(normed_low, up_weight, preferred_element_type=jnp.float32) + up_bias
    activated = gelu_exact(preact).astype(jnp.bfloat16)
    feedout = jnp.dot(activated, down_weight, preferred_element_type=jnp.float32) + down_bias
    result, normal_second, inverse_second = norm_forward(normed + feedout, norm2_gain, norm2_bias)
    grad_output = out_grad.astype(jnp.float32) * validity
    grad_second, gain_second_grad, bias_second_grad = norm_backward(
        grad_output, normal_second, inverse_second, norm2_gain
    )
    grad_feed = grad_second.astype(jnp.bfloat16)
    down_bias_grad = jnp.sum(grad_feed, axis=0, dtype=jnp.float32)
    down_weight_grad = contract_rows(activated, grad_feed)
    grad_preact = (contract_last(grad_feed, down_weight) * gelu_slope(preact)).astype(jnp.bfloat16)
    up_bias_grad = jnp.sum(grad_preact, axis=0, dtype=jnp.float32)
    up_weight_grad = contract_rows(normed_low, grad_preact)
    grad_normed = contract_last(grad_preact, up_weight) + grad_second
    grad_first, gain_first_grad, bias_first_grad = norm_backward(
        grad_normed, normal_first, inverse_first, norm1_gain
    )
    grad_attended = grad_first.astype(jnp.bfloat16)
    out_bias_grad = jnp.sum(grad_attended, axis=0, dtype=jnp.float32)
    out_weight_grad = contract_rows(context, grad_attended)
    context_grad = contract_last(grad_attended, out_weight).astype(jnp.bfloat16)
    context_grad = lax.all_to_all(context_grad, "head", split_axis=1, concat_axis=0, tiled=True)
    grad_query, grad_key, grad_value = attend_backward(
        queries, key_low, values, logsum, context_grad.reshape(blocked)
    )
    grad_query = grad_query.reshape(row_total, columns)
    grad_value = grad_value.reshape(row_total, columns)
    grad_joined = jnp.concatenate(
        [grad_query, grad_key.reshape(row_total, columns), grad_value], axis=1
    )
    weight_grad = contract_rows(gathered, grad_joined).reshape(features, 3, columns)
    first_grad = jnp.sum(grad_query, axis=0, dtype=jnp.float32)
    third_grad = jnp.sum(grad_value, axis=0, dtype=jnp.float32)
    input_part = contract_last(grad_joined, weight.reshape(features, 3 * columns))
    input_attn = lax.psum_scatter(
        input_part.astype(jnp.bfloat16), "head", scatter_dimension=0, tiled=True
    ).astype(jnp.float32)
    weight_grad, first_grad, third_grad = lax.psum((weight_grad, first_grad, third_grad), "dp")
    grad_inputs = input_attn + grad_first
    tokens_grad = jnp.where(masked, 0.0, grad_inputs)
    embedding_grad = jnp.sum(jnp.where(masked, grad_inputs, 0.0), axis=0)
    squares = jnp.stack(
        [
            jnp.sum(validity * inputs_wide * inputs_wide),
            jnp.sum(validity * attended * attended),
            jnp.sum(validity * feedout * feedout),
            jnp.sum(validity),
        ]
    )
    (
        out_weight_grad,
        out_bias_grad,
        gain_first_grad,
        bias_first_grad,
        down_bias_grad,
        gain_second_grad,
        bias_second_grad,
        embedding_grad,
        squares,
    ) = lax.psum(
        (
            out_weight_grad,
            out_bias_grad,
            gain_first_grad,
            bias_first_grad,
            down_bias_grad,
            gain_second_grad,
            bias_second_grad,
            embedding_grad,
            squares,
        ),
        ("dp", "head"),
    )
    share_up, share_down, share_bias = (
        lax.psum_scatter(up_weight_grad, ("dp", "head"), scatter_dimension=1, tiled=True),
        lax.psum_scatter(down_weight_grad, ("dp", "head"), scatter_dimension=0, tiled=True),
        lax.psum_scatter(up_bias_grad, ("dp", "head"), scatter_dimension=0, tiled=True),
    )
    up_weight_grad, down_weight_grad, up_bias_grad = (
        lax.all_gather(share_up.astype(jnp.bfloat16), ("dp", "head"), axis=1, tiled=True).astype(
            share_up.dtype
        ),
        lax.all_gather(share_down.astype(jnp.bfloat16), ("dp", "head"), axis=0, tiled=True).astype(
            share_down.dtype
        ),
        lax.all_gather(share_bias.astype(jnp.bfloat16), ("dp", "head"), axis=0, tiled=True).astype(
            share_bias.dtype
        ),
    )
    count = jnp.maximum(squares[3], 1.0)
    stream_rms = jnp.sqrt(squares[:3] / (count * features))
    return (
        result.astype(jnp.bfloat16),
        tokens_grad,
        embedding_grad,
        weight_grad,
        first_grad,
        third_grad,
        out_weight_grad,
        out_bias_grad,
        gain_first_grad,
        bias_first_grad,
        up_weight_grad,
        up_bias_grad,
        down_weight_grad,
        down_bias_grad,
        gain_second_grad,
        bias_second_grad,
        stream_rms,
    )


def solution(mesh):
    placed = (
        P(("dp", "head"), None),
        P(("dp", "head")),
        P(("dp", "head")),
        P(),
        P(None, None, "head"),
        P("head"),
        P("head"),
        P(),
        P(),
        P(),
        P(),
        P(),
        P(),
        P(),
        P(),
        P(),
        P(),
        P(("dp", "head"), None),
    )
    return jax.shard_map(
        body,
        mesh=mesh,
        in_specs=placed,
        out_specs=(
            P(("dp", "head"), None),
            P(("dp", "head"), None),
            P(),
            P(None, None, "head"),
            P("head"),
            P("head"),
            P(),
            P(),
            P(),
            P(),
            P(),
            P(),
            P(),
            P(),
            P(),
            P(),
            P(),
        ),
        check_vma=False,
    )
```

profile of v0, /device:TPU:0, one launch (start us, length us, event | category | flops | bytes accessed | tf_op | source)
XLA Modules:
  0.0 1031.4 jit_solution(12730927988103087368)
XLA Ops:
  10.5 118.2 %all-gather.4.cloned.1.call-done = bf16[4096,768]{0,1:T(8,128)(2,1)} async-done(((bf16[1024,768]{0,1:T(8,128)(2,1)}), bf16[4096,768]{0,1:T(8,128)(2,1)}) %all-gather.4.cloned.1.call-update) | async-done | bytes 6291472 | tf_op jit(solution)/shard_map/all_gather | solution.py:151
  128.7 6.1 fusion.86
  144.2 36.8 %while.26 = (s32[]{:T(128)}, bf16[8,512,3,64]{1,3,2,0:T(8,128)(2,1)}, f32[8,3,512]{2,1,0:T(4,128)S(1)}, bf16[8,512,3,64]{1,3,2,0:T(8,128)(2,1)}, bf16[8,512,3,64...) while((s32[]{:T(128)}, bf16[8,512,3,64]{1,3,2,0:T(8,128)(2,1)}, ...), condition=%wide.region_3.4_spmd, body=%wide.region_0.3_spmd.sunk | while | flops 208501248 | bytes 10281049 | solution.py:85
  146.4 2.4 fusion.126
  151.0 2.4 fusion.126
  155.6 2.4 fusion.126
  160.2 2.4 fusion.126
  164.8 2.4 fusion.126
  169.4 2.4 fusion.126
  174.0 2.4 fusion.126
  178.6 2.4 fusion.126
  181.0 3.4 copy.86
  184.4 3.7 all_to_all.26
  188.2 3.0 copy.87
  191.2 4.5 all-to-all-start
  196.0 2.6 copy.89
  198.5 34.6 %all-to-all-done = bf16[4,1024,192]{1,2,0:T(8,128)(2,1)} async-done(((bf16[4,1024,192]{1,2,0:T(8,128)(2,1)}), bf16[4,1024,192]{1,2,0:T(8,128)(2,1)}, u32[]{:S(2)}, u32[]{:S(2)}) %all-to-all-start) | async-done | bytes 1572896 | tf_op jit(solution)/shard_map/all_to_all | solution.py:162
  233.2 3.7 fusion.83
  237.7 11.2 %multiply_convert_fusion.1 = (bf16[1024,3072]{1,0:T(8,128)(2,1)}, f32[1024,3072]{1,0:T(8,128)}) fusion(f32[3072]{0:T(1024)S(1)} %copy-done.23, bf16[768,3072]{1,0:T(8,128)(2,1)S(1)} %bitcast.186, f32[1024,768]{0,1:T(8,128)S(1)} %get-tuple-element.263, f32[768]{0:T(1024)S(1)} %copy-done.24, f32[768]{0:T(1024)S(1)} %copy-done.20, ...), kind=kOutput, calls=%fused_computation.68 | convolution fusion | flops 4854644736 | bytes 26765312 | tf_op jit(solution)/shard_map/dot_general | solution.py:168
  249.0 9.0 fusion.82
  258.5 2.1 copy-done.3
  260.6 4.3 fusion.63
  264.9 2.9 convert_reduce_fusion.1
  267.8 12.3 %convert_reduce_fusion = (f32[3072]{0:T(1024)S(1)}, bf16[1024,3072]{1,0:T(8,128)(2,1)S(1)}) fusion(f32[1024,3072]{1,0:T(8,128)} %get-tuple-element.274, f32[3072]{0:T(1024)S(1)} %copy-done.23, bf16[1024,768]{0,1:T(8,128)(2,1)S(1)} %get-tuple-element.259, bf16[3072,768]{1,0:T(8,128)(2,1)S(1)} %bitcast.184), kind=kOutput, calls=%fused_computation.67 | convolution fusion | flops 4872729600 | bytes 25190400 | tf_op jit(solution)/shard_map/dot_general | solution.py:22
  280.1 2.7 copy-done.27
  282.8 8.4 fusion.77
  292.7 12.1 %multiply_reduce_fusion.3 = (f32[768]{0:T(1024)S(1)}, f32[1024]{0:T(1024)S(1)}, f32[1024]{0:T(1024)S(1)}, f32[768]{0:T(1024)S(1)}, f32[1024,768]{0,1:T(8,128)S(1)}) fusion(f32[1024,768]{0,1:T(8,128)} %copy-done.6, f32[1024]{0:T(1024)S(1)} %add_rsqrt_fusion.1, f32[1024]{0:T(1024)S(1)} %broadcast_multiply_fusion.5, f32[768]{0:T(1024)S(1)} %copy-done.20, ...), kind=kOutput, calls=%fused_computation.85 | convolution fusion | flops 4846776320 | bytes 22069248 | tf_op jit(solution)/shard_map/dot_general | solution.py:22
  305.6 2.6 convolution_convert_fusion.1
  308.1 3.7 all-to-all-start.1
  311.9 10.4 %fusion.85 = f32[3072,768]{1,0:T(8,128)} fusion(bf16[1024,3072]{1,0:T(8,128)(2,1)} %get-tuple-element.273, bf16[1024,768]{0,1:T(8,128)(2,1)S(1)} %copy-done.11), kind=kOutput, calls=%fused_computation.137 | convolution fusion | flops 4831838208 | bytes 17301504 | tf_op jit(solution)/shard_map/dot_general | solution.py:16
  322.4 36.1 %all-to-all-done.1 = bf16[1024,4,192]{0,2,1:T(8,128)(2,1)S(1)} async-done(((bf16[1024,4,192]{0,2,1:T(8,128)(2,1)}), bf16[1024,4,192]{0,2,1:T(8,128)(2,1)S(1)}, u32[]{:S(2)}, u32[]{:S(2)}) %all-to-all-start.1) | async-done | bytes 1572896 | tf_op jit(solution)/shard_map/all_to_all | solution.py:190
  363.6 76.2 %while.27 = (s32[]{:T(128)}, bf16[8,512,3,64]{1,3,2,0:T(8,128)(2,1)S(1)}, bf16[8,512,3,64]{1,3,2,0:T(8,128)(2,1)}, bf16[8,512,3,64]{1,3,2,0:T(8,128)(2,1)S(1)}, ...) while((s32[]{:T(128)}, ...), condition=%wide.region_14.15_spmd, body=%wide.region_12.14_spmd.sunk | while | flops 513243648 | bytes 25609328 | solution.py:123
  369.3 2.2 fusion.137
  374.8 1.9 multiply_reduce_fusion.12
  378.9 2.2 fusion.137
  384.4 1.9 multiply_reduce_fusion.12
  388.4 2.2 fusion.137
  398.0 2.2 fusion.137
  403.5 1.9 multiply_reduce_fusion.12
  407.5 2.2 fusion.137
  417.0 2.2 fusion.137
  422.5 1.8 multiply_reduce_fusion.12
  426.5 2.2 fusion.137
  432.0 1.8 multiply_reduce_fusion.12
  436.0 2.2 fusion.137
  445.0 2.2 copy-done.12
  447.1 7.2 convolution_convert_fusion
  456.4 116.0 %reduce-scatter.8.cloned.1.call-done = f32[96,768]{1,0:T(8,128)} async-done(((f32[3072,768]{1,0:T(8,128)}), f32[96,768]{1,0:T(8,128)}) %reduce-scatter.8.cloned.1.call-update) | async-done | bytes 294928 | tf_op jit(solution)/shard_map/reduce_scatter | solution.py:244
  574.1 5.2 fusion.74
  579.9 2.8 copy.100
  582.8 2.7 pad_maximum_fusion
  585.4 9.2 fusion.84
  595.5 12.8 %all-reduce.3 = (f32[192]{0:T(256)}, f32[192]{0:T(256)}) all-reduce(f32[192]{0:T(256)S(1)} %reduce_sum.230, f32[192]{0:T(256)S(1)} %reduce_sum.232), channel_id=1, replica_groups=mesh['dp'=8,'head'=4] {'dp'}, use_global_device_ids=true, to_apply=%region_20.21 | all-reduce | flops 384 | bytes 3072 | tf_op jit(solution)/shard_map/psum | solution.py:206
  608.3 76.0 %reduce-scatter.4.cloned.1.call-done = bf16[1024,768]{0,1:T(8,128)(2,1)} async-done(((bf16[4096,768]{0,1:T(8,128)(2,1)}), bf16[1024,768]{0,1:T(8,128)(2,1)}) %reduce-scatter.4.cloned.1.call-update) | async-done | bytes 1572880 | tf_op jit(solution)/shard_map/reduce_scatter | solution.py:203
  684.3 4.0 convert_reduce_fusion.2
  688.3 2.4 copy.101
  690.7 42.1 %all-reduce.2 = (f32[768]{0:T(1024)}, f32[768]{0:T(1024)}, f32[768]{0:T(1024)}, f32[768]{0:T(1024)}, bf16[3072]{0:T(1024)(128)(2,1)S(1)}, /*index=5*/f32[768]{0:...) all-reduce(f32[768]{0:T(1024)S(1)} %get-tuple-element.207, ...), channel_id=1, replica_groups=mesh['dp'=8,'head'=4] {'dp','head'}, use_global_device_ids=true, to_apply=%region_17.18 | all-reduce | flops 8452 | bytes 61472 | tf_op jit(solution)/shard_map/psum | solution.py:228
  733.0 39.6 %all-reduce = bf16[3072]{0:T(1024)(128)(2,1)S(1)} all-reduce(bf16[3072]{0:T(1024)(128)(2,1)S(1)} %dynamic-update-slice), channel_id=1, replica_groups=mesh['dp'=8,'head'=4] {'dp','head'}, use_global_device_ids=true, to_apply=%add | all-reduce | flops 3072 | bytes 12288
  775.0 7.5 copy.102
  782.5 34.4 %all-gather.8.cloned.1.call-done = bf16[3072,768]{1,0:T(8,128)(2,1)} async-done(((bf16[96,768]{1,0:T(8,128)(2,1)}), bf16[3072,768]{1,0:T(8,128)(2,1)}) %all-gather.8.cloned.1.call-update) | async-done | bytes 4718608 | tf_op jit(solution)/shard_map/all_gather | solution.py:251
  816.9 6.8 convert_element_type.142
  823.7 133.3 %all-reduce.9.cloned.1.call-done = f32[768,768]{1,0:T(8,128)} async-done(((f32[768,768]{1,0:T(8,128)}), f32[768,768]{1,0:T(8,128)}) %all-reduce.9.cloned.1.call-update) | async-done | bytes 2359312 | tf_op jit(solution)/shard_map/psum | solution.py:228
  957.1 62.9 %all-reduce.7.cloned.1.call-done = f32[768,3,192]{0,2,1:T(8,128)} async-done(((f32[768,3,192]{0,2,1:T(8,128)}), f32[768,3,192]{0,2,1:T(8,128)}) %all-reduce.7.cloned.1.call-update) | async-done | bytes 1769488 | tf_op jit(solution)/shard_map/psum | solution.py:206
  1020.0 2.9 copy.149
  (203 shorter events, 101.5 us)
Async XLA Ops:
  7.2 226.0 %copy-start = (bf16[768,768]{1,0:T(8,128)(2,1)S(1)}, bf16[768,768]{1,0:T(8,128)(2,1)}, u32[]{:S(2)}) copy-start(bf16[768,768]{1,0:T(8,128)(2,1)} %param.29) | copy-start | bytes 3538948
  7.2 1.9 copy-start.21
  7.2 1.9 copy-start.16
  7.2 121.5 %all-gather.4.cloned.1.call-start = ((), (), s32[]{:S(2)}) async-start(), calls=%async_computation.5 | async-start | bytes 7864320 | tf_op jit(solution)/shard_map/all_gather | solution.py:151
  9.1 1.4 copy-start.25
  9.1 1.4 copy-start.26
  188.2 7.8 copy-start.14
  191.2 42.0 %copy-start.17 = (f32[768]{0:T(1024)S(1)}, f32[768]{0:T(1024)}, u32[]{:S(2)}) copy-start(f32[768]{0:T(1024)} %param.30) | copy-start | bytes 9220
  191.2 42.0 %all-to-all-start = ((bf16[4,1024,192]{1,2,0:T(8,128)(2,1)}), bf16[4,1024,192]{1,2,0:T(8,128)(2,1)}, u32[]{:S(2)}, u32[]{:S(2)}) async-start(bf16[4,1024,192]{1,2,0:T(8,128)(2,1)} %copy.87), calls=%async_computation | async-start | bytes 3145728 | tf_op jit(solution)/shard_map/all_to_all | solution.py:162
  195.7 258.7 %reduce-scatter.6.cloned.1.call-start = ((), (), s32[]{:S(2)}) async-start(), calls=%async_computation.9 | async-start | bytes 9732096 | tf_op jit(solution)/shard_map/reduce_scatter | solution.py:243
  233.2 4.2 slice-start.2
  233.2 4.2 slice-start.3
  236.9 43.2 %copy-start.6 = (f32[1024,768]{0,1:T(8,128)}, f32[1024,768]{0,1:T(8,128)S(1)}, u32[]{:S(2)}) copy-start(f32[1024,768]{0,1:T(8,128)S(1)} %get-tuple-element.263) | copy-start | bytes 9437188
  236.9 0.7 copy-start.20
  236.9 0.8 copy-start.23
  236.9 0.8 copy-start.24
  237.7 11.2 %copy-start.18 = (f32[768]{0:T(1024)S(1)}, f32[768]{0:T(1024)}, u32[]{:S(2)}) copy-start(f32[768]{0:T(1024)} %param.36) | copy-start | bytes 9220
  258.0 6.9 copy-start.2
  258.0 2.5 copy-start.3
  258.0 2.5 copy-start.13
  258.1 9.7 slice-start
  260.6 4.3 copy-start.19
  260.6 7.2 slice-start.1
  267.8 12.3 %copy-start.10 = (bf16[1024,768]{0,1:T(8,128)(2,1)}, bf16[1024,768]{0,1:T(8,128)(2,1)S(1)}, u32[]{:S(2)}) copy-start(bf16[1024,768]{0,1:T(8,128)(2,1)S(1)} %get-tuple-element.259) | copy-start | bytes 4718596
  280.1 2.7 copy-start.27
  291.3 1.4 copy-start.4
  292.7 12.1 %copy-start.7 = (f32[1024,768]{0,1:T(8,128)S(1)}, f32[1024,768]{0,1:T(8,128)}, u32[]{:S(2)}) copy-start(f32[1024,768]{0,1:T(8,128)} %copy-done.6) | copy-start | bytes 9437188
  305.5 2.6 copy-start.5
  308.1 3.8 copy-start.11
  308.1 50.4 %all-to-all-start.1 = ((bf16[1024,4,192]{0,2,1:T(8,128)(2,1)}), bf16[1024,4,192]{0,2,1:T(8,128)(2,1)S(1)}, u32[]{:S(2)}, u32[]{:S(2)}) async-start(bf16[1024,4,192]{0,2,1:T(8,128)(2,1)} %bitcast.20), calls=%async_computation.1 | async-start | bytes 3145728 | tf_op jit(solution)/shard_map/all_to_all | solution.py:190
  311.8 260.5 %reduce-scatter.8.cloned.1.call-start = ((), (), s32[]{:S(2)}) async-start(), calls=%async_computation.11 | async-start | bytes 9732096 | tf_op jit(solution)/shard_map/reduce_scatter | solution.py:244
  322.3 361.9 %reduce-scatter.4.cloned.1.call-start = ((), (), s32[]{:S(2)}) async-start(), calls=%async_computation.6 | async-start | bytes 7864320 | tf_op jit(solution)/shard_map/reduce_scatter | solution.py:203
  439.9 1.6 copy-start.8
  444.6 2.5 copy-start.22
  445.0 2.2 copy-start.12
  454.4 320.6 %all-gather.6.cloned.1.call-start = ((), (), s32[]{:S(2)}) async-start(), calls=%async_computation.10 | async-start | bytes 4866048 | tf_op jit(solution)/shard_map/all_gather | solution.py:248
  456.1 360.8 %all-gather.8.cloned.1.call-start = ((), (), s32[]{:S(2)}) async-start(), calls=%async_computation.12 | async-start | bytes 4866048 | tf_op jit(solution)/shard_map/all_gather | solution.py:251
  574.0 5.3 copy-start.15
  574.0 383.1 %all-reduce.9.cloned.1.call-start = ((), (), s32[]{:S(2)}) async-start(), calls=%async_computation.8 | async-start | bytes 4718592 | tf_op jit(solution)/shard_map/psum | solution.py:228
  579.3 440.7 %all-reduce.7.cloned.1.call-start = ((), (), s32[]{:S(2)}) async-start(), calls=%async_computation.7 | async-start | bytes 3538944 | tf_op jit(solution)/shard_map/psum | solution.py:206
  1020.0 3.0 copy-start.9
  1020.0 4.4 copy-start.1
Sparse Core Ops, SparseCore 0:
  10.6 118.0 all-gather.3
  291.4 139.2 reduce-scatter.5
  437.2 135.1 reduce-scatter.7
  574.5 109.7 reduce-scatter.3
  687.5 64.6 all-gather.5
  754.8 62.0 all-gather.7
  823.1 133.9 all-reduce.8
  961.0 58.9 all-reduce.6
where the time goes:
time: 1040 us; the launch traced here: 1030 us
  waiting for transfers between devices  612 us (59%)
  matrix products  199 us (19%)
  blocking collectives  94.5 us (9%)
  local copies, waits for them, and re-layouts  60.1 us (6%)
  other arithmetic  41.4 us (4%)
  between operations  15.6 us (2%)
    psum x1, waiting for transfers between devices, body(): lax.psum((out_weight_grad, out_bias_grad, gain_first_grad, bias_first_gra...  133 us
    all_gather x1, waiting for transfers between devices, body(): gathered = lax.all_gather(inputs, 'head', axis=0, tiled=True)  118 us
    reduce_scatter x1, waiting for transfers between devices, body(): lax.psum_scatter(down_weight_grad, ('dp', 'head'), scatter_dimension=0, t...  116 us
    reduce_scatter x1, waiting for transfers between devices, body(): lax.psum_scatter(input_part.astype(jnp.bfloat16), 'head', scatter_dimensi...  76 us
    psum x1, waiting for transfers between devices, body(): lax.psum((weight_grad, first_grad, third_grad), 'dp')  62.9 us
    psum x1, blocking collectives, body(): lax.psum((out_weight_grad, out_bias_grad, gain_first_grad, bias_first_gra...  42.1 us
    unnamed x1, blocking collectives  39.6 us
    all_to_all x1, waiting for transfers between devices, body(): lax.all_to_all(context_grad, 'head', split_axis=1, concat_axis=0, tiled=T...  36.1 us
  transfers between devices with their start and end apart: 10, of which 8 were waited for; matrix products, arithmetic and copies ran while one was open for 16% of the time, Pallas kernels for 0%

commit v1 on v0

v1 whole, which is shorter than its diff:
```python
import functools
import math

import jax
import jax.numpy as jnp
from jax import lax
from jax.experimental import pallas as pl
from jax.experimental.pallas import tpu as pltpu
from jax.sharding import PartitionSpec as P

HEAD_DIM = 64
LEN = 512
EPS = 1e-12
BF = jnp.bfloat16
F32 = jnp.float32


def dot_nn(left, right):
    return lax.dot_general(left, right, (((1,), (0,)), ((), ())), preferred_element_type=F32)


def dot_nt(left, right):
    return lax.dot_general(left, right, (((1,), (1,)), ((), ())), preferred_element_type=F32)


def dot_tn(left, right):
    return lax.dot_general(left, right, (((0,), (0,)), ((), ())), preferred_element_type=F32)


def head_lanes(width, head):
    lanes = lax.broadcasted_iota(jnp.int32, (1, width), 1)
    return (lanes >= head * HEAD_DIM) & (lanes < (head + 1) * HEAD_DIM)


def forward_kernel(
    x_ref, w_ref, qb_ref, vb_ref, ow_ref, acc_ref, q_ref, k_ref, v_ref, ctx_ref, lse_ref, out_ref
):
    x = x_ref[...]
    width = w_ref.shape[2]
    heads = width // HEAD_DIM
    q = (dot_nn(x, w_ref[0]) + qb_ref[...]).astype(BF)
    k = dot_nn(x, w_ref[1]).astype(BF)
    v32 = dot_nn(x, w_ref[2]) + vb_ref[...]
    v = v32.astype(BF)
    q_ref[...] = q
    k_ref[...] = k
    v_ref[...] = v
    v_t = v.T
    q_scaled = q * jnp.asarray(0.125, BF)
    pieces = []
    for head in range(heads):
        k_head = jnp.where(head_lanes(width, head), k, jnp.zeros_like(k))
        scores = dot_nt(k_head, q_scaled)
        highest = jnp.max(scores, axis=0, keepdims=True)
        exponent = jnp.exp(scores - highest)
        totals = jnp.sum(exponent, axis=0, keepdims=True)
        probs = (exponent * (1.0 / totals)).astype(BF)
        pieces.append(dot_nn(v_t[head * HEAD_DIM : (head + 1) * HEAD_DIM], probs))
        lse_ref[0, head : head + 1, :] = highest + jnp.log(totals)
    ctx = jnp.concatenate(pieces, axis=0).T.astype(BF)
    ctx_ref[...] = ctx
    out_ref[...] = acc_ref[...] + dot_nn(ctx, ow_ref[...])


def backward_kernel(
    x_ref,
    w_ref,
    ow_ref,
    q_ref,
    k_ref,
    v_ref,
    ctx_ref,
    lse_ref,
    ga_ref,
    acc_ref,
    wg_ref,
    owg_ref,
    qbg_ref,
    vbg_ref,
    out_ref,
    wg_acc,
    owg_acc,
):
    row = pl.program_id(0)
    last = pl.num_programs(0) - 1
    width = w_ref.shape[2]
    heads = width // HEAD_DIM
    x = x_ref[...]
    ga = ga_ref[...]
    dctx = dot_nt(ga, ow_ref[...]).astype(BF)
    q = q_ref[...]
    k = k_ref[...]
    v = v_ref[...]
    k_t = k.T
    q_scaled = q * jnp.asarray(0.125, BF)
    dq_t = []
    dk = jnp.zeros(q.shape, F32)
    dv = jnp.zeros(q.shape, F32)
    for head in range(heads):
        mask = head_lanes(width, head)
        scores = dot_nt(jnp.where(mask, k, jnp.zeros_like(k)), q_scaled)
        probs = jnp.exp(scores - lse_ref[0, head : head + 1, :])
        dprobs = dot_nt(jnp.where(mask, v, jnp.zeros_like(v)), dctx)
        delta = jnp.sum(probs * dprobs, axis=0, keepdims=True)
        dscores = (probs * (dprobs - delta)).astype(BF)
        dv = jnp.where(mask, dot_nn(probs.astype(BF), dctx), dv)
        dk = jnp.where(mask, dot_nn(dscores, q_scaled), dk)
        dq_t.append(dot_nn(k_t[head * HEAD_DIM : (head + 1) * HEAD_DIM], dscores))
    dq32 = (jnp.concatenate(dq_t, axis=0) * 0.125).T
    dq = dq32.astype(BF)
    dk = dk.astype(BF)
    dv = dv.astype(BF)
    out_ref[...] = (
        acc_ref[...] + dot_nt(dq, w_ref[0]) + dot_nt(dk, w_ref[1]) + dot_nt(dv, w_ref[2])
    )

    @pl.when(row == 0)
    def _():
        wg_acc[...] = jnp.zeros_like(wg_acc)
        owg_acc[...] = jnp.zeros_like(owg_acc)
        qbg_ref[...] = jnp.zeros_like(qbg_ref)
        vbg_ref[...] = jnp.zeros_like(vbg_ref)

    wg_acc[0] += dot_tn(x, dq)
    wg_acc[1] += dot_tn(x, dk)
    wg_acc[2] += dot_tn(x, dv)
    owg_acc[...] += dot_tn(ctx_ref[...], ga)
    qbg_ref[...] += jnp.sum(dq.astype(F32), axis=0, keepdims=True)
    vbg_ref[...] += jnp.sum(dv.astype(F32), axis=0, keepdims=True)

    @pl.when(row == last)
    def _():
        wg_ref[...] = wg_acc[...].astype(BF)
        owg_ref[...] = owg_acc[...].astype(BF)


def by_row(block):
    rank = len(block)
    return pl.BlockSpec(block, lambda r: (r,) + (0,) * (rank - 1))


def fixed(block):
    rank = len(block)
    return pl.BlockSpec(block, lambda r: (0,) * rank)


def attention_forward(x, w, qb, vb, ow, acc):
    tokens, features = x.shape
    width = w.shape[2]
    rows = tokens // LEN
    flops = 2 * tokens * features * width * 4 + 4 * tokens * LEN * width
    return pl.pallas_call(
        forward_kernel,
        grid=(rows,),
        in_specs=[
            by_row((LEN, features)),
            fixed(w.shape),
            fixed((1, width)),
            fixed((1, width)),
            fixed((width, features)),
            by_row((LEN, features)),
        ],
        out_specs=[
            by_row((LEN, width)),
            by_row((LEN, width)),
            by_row((LEN, width)),
            by_row((LEN, width)),
            by_row((1, 8, LEN)),
            by_row((LEN, features)),
        ],
        out_shape=[jax.ShapeDtypeStruct((tokens, width), BF)] * 4
        + [
            jax.ShapeDtypeStruct((rows, 8, LEN), F32),
            jax.ShapeDtypeStruct((tokens, features), F32),
        ],
        compiler_params=pltpu.CompilerParams(
            dimension_semantics=("arbitrary",), vmem_limit_bytes=48 << 20
        ),
        cost_estimate=pl.CostEstimate(
            flops=4 * flops, bytes_accessed=12 << 20, transcendentals=tokens * LEN * 3
        ),
        name="attention_forward",
    )(x, w, qb, vb, ow, acc)


def attention_backward(x, w, ow, q, k, v, ctx, lse, ga, acc):
    tokens, features = x.shape
    width = w.shape[2]
    rows = tokens // LEN
    flops = 2 * tokens * features * width * 8 + 10 * tokens * LEN * width
    return pl.pallas_call(
        backward_kernel,
        grid=(rows,),
        in_specs=[
            by_row((LEN, features)),
            fixed(w.shape),
            fixed((width, features)),
            by_row((LEN, width)),
            by_row((LEN, width)),
            by_row((LEN, width)),
            by_row((LEN, width)),
            by_row((1, 8, LEN)),
            by_row((LEN, features)),
            by_row((LEN, features)),
        ],
        out_specs=[
            fixed(w.shape),
            fixed((width, features)),
            fixed((1, width)),
            fixed((1, width)),
            by_row((LEN, features)),
        ],
        out_shape=[
            jax.ShapeDtypeStruct(w.shape, BF),
            jax.ShapeDtypeStruct((width, features), BF),
            jax.ShapeDtypeStruct((1, width), F32),
            jax.ShapeDtypeStruct((1, width), F32),
            jax.ShapeDtypeStruct((tokens, features), F32),
        ],
        scratch_shapes=[pltpu.VMEM(w.shape, F32), pltpu.VMEM((width, features), F32)],
        compiler_params=pltpu.CompilerParams(
            dimension_semantics=("arbitrary",), vmem_limit_bytes=48 << 20
        ),
        cost_estimate=pl.CostEstimate(
            flops=4 * flops, bytes_accessed=16 << 20, transcendentals=tokens * LEN * 3
        ),
        name="attention_backward",
    )(x, w, ow, q, k, v, ctx, lse, ga, acc)


def swap(value, axis, mask, size):
    return lax.ppermute(value, axis, [(i, i ^ mask) for i in range(size)])


def bit_of(axis, bit):
    return (lax.axis_index(axis) >> bit) & 1


def joined(mine, other, upper, dim, kind=None):
    low = jnp.where(upper == 1, other, mine)
    high = jnp.where(upper == 1, mine, other)
    if kind is not None:
        low, high = low.astype(kind), high.astype(kind)
    return jnp.concatenate([low, high], axis=dim)


def halve(value, bit, size, dim):
    half = value.shape[dim] // 2
    mine = bit_of("dp", bit)
    sent = lax.dynamic_slice_in_dim(value, (1 - mine) * half, half, dim)
    kept = lax.dynamic_slice_in_dim(value, mine * half, half, dim)
    received = swap(sent, "dp", 1 << bit, size)
    return (kept.astype(F32) + received.astype(F32)).astype(BF)


def double(value, bit, size, dim, kind=None):
    return joined(value, swap(value, "dp", 1 << bit, size), bit_of("dp", bit), dim, kind)


def plane_orders(size):
    bits = size.bit_length() - 1
    rest = list(range(1, bits))
    return rest, rest[::-1]


def reduce_plane(value, size, dim):
    value = halve(value, 0, size, dim)
    half = value.shape[dim] // 2
    parts = []
    for index, order in enumerate(plane_orders(size)):
        part = lax.slice_in_dim(value, index * half, (index + 1) * half, axis=dim)
        for bit in order:
            part = halve(part, bit, size, dim)
        parts.append(part)
    return parts


def gather_plane(parts, size, dim, kind=None):
    done = []
    for part, order in zip(parts, plane_orders(size)):
        for bit in order[::-1]:
            part = double(part, bit, size, dim)
        done.append(part)
    return double(jnp.concatenate(done, axis=dim), 0, size, dim, kind)


def reduce_head(pieces, size):
    total = pieces[0].astype(F32)
    for offset in range(1, size):
        total = total + swap(pieces[offset], "head", offset, size).astype(F32)
    return total


def gather_head(piece, size):
    return [piece] + [swap(piece, "head", offset, size) for offset in range(1, size)]


def absolute(pieces, dim):
    count = len(pieces)
    bit = 0
    while (1 << bit) < count:
        upper = bit_of("head", bit)
        step = 1 << bit
        pieces = [
            jnp.where(upper == 1, pieces[index ^ step], pieces[index]) for index in range(count)
        ]
        bit += 1
    return jnp.concatenate(pieces, axis=dim)


def own_pieces(value, size, dim):
    width = value.shape[dim] // size
    me = lax.axis_index("head")
    return [
        lax.dynamic_slice_in_dim(value, (me ^ offset) * width, width, dim)
        for offset in range(size)
    ]


def all_reduce_matrix(value, dp, head, head_dim):
    parts = []
    for part in reduce_plane(value, dp, 0):
        piece = reduce_head(own_pieces(part, head, head_dim), head).astype(BF)
        parts.append(absolute(gather_head(piece, head), head_dim))
    return gather_plane(parts, dp, 0, F32)


def all_reduce_small(vector, dp, head):
    bit = 1
    while bit < dp:
        vector = vector + swap(vector, "dp", bit, dp)
        bit *= 2
    bit = 1
    while bit < head:
        vector = vector + swap(vector, "head", bit, head)
        bit *= 2
    return vector


def norm_forward(hidden, gain, bias):
    center = hidden - jnp.mean(hidden, axis=-1, keepdims=True)
    inverse = lax.rsqrt(jnp.mean(center * center, axis=-1, keepdims=True) + EPS)
    normal = center * inverse
    return (normal * gain + bias, normal, inverse)


def norm_backward(upstream, normal, inverse, gain):
    gain_grad = jnp.sum(upstream * normal, axis=0)
    bias_grad = jnp.sum(upstream, axis=0)
    scaled = upstream * gain
    hidden_grad = inverse * (
        scaled
        - jnp.mean(scaled, axis=-1, keepdims=True)
        - normal * jnp.mean(scaled * normal, axis=-1, keepdims=True)
    )
    return (hidden_grad, gain_grad, bias_grad)


def phi(values):
    return 0.5 * (1.0 + jax.scipy.special.erf(values * (1.0 / math.sqrt(2.0))))


def body(
    dp,
    head,
    tokens,
    span_mask,
    valid_mask,
    mask_embedding,
    qkv_weight,
    query_bias,
    value_bias,
    out_weight,
    out_bias,
    norm1_gain,
    norm1_bias,
    up_weight,
    up_bias,
    down_weight,
    down_bias,
    norm2_gain,
    norm2_bias,
    out_grad,
):
    features = tokens.shape[1]
    width = qkv_weight.shape[2]
    masked = (span_mask == 1)[:, None]
    inputs = jnp.where(masked, mask_embedding[None, :], tokens)
    inputs_wide = inputs.astype(F32)
    validity = valid_mask.astype(F32)[:, None]

    own = jnp.transpose(qkv_weight, (1, 0, 2))
    core = bit_of("dp", 0)
    half = lax.dynamic_slice_in_dim(own, core * (features // 2), features // 2, 1)
    halves = [half]
    for bit in range(head.bit_length() - 1):
        halves = halves + [swap(part, "head", 1 << bit, head) for part in halves]
    weights = [own] + [double(part, 0, dp, 1) for part in halves[1:]]
    biases = jnp.stack([query_bias, value_bias]).astype(F32)
    bias_parts = [biases]
    for bit in range(head.bit_length() - 1):
        bias_parts = bias_parts + [swap(part, "head", 1 << bit, head) for part in bias_parts]
    out_parts = own_pieces(out_weight, head, 0)

    attended = jnp.broadcast_to(out_bias[None, :], tokens.shape)
    saved = []
    for group in range(head):
        q, k, v, ctx, lse, attended = attention_forward(
            inputs,
            weights[group],
            bias_parts[group][0:1],
            bias_parts[group][1:2],
            out_parts[group],
            attended,
        )
        saved.append((q, k, v, ctx, lse))

    normed, normal_first, inverse_first = norm_forward(
        inputs_wide + attended, norm1_gain, norm1_bias
    )
    normed_low = normed.astype(BF)
    preact = dot_nn(normed_low, up_weight) + up_bias
    activated = (preact * phi(preact)).astype(BF)
    feedout = dot_nn(activated, down_weight) + down_bias
    result, normal_second, inverse_second = norm_forward(normed + feedout, norm2_gain, norm2_bias)
    grad_output = out_grad.astype(F32) * validity
    grad_second, gain_second_grad, bias_second_grad = norm_backward(
        grad_output, normal_second, inverse_second, norm2_gain
    )
    grad_feed = grad_second.astype(BF)
    down_bias_grad = jnp.sum(grad_feed, axis=0, dtype=F32)
    down_local = dot_tn(activated, grad_feed).astype(BF)
    down_weight_grad = all_reduce_matrix(down_local, dp, head, 0)
    slope = phi(preact) + preact * jnp.exp(-0.5 * preact * preact) * (
        1.0 / math.sqrt(2.0 * math.pi)
    )
    grad_preact = (dot_nt(grad_feed, down_weight) * slope).astype(BF)
    up_bias_grad = jnp.sum(grad_preact, axis=0, dtype=F32)
    up_local = dot_tn(normed_low, grad_preact).astype(BF)
    up_weight_grad = all_reduce_matrix(up_local, dp, head, 1)
    grad_normed = dot_nt(grad_preact, up_weight) + grad_second
    grad_first, gain_first_grad, bias_first_grad = norm_backward(
        grad_normed, normal_first, inverse_first, norm1_gain
    )
    grad_attended = grad_first.astype(BF)
    out_bias_grad = jnp.sum(grad_attended, axis=0, dtype=F32)
    squares = jnp.stack(
        [
            jnp.sum(validity * inputs_wide * inputs_wide),
            jnp.sum(validity * attended * attended),
            jnp.sum(validity * feedout * feedout),
            jnp.sum(validity),
        ]
    )
    early = [
        down_bias_grad,
        gain_second_grad,
        bias_second_grad,
        gain_first_grad,
        bias_first_grad,
        out_bias_grad,
        up_bias_grad,
        squares,
    ]
    early_sum = all_reduce_small(jnp.concatenate(early), dp, head)

    grad_inputs = grad_first
    weight_pieces = []
    out_pieces = []
    query_parts = []
    value_parts = []
    for group in range(head):
        q, k, v, ctx, lse = saved[group]
        weight_piece, out_piece, query_part, value_part, grad_inputs = attention_backward(
            inputs,
            weights[group],
            out_parts[group],
            q,
            k,
            v,
            ctx,
            lse,
            grad_attended,
            grad_inputs,
        )
        weight_pieces.append(reduce_plane(weight_piece, dp, 1))
        out_pieces.append(out_piece)
        query_parts.append(query_part[0])
        value_parts.append(value_part[0])

    weight_grad = gather_plane(
        [
            reduce_head([weight_pieces[group][part] for group in range(head)], head).astype(BF)
            for part in range(2)
        ],
        dp,
        1,
        F32,
    )
    weight_grad = jnp.transpose(weight_grad, (1, 0, 2))

    out_reduced = jnp.stack(out_pieces)
    for bit in range(dp.bit_length() - 1):
        out_reduced = halve(out_reduced, bit, dp, 1)
    out_piece = reduce_head([out_reduced[group] for group in range(head)], head).astype(BF)
    for bit in range(dp.bit_length() - 2, -1, -1):
        out_piece = double(out_piece, bit, dp, 0)
    out_weight_grad = absolute(gather_head(out_piece, head), 0).astype(F32)

    tokens_grad = jnp.where(masked, 0.0, grad_inputs)
    embedding_grad = jnp.sum(jnp.where(masked, grad_inputs, 0.0), axis=0)
    late = jnp.concatenate([embedding_grad, absolute(query_parts, 0), absolute(value_parts, 0)])
    late_sum = all_reduce_small(late, dp, head)
    embedding_grad = late_sum[:features]
    me = lax.axis_index("head")
    first_grad = lax.dynamic_slice_in_dim(late_sum, features + me * width, width)
    third_grad = lax.dynamic_slice_in_dim(late_sum, 2 * features + me * width, width)

    pieces = []
    offset = 0
    for part in early:
        pieces.append(lax.slice_in_dim(early_sum, offset, offset + part.shape[0]))
        offset += part.shape[0]
    (
        down_bias_grad,
        gain_second_grad,
        bias_second_grad,
        gain_first_grad,
        bias_first_grad,
        out_bias_grad,
        up_bias_grad,
        squares,
    ) = pieces
    count = jnp.maximum(squares[3], 1.0)
    stream_rms = jnp.sqrt(squares[:3] / (count * features))
    return (
        result.astype(BF),
        tokens_grad,
        embedding_grad,
        weight_grad,
        first_grad,
        third_grad,
        out_weight_grad,
        out_bias_grad,
        gain_first_grad,
        bias_first_grad,
        up_weight_grad,
        up_bias_grad,
        down_weight_grad,
        down_bias_grad,
        gain_second_grad,
        bias_second_grad,
        stream_rms,
    )


def solution(mesh):
    split = P(("dp", "head"), None)
    flat = P(("dp", "head"))
    placed = (split, flat, flat, P(), P(None, None, "head"), P("head"), P("head")) + (P(),) * 10
    placed = placed + (split,)
    outs = (split, split, P(), P(None, None, "head"), P("head"), P("head")) + (P(),) * 11
    return jax.shard_map(
        functools.partial(body, mesh.shape["dp"], mesh.shape["head"]),
        mesh=mesh,
        in_specs=placed,
        out_specs=outs,
        check_vma=False,
    )
```

time: 1040 us -> 571 us (0.55)
  waiting for transfers between devices: 612 us -> 145 us
  matrix products: 199 us -> 61.5 us
  starting transfers between devices: 8.93 us -> 114 us
  blocking collectives: 94.5 us -> 0 us
  Pallas kernels: 0 us -> 87.7 us
  other arithmetic: 41.4 us -> 72.7 us
  local copies, waits for them, and re-layouts: 60.1 us -> 77 us
  between operations: 15.6 us -> 3.61 us
    psum x2 -> x0, waiting for transfers between devices: 196 us -> none  [the longest x1 133 us: body(): lax.psum((out_weight_grad, out_bias_grad, gain_first_grad, bias_first_gra...]
    reduce_scatter x3 -> x0, waiting for transfers between devices: 192 us -> none  [the longest x1 116 us: body(): lax.psum_scatter(down_weight_grad, ('dp', 'head'), scatter_dimension=0, t...]
    all_gather x3 -> x0, waiting for transfers between devices: 153 us -> none  [the longest x1 118 us: body(): gathered = lax.all_gather(inputs, 'head', axis=0, tiled=True)]
    ppermute x0 -> x106, waiting for transfers between devices: none -> 145 us  [swap(): return lax.ppermute(value, axis, [(i, i ^ mask) for i in range(size)])]
    dot_general x68 -> x6, matrix products: 199 us -> 61.5 us  [the longest x2 22.8 us: dot_nt(): lax.dot_general(left, right, (((1,), (1,)), ((), ())), preferred_element_...]
    ppermute x0 -> x106, starting transfers between devices: none -> 114 us  [swap(): return lax.ppermute(value, axis, [(i, i ^ mask) for i in range(size)])]
    pallas_call x0 -> x8, Pallas kernels: none -> 87.7 us  [the longest x4 54.7 us: attention_backward(): pl.pallas_call(backward_kernel, grid=(rows,), in_specs=[by_row((LEN, feat...]
    all_to_all x2 -> x0, waiting for transfers between devices: 70.8 us -> none  [the longest x1 36.1 us: body(): lax.all_to_all(context_grad, 'head', split_axis=1, concat_axis=0, tiled=T...]
  transfers between devices with their start and end apart: 10 -> 106, of which waited for: 8 -> 53; matrix products, arithmetic and copies ran while one was open for 16% -> 18% of each run, Pallas kernels for 0% -> 4%
where the time goes in v1:
time: 571 us; the launch traced here: 562 us
  waiting for transfers between devices  145 us (25%)
  starting transfers between devices  114 us (20%)
  Pallas kernels  87.7 us (15%)
  local copies, waits for them, and re-layouts  77 us (13%)
  other arithmetic  72.7 us (13%)
  matrix products  61.5 us (11%)
    ppermute x106, waiting for transfers between devices, swap(): return lax.ppermute(value, axis, [(i, i ^ mask) for i in range(size)])  145 us
    ppermute x106, starting transfers between devices, swap(): return lax.ppermute(value, axis, [(i, i ^ mask) for i in range(size)])  114 us
    pallas_call x4, Pallas kernels, attention_backward(): pl.pallas_call(backward_kernel, grid=(rows,), in_specs=[by_row((LEN, feat...  54.7 us
    pallas_call x4, Pallas kernels, attention_forward(): pl.pallas_call(forward_kernel, grid=(rows,), in_specs=[by_row((LEN, featu...  33 us
    dot_general x2, matrix products, dot_nt(): lax.dot_general(left, right, (((1,), (1,)), ((), ())), preferred_element_...  22.8 us
    dynamic_slice x37, local copies, waits for them, and re-layouts, halve(): sent = lax.dynamic_slice_in_dim(value, (1 - mine) * half, half, dim)  22.2 us
    dot_general x2, matrix products, dot_tn(): lax.dot_general(left, right, (((0,), (0,)), ((), ())), preferred_element_...  19.6 us
    dot_general x2, matrix products, dot_nn(): lax.dot_general(left, right, (((1,), (0,)), ((), ())), preferred_element_...  19.2 us
  transfers between devices with their start and end apart: 106, of which 53 were waited for; matrix products, arithmetic and copies ran while one was open for 18% of the time, Pallas kernels for 4%

profile of v1, /device:TPU:0, one launch (start us, length us, event | category | flops | bytes accessed | tf_op | source)
XLA Modules:
  0.0 561.5 jit_solution(4741105470151813490)
XLA Ops:
  2.5 3.1 collective-permute-start
  5.5 2.6 collective-permute-start.5
  16.9 8.1 %attention_forward.4 = (bf16[1024,192]{1,0:T(8,128)(2,1)S(1)}, bf16[1024,192]{1,0:T(8,128)(2,1)S(1)}, bf16[1024,192]{1,0:T(8,128)(2,1)S(1)}, bf16[1024,192]{1,0:...) custom-call(bf16[1024,768]{1,0:T(8,128)(2,1)S(1)} %broadcast_select_fusion.5.x_ref, ...), custom_call_target="tpu_custom_call" | custom-call | flops 6442450944 | bytes 12582912 | tf_op jit(solution)/shard_map/attention_forward/pallas_call | solution.py:152
  28.7 2.9 collective-permute-start.4
  33.2 2.9 collective-permute-start.1
  44.7 8.5 %attention_forward.5 = (bf16[1024,192]{1,0:T(8,128)(2,1)S(1)}, bf16[1024,192]{1,0:T(8,128)(2,1)S(1)}, bf16[1024,192]{1,0:T(8,128)(2,1)S(1)}, bf16[1024,192]{1,0:...) custom-call(bf16[1024,768]{1,0:T(8,128)(2,1)S(1)} %broadcast_select_fusion.5.x_ref, ...), custom_call_target="tpu_custom_call" | custom-call | flops 6442450944 | bytes 12582912 | tf_op jit(solution)/shard_map/attention_forward/pallas_call | solution.py:152
  58.4 8.1 %attention_forward.6 = (bf16[1024,192]{1,0:T(8,128)(2,1)S(1)}, bf16[1024,192]{1,0:T(8,128)(2,1)S(1)}, bf16[1024,192]{1,0:T(8,128)(2,1)S(1)}, bf16[1024,192]{1,0:...) custom-call(bf16[1024,768]{1,0:T(8,128)(2,1)S(1)} %broadcast_select_fusion.5.x_ref, ...), custom_call_target="tpu_custom_call" | custom-call | flops 6442450944 | bytes 12582912 | tf_op jit(solution)/shard_map/attention_forward/pallas_call | solution.py:152
  73.3 8.3 %attention_forward.7 = (bf16[1024,192]{1,0:T(8,128)(2,1)S(1)}, bf16[1024,192]{1,0:T(8,128)(2,1)S(1)}, bf16[1024,192]{1,0:T(8,128)(2,1)S(1)}, bf16[1024,192]{1,0:...) custom-call(bf16[1024,768]{1,0:T(8,128)(2,1)S(1)} %broadcast_select_fusion.5.x_ref, ...), custom_call_target="tpu_custom_call" | custom-call | flops 6442450944 | bytes 12582912 | tf_op jit(solution)/shard_map/attention_forward/pallas_call | solution.py:152
  81.7 2.7 fusion.23
  85.3 11.5 %multiply_convert_fusion = (bf16[1024,3072]{1,0:T(8,128)(2,1)}, f32[1024,3072]{1,0:T(8,128)}) fusion(f32[3072]{0:T(1024)S(1)} %copy-done.93, bf16[768,3072]{1,0:T(8,128)(2,1)S(1)} %bitcast.60, f32[1024,768]{1,0:T(8,128)S(1)} %get-tuple-element.162, f32[768]{0:T(1024)S(1)} %copy-done.94, f32[768]{0:T(1024)S(1)} %copy-done.92, f32[1024]{0:T(1024)S(1)} %add_rsqrt_fusion.1, ...), kind=kOutput, calls=%fused_computation.8 | convolution fusion | flops 4854644736 | bytes 26765312 | tf_op jit(solution)/shard_map/dot_general | solution.py:19
  96.8 7.6 %fusion.22 = (f32[1024]{0:T(1024)S(1)}, f32[1024,768]{1,0:T(8,128)S(1)}, f32[1024,768]{1,0:T(8,128)S(1)}) fusion(f32[768]{0:T(1024)S(1)} %copy-done.90, f32[768]{0:T(1024)S(1)} %copy-done.94, f32[768]{0:T(1024)S(1)} %copy-done.92, f32[1024]{0:T(1024)S(1)} %add_rsqrt_fusion.1, f32[1024,768]{1,0:T(8,128)S(1)} %get-tuple-element.162, ...), kind=kOutput, calls=%fused_computation.279 | convolution fusion | flops 4837342208 | bytes 20468736 | tf_op jit(solution)/shard_map/dot_general | solution.py:19
  106.4 4.2 fusion.8
  110.6 3.3 convert_reduce_fusion.2
  113.8 13.8 %convert_reduce_fusion = (f32[3072]{0:T(1024)}, bf16[1024,3072]{1,0:T(8,128)(2,1)}) fusion(f32[1024,3072]{1,0:T(8,128)} %get-tuple-element.284, f32[3072]{0:T(1024)S(1)} %copy-done.93, bf16[3072,768]{1,0:T(8,128)(2,1)S(1)} %bitcast.58, f32[1024,768]{1,0:T(8,128)S(1)} %get-tuple-element.158), kind=kOutput, calls=%fused_computation.7 | convolution fusion | flops 4873516032 | bytes 26763264 | tf_op jit(solution)/shard_map/dot_general | solution.py:23
  127.6 9.0 %multiply_reduce_fusion = (f32[768]{0:T(1024)}, f32[1024]{0:T(1024)S(1)}, f32[1024]{0:T(1024)S(1)}, f32[768]{0:T(1024)}, f32[1024,768]{1,0:T(8,128)S(1)}) fusion(f32[1024,768]{1,0:T(8,128)S(1)} %get-tuple-element.162, f32[1024]{0:T(1024)S(1)} %add_rsqrt_fusion.1, f32[1024]{0:T(1024)S(1)} %broadcast_multiply_fusion.5, f32[768]{0:T(1024)S(1)} %copy-done.92, ...), kind=kOutput, calls=%fused_computation.24 | convolution fusion | flops 4839698432 | bytes 20472832 | tf_op jit(solution)/shard_map/dot_general | solution.py:23
  136.6 9.9 %convolution_convert_fusion.1 = bf16[768,3072]{1,0:T(8,128)(2,1)} fusion(bf16[1024,3072]{1,0:T(8,128)(2,1)} %get-tuple-element.288, f32[1024,768]{1,0:T(8,128)S(1)} %get-tuple-element.162, f32[768]{0:T(1024)S(1)} %copy-done.94, f32[768]{0:T(1024)S(1)} %copy-done.92, f32[1024]{0:T(1024)S(1)} %add_rsqrt_fusion.1, f32[1024]{0:T(1024)S(1)} %broadcast_multiply_fusion.5), kind=kOutput, calls=%fused_computation.11 | convolution fusion | flops 4838129664 | bytes 14170112 | tf_op jit(solution)/shard_map/dot_general | solution.py:27
  146.5 9.7 %convolution_convert_fusion = bf16[3072,768]{1,0:T(8,128)(2,1)} fusion(bf16[1024,3072]{1,0:T(8,128)(2,1)} %get-tuple-element.283, f32[1024,768]{1,0:T(8,128)S(1)} %get-tuple-element.158), kind=kOutput, calls=%fused_computation.10 | convolution fusion | flops 4834983936 | bytes 14155776 | tf_op jit(solution)/shard_map/dot_general | solution.py:27
  156.3 3.4 convert_reduce_fusion.1
  159.7 14.0 %attention_backward.4 = (bf16[3,768,192]{2,1,0:T(8,128)(2,1)S(1)}, bf16[192,768]{1,0:T(8,128)(2,1)S(1)}, f32[1,192]{1,0:T(1,128)S(1)}, f32[1,192]{1,0:T(1,128)S(1)}, f32[1024,768]{1,0:T(8,128)}) custom-call(bf16[1024,768]{1,0:T(8,128)(2,1)} %copy-done, bf16[3,768,192]{2,1,0:T(8,128)(2,1)S(1)} %bitcast.42, bf16[192,768]{1,0:T(8,128)(2,1)S(1)} %copy-done.21, ...), custom_call_target="tpu_custom_call" | custom-call | flops 13690208256 | bytes 16777216 | tf_op jit(solution)/shard_map/attention_backward/pallas_call | solution.py:191
  174.5 13.5 %attention_backward.5 = (bf16[3,768,192]{2,1,0:T(8,128)(2,1)S(1)}, bf16[192,768]{1,0:T(8,128)(2,1)S(1)}, f32[1,192]{1,0:T(1,128)S(1)}, f32[1,192]{1,0:T(1,128)S(1)}, f32[1024,768]{1,0:T(8,128)}) custom-call(bf16[1024,768]{1,0:T(8,128)(2,1)} %copy-done, bf16[3,768,192]{2,1,0:T(8,128)(2,1)S(1)} %copy-done.2, bf16[192,768]{1,0:T(8,128)(2,1)S(1)} %copy-done.19, ...), custom_call_target="tpu_custom_call" | custom-call | flops 13690208256 | bytes 16777216 | tf_op jit(solution)/shard_map/attention_backward/pallas_call | solution.py:191
  188.7 13.7 %attention_backward.6 = (bf16[3,768,192]{2,1,0:T(8,128)(2,1)S(1)}, bf16[192,768]{1,0:T(8,128)(2,1)S(1)}, f32[1,192]{1,0:T(1,128)S(1)}, f32[1,192]{1,0:T(1,128)S(1)}, f32[1024,768]{1,0:T(8,128)}) custom-call(bf16[1024,768]{1,0:T(8,128)(2,1)} %copy-done, bf16[3,768,192]{2,1,0:T(8,128)(2,1)S(1)} %pad_maximum_fusion.3.w_ref, ...), custom_call_target="tpu_custom_call" | custom-call | flops 13690208256 | bytes 16777216 | tf_op jit(solution)/shard_map/attention_backward/pallas_call | solution.py:191
  203.4 13.6 %attention_backward.7 = (bf16[3,768,192]{2,1,0:T(8,128)(2,1)S(1)}, bf16[192,768]{1,0:T(8,128)(2,1)S(1)}, f32[1,192]{1,0:T(1,128)S(1)}, f32[1,192]{1,0:T(1,128)S(1)}, f32[1024,768]{1,0:T(8,128)}) custom-call(bf16[1024,768]{1,0:T(8,128)(2,1)} %copy-done, bf16[3,768,192]{2,1,0:T(8,128)(2,1)S(1)} %pad_maximum_fusion.2.w_ref, ...), custom_call_target="tpu_custom_call" | custom-call | flops 13690208256 | bytes 16777216 | tf_op jit(solution)/shard_map/attention_backward/pallas_call | solution.py:191
  217.0 5.1 select_reduce_fusion
  226.0 2.1 copy.57
  234.5 3.9 concatenate.94
  238.9 3.2 constant_dynamic-slice_fusion.21
  244.5 3.2 constant_dynamic-slice_fusion.10
  260.2 2.1 copy.51
  266.0 3.1 collective-permute-done.61
  271.5 2.1 copy.58
  299.1 2.5 collective-permute-done.18
  302.3 2.5 collective-permute-done.15
  314.9 2.4 collective-permute-start.35
  329.2 6.7 %collective-permute-done.42 = bf16[3,48,192]{2,1,0:T(8,128)(2,1)S(1)} collective-permute-done((bf16[3,48,192]{2,1,0:T(8,128)(2,1)S(1)}, bf16[3,48,192]{2,1,0:T(8,128)(2,1)S(1)}, u32[]{:S(2)}, u32[]{:S(2)}) %collective-permute-start.42) | collective-permute-done | bytes 55328 | tf_op jit(solution)/shard_map/ppermute | solution.py:232
  338.3 5.6 collective-permute-done.47
  343.9 3.1 collective-permute-start.50
  352.4 2.5 collective-permute-done.30
  358.3 3.0 collective-permute-done.52
  362.9 3.4 add_convert_fusion.1
  370.5 12.3 %collective-permute-done.73 = bf16[96,3072]{1,0:T(8,128)(2,1)S(1)} collective-permute-done((bf16[96,3072]{1,0:T(8,128)(2,1)S(1)}, bf16[96,3072]{1,0:T(8,128)(2,1)S(1)}, u32[]{:S(2)}, u32[]{:S(2)}) %collective-permute-start.73) | collective-permute-done | bytes 589856 | tf_op jit(solution)/shard_map/ppermute | solution.py:232
  385.3 9.5 %collective-permute-done.95 = bf16[384,768]{1,0:T(8,128)(2,1)S(1)} collective-permute-done((bf16[384,768]{1,0:T(8,128)(2,1)S(1)}, bf16[384,768]{1,0:T(8,128)(2,1)S(1)}, u32[]{:S(2)}, u32[]{:S(2)}) %collective-permute-start.95) | collective-permute-done | bytes 589856 | tf_op jit(solution)/shard_map/ppermute | solution.py:232
  395.5 3.6 collective-permute-done.85
  399.8 5.6 collective-permute-done.74
  405.9 2.2 collective-permute-start.77
  412.8 3.0 collective-permute-start.67
  417.9 2.5 collective-permute-start.65
  422.4 2.3 collective-permute-done.66
  424.9 2.4 collective-permute-start.97
  431.1 2.1 collective-permute-start.87
  439.7 2.3 collective-permute-start.68
  452.4 2.2 collective-permute-start.90
  456.5 2.1 collective-permute-start.92
  458.7 4.9 collective-permute-start.81
  465.9 5.5 collective-permute-done.81
  471.4 2.2 collective-permute-start.93
  475.5 2.2 collective-permute-done.103
  483.6 7.2 %collective-permute-done.82 = bf16[96,3072]{1,0:T(8,128)(2,1)S(1)} collective-permute-done((bf16[96,3072]{1,0:T(8,128)(2,1)S(1)}, bf16[96,3072]{1,0:T(8,128)(2,1)S(1)}, u32[]{:S(2)}, u32[]{:S(2)}) %collective-permute-start.82) | collective-permute-done | bytes 589856 | tf_op jit(solution)/shard_map/ppermute | solution.py:232
  501.6 8.9 %collective-permute-done.94 = bf16[384,768]{1,0:T(8,128)(2,1)} collective-permute-done((bf16[384,768]{1,0:T(8,128)(2,1)}, bf16[384,768]{1,0:T(8,128)(2,1)}, u32[]{:S(2)}, u32[]{:S(2)}) %collective-permute-start.94) | collective-permute-done | bytes 589856 | tf_op jit(solution)/shard_map/ppermute | solution.py:232
  521.0 5.5 collective-permute-done.54
  526.4 17.3 %collective-permute-done.55 = bf16[192,768]{1,0:T(8,128)(2,1)} collective-permute-done((bf16[192,768]{1,0:T(8,128)(2,1)}, bf16[192,768]{1,0:T(8,128)(2,1)}, u32[]{:S(2)}, u32[]{:S(2)}) %collective-permute-start.55) | collective-permute-done | bytes 294944 | tf_op jit(solution)/shard_map/ppermute | solution.py:232
  546.8 2.4 broadcast_select_fusion.3
  549.3 5.0 maximum_convert_fusion
  554.3 2.3 broadcast_select_fusion.1
  556.6 4.5 maximum_convert_fusion.1
  (568 shorter events, 207.1 us)
Async XLA Ops:
  2.5 29.2 %collective-permute-start = (bf16[3,384,192]{1,2,0:T(8,128)(2,1)}, bf16[3,384,192]{1,2,0:T(8,128)(2,1)}, u32[]{:S(2)}, u32[]{:S(2)}) collective-permute-start(bf16[3,384,192]{1,2,0:T(8,128)(2,1)} %dynamic-slice_bitcast_fusion), channel_id=1, source_target_pairs={{0,1},{1,0},{2,3},{3,2},{4,5},{5,4},{6,7},{7,6},{8,9},{9,8},{10,11... | collective-permute-start | bytes 1327112 | tf_op jit(solution)/shard_map/ppermute | solution.py:232
  5.5 26.1 %collective-permute-start.5 = (bf16[3,384,192]{1,2,0:T(8,128)(2,1)}, bf16[3,384,192]{1,2,0:T(8,128)(2,1)}, u32[]{:S(2)}, u32[]{:S(2)}) collective-permute-start(bf16[3,384,192]{1,2,0:T(8,128)(2,1)} %dynamic-slice_bitcast_fusion), channel_id=1, source_target_pairs={{0,2},{1,3},{2,0},{3,1},{4,6},{5,7},{6,4},{7,5},{8,10},{9,11},{10,... | collective-permute-start | bytes 1327112 | tf_op jit(solution)/shard_map/ppermute | solution.py:232
  9.5 19.3 %collective-permute-start.3 = (f32[2,192]{1,0:T(2,128)S(1)}, f32[2,192]{1,0:T(2,128)S(1)}, u32[]{:S(2)}, u32[]{:S(2)}) collective-permute-start(f32[2,192]{1,0:T(2,128)S(1)} %maximum_convert_fusion.3), channel_id=1, source_target_pairs={{0,1},{1,0},{2,3},{3,2},{4,5},{5,4},{6,7},{7,6},{8,9},{9,8},{10,11... | collective-permute-start | bytes 4616 | tf_op jit(solution)/shard_map/ppermute | solution.py:232
  10.0 21.7 %collective-permute-start.7 = (f32[2,192]{1,0:T(2,128)S(1)}, f32[2,192]{1,0:T(2,128)S(1)}, u32[]{:S(2)}, u32[]{:S(2)}) collective-permute-start(f32[2,192]{1,0:T(2,128)S(1)} %maximum_convert_fusion.3), channel_id=1, source_target_pairs={{0,2},{1,3},{2,0},{3,1},{4,6},{5,7},{6,4},{7,5},{8,10},{9,11},{10,... | collective-permute-start | bytes 4616 | tf_op jit(solution)/shard_map/ppermute | solution.py:232
  31.7 7.8 %collective-permute-start.6 = (bf16[3,384,192]{1,2,0:T(8,128)(2,1)}, bf16[3,384,192]{1,2,0:T(8,128)(2,1)}, u32[]{:S(2)}, u32[]{:S(2)}) collective-permute-start(bf16[3,384,192]{1,2,0:T(8,128)(2,1)} %collective-permute-done.5), channel_id=1, source_target_pairs={{0,4},{4,0},{8,12},{12,8},{16,20},{20,16},{24,28},{28,24},{1,5},{5... | collective-permute-start | bytes 1327112 | tf_op jit(solution)/shard_map/ppermute | solution.py:232
  31.7 9.3 %collective-permute-start.8 = (bf16[3,384,192]{1,2,0:T(8,128)(2,1)}, bf16[3,384,192]{1,2,0:T(8,128)(2,1)}, u32[]{:S(2)}, u32[]{:S(2)}) collective-permute-start(bf16[3,384,192]{1,2,0:T(8,128)(2,1)} %collective-permute-done), channel_id=1, source_target_pairs={{0,4},{4,0},{8,12},{12,8},{16,20},{20,16},{24,28},{28,24},{1,5},{5... | collective-permute-start | bytes 1327112 | tf_op jit(solution)/shard_map/ppermute | solution.py:232
  33.2 23.1 %collective-permute-start.1 = (bf16[3,384,192]{1,2,0:T(8,128)(2,1)}, bf16[3,384,192]{1,2,0:T(8,128)(2,1)}, u32[]{:S(2)}, u32[]{:S(2)}) collective-permute-start(bf16[3,384,192]{1,2,0:T(8,128)(2,1)} %collective-permute-done), channel_id=1, source_target_pairs={{0,2},{1,3},{2,0},{3,1},{4,6},{5,7},{6,4},{7,5},{8,10},{9,11},{10,... | collective-permute-start | bytes 1327112 | tf_op jit(solution)/shard_map/ppermute | solution.py:232
  56.4 13.4 %collective-permute-start.2 = (bf16[3,384,192]{1,2,0:T(8,128)(2,1)}, bf16[3,384,192]{1,2,0:T(8,128)(2,1)}, u32[]{:S(2)}, u32[]{:S(2)}) collective-permute-start(bf16[3,384,192]{1,2,0:T(8,128)(2,1)} %collective-permute-done.1), channel_id=1, source_target_pairs={{0,4},{4,0},{8,12},{12,8},{16,20},{20,16},{24,28},{28,24},{1,5},{5... | collective-permute-start | bytes 1327112 | tf_op jit(solution)/shard_map/ppermute | solution.py:232
  223.6 18.6 %collective-permute-start.9 = (f32[2304]{0:T(1024)S(1)}, f32[2304]{0:T(1024)}, u32[]{:S(2)}, u32[]{:S(2)}) collective-permute-start(f32[2304]{0:T(1024)S(1)} %concatenate.85), channel_id=1, source_target_pairs={{0,4},{4,0},{8,12},{12,8},{16,20},{20,16},{24,28},{28,24},{1,5},{5... | collective-permute-start | bytes 27656 | tf_op jit(solution)/shard_map/ppermute | solution.py:232
  228.1 42.9 %collective-permute-start.25 = (bf16[3,384,192]{1,2,0:T(8,128)(2,1)}, bf16[3,384,192]{1,2,0:T(8,128)(2,1)}, u32[]{:S(2)}, u32[]{:S(2)}) collective-permute-start(bf16[3,384,192]{1,2,0:T(8,128)(2,1)} %copy.57), channel_id=1, source_target_pairs={{0,4},{4,0},{8,12},{12,8},{16,20},{20,16},{24,28},{28,24},{1,5},{5... | collective-permute-start | bytes 1327112 | tf_op jit(solution)/shard_map/ppermute | solution.py:232
  231.1 42.6 %collective-permute-start.21 = (bf16[3,384,192]{1,2,0:T(8,128)(2,1)}, bf16[3,384,192]{1,2,0:T(8,128)(2,1)}, u32[]{:S(2)}, u32[]{:S(2)}) collective-permute-start(bf16[3,384,192]{1,2,0:T(8,128)(2,1)} %copy.55), channel_id=1, source_target_pairs={{0,4},{4,0},{8,12},{12,8},{16,20},{20,16},{24,28},{28,24},{1,5},{5... | collective-permute-start | bytes 1327112 | tf_op jit(solution)/shard_map/ppermute | solution.py:232
  234.5 45.9 %collective-permute-start.17 = (bf16[3,384,192]{1,2,0:T(8,128)(2,1)}, bf16[3,384,192]{1,2,0:T(8,128)(2,1)}, u32[]{:S(2)}, u32[]{:S(2)}) collective-permute-start(bf16[3,384,192]{1,2,0:T(8,128)(2,1)} %copy.53), channel_id=1, source_target_pairs={{0,4},{4,0},{8,12},{12,8},{16,20},{20,16},{24,28},{28,24},{1,5},{5... | collective-permute-start | bytes 1327112 | tf_op jit(solution)/shard_map/ppermute | solution.py:232
  238.4 10.8 %collective-permute-start.57 = (f32[7684]{0:T(1024)}, f32[7684]{0:T(1024)S(1)}, u32[]{:S(2)}, u32[]{:S(2)}) collective-permute-start(f32[7684]{0:T(1024)} %concatenate.94), channel_id=1, source_target_pairs={{0,4},{4,0},{8,12},{12,8},{16,20},{20,16},{24,28},{28,24},{1,5},{5... | collective-permute-start | bytes 92216 | tf_op jit(solution)/shard_map/ppermute | solution.py:232
  255.5 6.8 %collective-permute-start.13 = (f32[2304]{0:T(1024)S(1)}, f32[2304]{0:T(1024)}, u32[]{:S(2)}, u32[]{:S(2)}) collective-permute-start(f32[2304]{0:T(1024)S(1)} %add.452), channel_id=1, source_target_pairs={{0,2},{1,3},{2,0},{3,1},{4,6},{5,7},{6,4},{7,5},{8,10},{9,11},{10,... | collective-permute-start | bytes 27656 | tf_op jit(solution)/shard_map/ppermute | solution.py:232
  262.3 21.4 %collective-permute-start.14 = (bf16[3,384,192]{1,2,0:T(8,128)(2,1)}, bf16[3,384,192]{1,2,0:T(8,128)(2,1)}, u32[]{:S(2)}, u32[]{:S(2)}) collective-permute-start(bf16[3,384,192]{1,2,0:T(8,128)(2,1)} %copy.51), channel_id=1, source_target_pairs={{0,4},{4,0},{8,12},{12,8},{16,20},{20,16},{24,28},{28,24},{1,5},{5... | collective-permute-start | bytes 1327112 | tf_op jit(solution)/shard_map/ppermute | solution.py:232
  269.1 36.4 %collective-permute-start.45 = (bf16[4,96,768]{2,1,0:T(8,128)(2,1)}, bf16[4,96,768]{2,1,0:T(8,128)(2,1)}, u32[]{:S(2)}, u32[]{:S(2)}) collective-permute-start(bf16[4,96,768]{2,1,0:T(8,128)(2,1)} %constant_dynamic-slice_fusion.24), channel_id=1, source_target_pairs={{0,4},{4,0},{8,12},{12,8},{16,20},{20,16},{24,28},{28,24},{1,5},{5... | collective-permute-start | bytes 1769480 | tf_op jit(solution)/shard_map/ppermute | solution.py:232
  271.0 92.0 %collective-permute-start.62 = (bf16[384,3072]{1,0:T(8,128)(2,1)}, bf16[384,3072]{1,0:T(8,128)(2,1)}, u32[]{:S(2)}, u32[]{:S(2)}) collective-permute-start(bf16[384,3072]{1,0:T(8,128)(2,1)} %constant_dynamic-slice_fusion.21), channel_id=1, source_target_pairs={{0,4},{4,0},{8,12},{12,8},{16,20},{20,16},{24,28},{28,24},{1,5},{5... | collective-permute-start | bytes 7077896 | tf_op jit(solution)/shard_map/ppermute | solution.py:232
  278.9 7.2 %collective-permute-start.39 = (bf16[3,96,192]{2,1,0:T(8,128)(2,1)}, bf16[3,96,192]{2,1,0:T(8,128)(2,1)}, u32[]{:S(2)}, u32[]{:S(2)}) collective-permute-start(bf16[3,96,192]{2,1,0:T(8,128)(2,1)} %constant_dynamic-slice_fusion.26), channel_id=1, source_target_pairs={{0,16},{4,20},{8,24},{12,28},{16,0},{20,4},{24,8},{28,12},{1,17},{... | collective-permute-start | bytes 331784 | tf_op jit(solution)/shard_map/ppermute | solution.py:232
  280.4 8.2 %collective-permute-start.36 = (bf16[3,96,192]{2,1,0:T(8,128)(2,1)}, bf16[3,96,192]{2,1,0:T(8,128)(2,1)}, u32[]{:S(2)}, u32[]{:S(2)}) collective-permute-start(bf16[3,96,192]{2,1,0:T(8,128)(2,1)} %constant_dynamic-slice_fusion.28), channel_id=1, source_target_pairs={{0,16},{4,20},{8,24},{12,28},{16,0},{20,4},{24,8},{28,12},{1,17},{... | collective-permute-start | bytes 331784 | tf_op jit(solution)/shard_map/ppermute | solution.py:232
  285.3 6.8 %collective-permute-start.33 = (bf16[3,96,192]{2,1,0:T(8,128)(2,1)S(1)}, bf16[3,96,192]{2,1,0:T(8,128)(2,1)S(1)}, u32[]{:S(2)}, u32[]{:S(2)}) collective-permute-start(bf16[3,96,192]{2,1,0:T(8,128)(2,1)S(1)} %constant_dynamic-slice_fusion.30), channel_id=1, source_target_pairs={{0,16},{4,20},{8,24},{12,28},{16,0},{20,4},{24,8},{28,12},{1,17},{... | collective-permute-start | bytes 331784 | tf_op jit(solution)/shard_map/ppermute | solution.py:232
  286.1 8.2 %collective-permute-start.31 = (bf16[3,96,192]{2,1,0:T(8,128)(2,1)S(1)}, bf16[3,96,192]{2,1,0:T(8,128)(2,1)S(1)}, u32[]{:S(2)}, u32[]{:S(2)}) collective-permute-start(bf16[3,96,192]{2,1,0:T(8,128)(2,1)S(1)} %constant_dynamic-slice_fusion.32), channel_id=1, source_target_pairs={{0,16},{4,20},{8,24},{12,28},{16,0},{20,4},{24,8},{28,12},{1,17},{... | collective-permute-start | bytes 331784 | tf_op jit(solution)/shard_map/ppermute | solution.py:232
  294.3 7.4 %collective-permute-start.18 = (bf16[3,96,192]{2,1,0:T(8,128)(2,1)S(1)}, bf16[3,96,192]{2,1,0:T(8,128)(2,1)S(1)}, u32[]{:S(2)}, u32[]{:S(2)}) collective-permute-start(bf16[3,96,192]{2,1,0:T(8,128)(2,1)S(1)} %constant_dynamic-slice_fusion.40), channel_id=1, source_target_pairs={{0,8},{4,12},{8,0},{12,4},{16,24},{20,28},{24,16},{28,20},{1,9},{5... | collective-permute-start | bytes 331784 | tf_op jit(solution)/shard_map/ppermute | solution.py:232
  294.9 9.9 %collective-permute-start.15 = (bf16[3,96,192]{2,1,0:T(8,128)(2,1)S(1)}, bf16[3,96,192]{2,1,0:T(8,128)(2,1)S(1)}, u32[]{:S(2)}, u32[]{:S(2)}) collective-permute-start(bf16[3,96,192]{2,1,0:T(8,128)(2,1)S(1)} %constant_dynamic-slice_fusion.43), channel_id=1, source_target_pairs={{0,8},{4,12},{8,0},{12,4},{16,24},{20,28},{24,16},{28,20},{1,9},{5... | collective-permute-start | bytes 331784 | tf_op jit(solution)/shard_map/ppermute | solution.py:232
  298.5 9.7 %collective-permute-start.40 = (bf16[3,48,192]{2,1,0:T(8,128)(2,1)S(1)}, bf16[3,48,192]{2,1,0:T(8,128)(2,1)S(1)}, u32[]{:S(2)}, u32[]{:S(2)}) collective-permute-start(bf16[3,48,192]{2,1,0:T(8,128)(2,1)S(1)} %constant_dynamic-slice_fusion.25), channel_id=1, source_target_pairs={{0,8},{4,12},{8,0},{12,4},{16,24},{20,28},{24,16},{28,20},{1,9},{5... | collective-permute-start | bytes 165896 | tf_op jit(solution)/shard_map/ppermute | solution.py:232
  305.5 11.8 %collective-permute-start.32 = (bf16[3,48,192]{2,1,0:T(8,128)(2,1)S(1)}, bf16[3,48,192]{2,1,0:T(8,128)(2,1)S(1)}, u32[]{:S(2)}, u32[]{:S(2)}) collective-permute-start(bf16[3,48,192]{2,1,0:T(8,128)(2,1)S(1)} %constant_dynamic-slice_fusion.31), channel_id=1, source_target_pairs={{0,8},{4,12},{8,0},{12,4},{16,24},{20,28},{24,16},{28,20},{1,9},{5... | collective-permute-start | bytes 165896 | tf_op jit(solution)/shard_map/ppermute | solution.py:232
  314.1 8.6 %collective-permute-start.38 = (bf16[3,48,192]{2,1,0:T(8,128)(2,1)S(1)}, bf16[3,48,192]{2,1,0:T(8,128)(2,1)S(1)}, u32[]{:S(2)}, u32[]{:S(2)}) collective-permute-start(bf16[3,48,192]{2,1,0:T(8,128)(2,1)S(1)} %add_convert_fusion.32), channel_id=1, source_target_pairs={{0,2},{1,3},{2,0},{3,1},{4,6},{5,7},{6,4},{7,5},{8,10},{9,11},{10,... | collective-permute-start | bytes 165896 | tf_op jit(solution)/shard_map/ppermute | solution.py:232
  314.9 7.9 %collective-permute-start.35 = (bf16[3,48,192]{2,1,0:T(8,128)(2,1)S(1)}, bf16[3,48,192]{2,1,0:T(8,128)(2,1)S(1)}, u32[]{:S(2)}, u32[]{:S(2)}) collective-permute-start(bf16[3,48,192]{2,1,0:T(8,128)(2,1)S(1)} %add_convert_fusion.33), channel_id=1, source_target_pairs={{0,1},{1,0},{2,3},{3,2},{4,5},{5,4},{6,7},{7,6},{8,9},{9,8},{10,11... | collective-permute-start | bytes 165896 | tf_op jit(solution)/shard_map/ppermute | solution.py:232
  317.3 7.5 %collective-permute-start.16 = (bf16[3,48,192]{2,1,0:T(8,128)(2,1)S(1)}, bf16[3,48,192]{2,1,0:T(8,128)(2,1)S(1)}, u32[]{:S(2)}, u32[]{:S(2)}) collective-permute-start(bf16[3,48,192]{2,1,0:T(8,128)(2,1)S(1)} %constant_dynamic-slice_fusion.42), channel_id=1, source_target_pairs={{0,16},{4,20},{8,24},{12,28},{16,0},{20,4},{24,8},{28,12},{1,17},{... | collective-permute-start | bytes 165896 | tf_op jit(solution)/shard_map/ppermute | solution.py:232
  324.8 43.0 %collective-permute-start.84 = (bf16[1536,768]{1,0:T(8,128)(2,1)}, bf16[1536,768]{1,0:T(8,128)(2,1)S(1)}, u32[]{:S(2)}, u32[]{:S(2)}) collective-permute-start(bf16[1536,768]{1,0:T(8,128)(2,1)} %constant_dynamic-slice_fusion.10), channel_id=1, source_target_pairs={{0,4},{4,0},{8,12},{12,8},{16,20},{20,16},{24,28},{28,24},{1,5},{5... | collective-permute-start | bytes 7077896 | tf_op jit(solution)/shard_map/ppermute | solution.py:232
  325.6 10.9 %collective-permute-start.46 = (bf16[4,48,768]{2,1,0:T(8,128)(2,1)S(1)}, bf16[4,48,768]{2,1,0:T(8,128)(2,1)S(1)}, u32[]{:S(2)}, u32[]{:S(2)}) collective-permute-start(bf16[4,48,768]{2,1,0:T(8,128)(2,1)S(1)} %constant_dynamic-slice_fusion.23), channel_id=1, source_target_pairs={{0,8},{4,12},{8,0},{12,4},{16,24},{20,28},{24,16},{28,20},{1,9},{5... | collective-permute-start | bytes 884744 | tf_op jit(solution)/shard_map/ppermute | solution.py:232
  328.0 7.9 %collective-permute-start.42 = (bf16[3,48,192]{2,1,0:T(8,128)(2,1)S(1)}, bf16[3,48,192]{2,1,0:T(8,128)(2,1)S(1)}, u32[]{:S(2)}, u32[]{:S(2)}) collective-permute-start(bf16[3,48,192]{2,1,0:T(8,128)(2,1)S(1)} %add_convert_fusion.30), channel_id=1, source_target_pairs={{0,8},{4,12},{8,0},{12,4},{16,24},{20,28},{24,16},{28,20},{1,9},{5... | collective-permute-start | bytes 165896 | tf_op jit(solution)/shard_map/ppermute | solution.py:232
  328.6 9.6 %collective-permute-start.29 = (bf16[3,48,192]{2,1,0:T(8,128)(2,1)S(1)}, bf16[3,48,192]{2,1,0:T(8,128)(2,1)S(1)}, u32[]{:S(2)}, u32[]{:S(2)}) collective-permute-start(bf16[3,48,192]{2,1,0:T(8,128)(2,1)S(1)} %add_convert_fusion.35), channel_id=1, source_target_pairs={{0,16},{4,20},{8,24},{12,28},{16,0},{20,4},{24,8},{28,12},{1,17},{... | collective-permute-start | bytes 165896 | tf_op jit(solution)/shard_map/ppermute | solution.py:232
  336.0 11.1 %collective-permute-start.43 = (bf16[3,96,192]{2,1,0:T(8,128)(2,1)S(1)}, bf16[3,96,192]{2,1,0:T(8,128)(2,1)S(1)}, u32[]{:S(2)}, u32[]{:S(2)}) collective-permute-start(bf16[3,96,192]{2,1,0:T(8,128)(2,1)S(1)} %pad_maximum_fusion.17), channel_id=1, source_target_pairs={{0,16},{4,20},{8,24},{12,28},{16,0},{20,4},{24,8},{28,12},{1,17},{... | collective-permute-start | bytes 331784 | tf_op jit(solution)/shard_map/ppermute | solution.py:232
  336.6 7.3 %collective-permute-start.47 = (bf16[4,24,768]{2,1,0:T(8,128)(2,1)S(1)}, bf16[4,24,768]{2,1,0:T(8,128)(2,1)S(1)}, u32[]{:S(2)}, u32[]{:S(2)}) collective-permute-start(bf16[4,24,768]{2,1,0:T(8,128)(2,1)S(1)} %constant_dynamic-slice_fusion.22), channel_id=1, source_target_pairs={{0,16},{4,20},{8,24},{12,28},{16,0},{20,4},{24,8},{28,12},{1,17},{... | collective-permute-start | bytes 442376 | tf_op jit(solution)/shard_map/ppermute | solution.py:232
  358.3 139.7 %collective-permute-start.44 = (bf16[3,384,192]{1,2,0:T(8,128)(2,1)}, bf16[3,384,192]{1,2,0:T(8,128)(2,1)}, u32[]{:S(2)}, u32[]{:S(2)}) collective-permute-start(bf16[3,384,192]{1,2,0:T(8,128)(2,1)} %copy.59), channel_id=1, source_target_pairs={{0,4},{4,0},{8,12},{12,8},{16,20},{20,16},{24,28},{28,24},{1,5},{5... | collective-permute-start | bytes 1327112 | tf_op jit(solution)/shard_map/ppermute | solution.py:232
  362.9 136.3 %collective-permute-start.53 = (bf16[96,768]{1,0:T(8,128)(2,1)}, bf16[96,768]{1,0:T(8,128)(2,1)}, u32[]{:S(2)}, u32[]{:S(2)}) collective-permute-start(bf16[96,768]{1,0:T(8,128)(2,1)} %pad_maximum_fusion.18), channel_id=1, source_target_pairs={{0,4},{4,0},{8,12},{12,8},{16,20},{20,16},{24,28},{28,24},{1,5},{5... | collective-permute-start | bytes 442376 | tf_op jit(solution)/shard_map/ppermute | solution.py:232
  366.6 16.3 %collective-permute-start.73 = (bf16[96,3072]{1,0:T(8,128)(2,1)S(1)}, bf16[96,3072]{1,0:T(8,128)(2,1)S(1)}, u32[]{:S(2)}, u32[]{:S(2)}) collective-permute-start(bf16[96,3072]{1,0:T(8,128)(2,1)S(1)} %constant_dynamic-slice_fusion.15), channel_id=1, source_target_pairs={{0,16},{4,20},{8,24},{12,28},{16,0},{20,4},{24,8},{28,12},{1,17},{... | collective-permute-start | bytes 1769480 | tf_op jit(solution)/shard_map/ppermute | solution.py:232
  367.1 16.5 %collective-permute-start.63 = (bf16[96,3072]{1,0:T(8,128)(2,1)S(1)}, bf16[96,3072]{1,0:T(8,128)(2,1)S(1)}, u32[]{:S(2)}, u32[]{:S(2)}) collective-permute-start(bf16[96,3072]{1,0:T(8,128)(2,1)S(1)} %constant_dynamic-slice_fusion.20), channel_id=1, source_target_pairs={{0,8},{4,12},{8,0},{12,4},{16,24},{20,28},{24,16},{28,20},{1,9},{5... | collective-permute-start | bytes 1769480 | tf_op jit(solution)/shard_map/ppermute | solution.py:232
  368.9 25.9 %collective-permute-start.95 = (bf16[384,768]{1,0:T(8,128)(2,1)S(1)}, bf16[384,768]{1,0:T(8,128)(2,1)S(1)}, u32[]{:S(2)}, u32[]{:S(2)}) collective-permute-start(bf16[384,768]{1,0:T(8,128)(2,1)S(1)} %constant_dynamic-slice_fusion.4), channel_id=1, source_target_pairs={{0,16},{4,20},{8,24},{12,28},{16,0},{20,4},{24,8},{28,12},{1,17},{... | collective-permute-start | bytes 1769480 | tf_op jit(solution)/shard_map/ppermute | solution.py:232
  382.9 16.2 %collective-permute-start.85 = (bf16[384,768]{1,0:T(8,128)(2,1)S(1)}, bf16[384,768]{1,0:T(8,128)(2,1)S(1)}, u32[]{:S(2)}, u32[]{:S(2)}) collective-permute-start(bf16[384,768]{1,0:T(8,128)(2,1)S(1)} %constant_dynamic-slice_fusion.9), channel_id=1, source_target_pairs={{0,8},{4,12},{8,0},{12,4},{16,24},{20,28},{24,16},{28,20},{1,9},{5... | collective-permute-start | bytes 1769480 | tf_op jit(solution)/shard_map/ppermute | solution.py:232
  383.6 21.8 %collective-permute-start.74 = (bf16[48,3072]{1,0:T(8,128)(2,1)S(1)}, bf16[48,3072]{1,0:T(8,128)(2,1)S(1)}, u32[]{:S(2)}, u32[]{:S(2)}) collective-permute-start(bf16[48,3072]{1,0:T(8,128)(2,1)S(1)} %constant_dynamic-slice_fusion.14), channel_id=1, source_target_pairs={{0,8},{4,12},{8,0},{12,4},{16,24},{20,28},{24,16},{28,20},{1,9},{5... | collective-permute-start | bytes 884744 | tf_op jit(solution)/shard_map/ppermute | solution.py:232
  394.9 11.0 %collective-permute-start.64 = (bf16[48,3072]{1,0:T(8,128)(2,1)S(1)}, bf16[48,3072]{1,0:T(8,128)(2,1)S(1)}, u32[]{:S(2)}, u32[]{:S(2)}) collective-permute-start(bf16[48,3072]{1,0:T(8,128)(2,1)S(1)} %constant_dynamic-slice_fusion.19), channel_id=1, source_target_pairs={{0,16},{4,20},{8,24},{12,28},{16,0},{20,4},{24,8},{28,12},{1,17},{... | collective-permute-start | bytes 884744 | tf_op jit(solution)/shard_map/ppermute | solution.py:232
  399.1 10.5 %collective-permute-start.96 = (bf16[192,768]{1,0:T(8,128)(2,1)S(1)}, bf16[192,768]{1,0:T(8,128)(2,1)S(1)}, u32[]{:S(2)}, u32[]{:S(2)}) collective-permute-start(bf16[192,768]{1,0:T(8,128)(2,1)S(1)} %constant_dynamic-slice_fusion.3), channel_id=1, source_target_pairs={{0,8},{4,12},{8,0},{12,4},{16,24},{20,28},{24,16},{28,20},{1,9},{5... | collective-permute-start | bytes 884744 | tf_op jit(solution)/shard_map/ppermute | solution.py:232
  405.9 6.9 %collective-permute-start.77 = (bf16[48,768]{1,0:T(8,128)(2,1)S(1)}, bf16[48,768]{1,0:T(8,128)(2,1)S(1)}, u32[]{:S(2)}, u32[]{:S(2)}) collective-permute-start(bf16[48,768]{1,0:T(8,128)(2,1)S(1)} %get-tuple-element.240), channel_id=1, source_target_pairs={{0,3},{1,2},{2,1},{3,0},{4,7},{5,6},{6,5},{7,4},{8,11},{9,10},{10,... | collective-permute-start | bytes 221192 | tf_op jit(solution)/shard_map/ppermute | solution.py:232
  409.6 8.3 %collective-permute-start.76 = (bf16[48,768]{1,0:T(8,128)(2,1)S(1)}, bf16[48,768]{1,0:T(8,128)(2,1)S(1)}, u32[]{:S(2)}, u32[]{:S(2)}) collective-permute-start(bf16[48,768]{1,0:T(8,128)(2,1)S(1)} %get-tuple-element.241), channel_id=1, source_target_pairs={{0,2},{1,3},{2,0},{3,1},{4,6},{5,7},{6,4},{7,5},{8,10},{9,11},{10,... | collective-permute-start | bytes 221192 | tf_op jit(solution)/shard_map/ppermute | solution.py:232
  412.8 7.7 %collective-permute-start.67 = (bf16[48,768]{1,0:T(8,128)(2,1)S(1)}, bf16[48,768]{1,0:T(8,128)(2,1)S(1)}, u32[]{:S(2)}, u32[]{:S(2)}) collective-permute-start(bf16[48,768]{1,0:T(8,128)(2,1)S(1)} %get-tuple-element.233), channel_id=1, source_target_pairs={{0,3},{1,2},{2,1},{3,0},{4,7},{5,6},{6,5},{7,4},{8,11},{9,10},{10,... | collective-permute-start | bytes 221192 | tf_op jit(solution)/shard_map/ppermute | solution.py:232
  417.9 6.8 %collective-permute-start.66 = (bf16[48,768]{1,0:T(8,128)(2,1)S(1)}, bf16[48,768]{1,0:T(8,128)(2,1)S(1)}, u32[]{:S(2)}, u32[]{:S(2)}) collective-permute-start(bf16[48,768]{1,0:T(8,128)(2,1)S(1)} %get-tuple-element.234), channel_id=1, source_target_pairs={{0,2},{1,3},{2,0},{3,1},{4,6},{5,7},{6,4},{7,5},{8,10},{9,11},{10,... | collective-permute-start | bytes 221192 | tf_op jit(solution)/shard_map/ppermute | solution.py:232
  417.9 7.0 %collective-permute-start.65 = (bf16[48,768]{1,0:T(8,128)(2,1)S(1)}, bf16[48,768]{1,0:T(8,128)(2,1)S(1)}, u32[]{:S(2)}, u32[]{:S(2)}) collective-permute-start(bf16[48,768]{1,0:T(8,128)(2,1)S(1)} %get-tuple-element.232), channel_id=1, source_target_pairs={{0,1},{1,0},{2,3},{3,2},{4,5},{5,4},{6,7},{7,6},{8,9},{9,8},{10,11... | collective-permute-start | bytes 221192 | tf_op jit(solution)/shard_map/ppermute | solution.py:232
  420.5 6.8 %collective-permute-start.99 = (bf16[48,768]{1,0:T(8,128)(2,1)S(1)}, bf16[48,768]{1,0:T(8,128)(2,1)S(1)}, u32[]{:S(2)}, u32[]{:S(2)}) collective-permute-start(bf16[48,768]{1,0:T(8,128)(2,1)S(1)} %get-tuple-element.226), channel_id=1, source_target_pairs={{0,3},{1,2},{2,1},{3,0},{4,7},{5,6},{6,5},{7,4},{8,11},{9,10},{10,... | collective-permute-start | bytes 221192 | tf_op jit(solution)/shard_map/ppermute | solution.py:232
  456.5 7.1 %collective-permute-start.91 = (bf16[48,768]{1,0:T(8,128)(2,1)S(1)}, bf16[48,768]{1,0:T(8,128)(2,1)S(1)}, u32[]{:S(2)}, u32[]{:S(2)}) collective-permute-start(bf16[48,768]{1,0:T(8,128)(2,1)S(1)} %add_convert_fusion.27), channel_id=1, source_target_pairs={{0,2},{1,3},{2,0},{3,1},{4,6},{5,7},{6,4},{7,5},{8,10},{9,11},{10,... | collective-permute-start | bytes 221192 | tf_op jit(solution)/shard_map/ppermute | solution.py:232
  456.5 9.0 %collective-permute-start.92 = (bf16[48,768]{1,0:T(8,128)(2,1)S(1)}, bf16[48,768]{1,0:T(8,128)(2,1)S(1)}, u32[]{:S(2)}, u32[]{:S(2)}) collective-permute-start(bf16[48,768]{1,0:T(8,128)(2,1)S(1)} %add_convert_fusion.27), channel_id=1, source_target_pairs={{0,1},{1,0},{2,3},{3,2},{4,5},{5,4},{6,7},{7,6},{8,9},{9,8},{10,11... | collective-permute-start | bytes 221192 | tf_op jit(solution)/shard_map/ppermute | solution.py:232
  458.7 12.7 %collective-permute-start.81 = (bf16[48,3072]{1,0:T(8,128)(2,1)S(1)}, bf16[48,3072]{1,0:T(8,128)(2,1)S(1)}, u32[]{:S(2)}, u32[]{:S(2)}) collective-permute-start(bf16[48,3072]{1,0:T(8,128)(2,1)S(1)} %pad_maximum_fusion.13), channel_id=1, source_target_pairs={{0,8},{4,12},{8,0},{12,4},{16,24},{20,28},{24,16},{28,20},{1,9},{5... | collective-permute-start | bytes 884744 | tf_op jit(solution)/shard_map/ppermute | solution.py:232
  463.6 10.2 %collective-permute-start.71 = (bf16[48,3072]{1,0:T(8,128)(2,1)S(1)}, bf16[48,3072]{1,0:T(8,128)(2,1)S(1)}, u32[]{:S(2)}, u32[]{:S(2)}) collective-permute-start(bf16[48,3072]{1,0:T(8,128)(2,1)S(1)} %pad_maximum_fusion.12), channel_id=1, source_target_pairs={{0,16},{4,20},{8,24},{12,28},{16,0},{20,4},{24,8},{28,12},{1,17},{... | collective-permute-start | bytes 884744 | tf_op jit(solution)/shard_map/ppermute | solution.py:232
  465.4 12.2 %collective-permute-start.103 = (bf16[192,768]{1,0:T(8,128)(2,1)S(1)}, bf16[192,768]{1,0:T(8,128)(2,1)S(1)}, u32[]{:S(2)}, u32[]{:S(2)}) collective-permute-start(bf16[192,768]{1,0:T(8,128)(2,1)S(1)} %pad_maximum_fusion.15), channel_id=1, source_target_pairs={{0,8},{4,12},{8,0},{12,4},{16,24},{20,28},{24,16},{28,20},{1,9},{5... | collective-permute-start | bytes 884744 | tf_op jit(solution)/shard_map/ppermute | solution.py:232
  471.4 10.0 %collective-permute-start.93 = (bf16[192,768]{1,0:T(8,128)(2,1)S(1)}, bf16[192,768]{1,0:T(8,128)(2,1)S(1)}, u32[]{:S(2)}, u32[]{:S(2)}) collective-permute-start(bf16[192,768]{1,0:T(8,128)(2,1)S(1)} %pad_maximum_fusion.14), channel_id=1, source_target_pairs={{0,16},{4,20},{8,24},{12,28},{16,0},{20,4},{24,8},{28,12},{1,17},{... | collective-permute-start | bytes 884744 | tf_op jit(solution)/shard_map/ppermute | solution.py:232
  473.8 17.0 %collective-permute-start.82 = (bf16[96,3072]{1,0:T(8,128)(2,1)S(1)}, bf16[96,3072]{1,0:T(8,128)(2,1)S(1)}, u32[]{:S(2)}, u32[]{:S(2)}) collective-permute-start(bf16[96,3072]{1,0:T(8,128)(2,1)S(1)} %pad_maximum_fusion.8), channel_id=1, source_target_pairs={{0,16},{4,20},{8,24},{12,28},{16,0},{20,4},{24,8},{28,12},{1,17},{... | collective-permute-start | bytes 1769480 | tf_op jit(solution)/shard_map/ppermute | solution.py:232
  477.6 13.4 %collective-permute-start.72 = (bf16[96,3072]{1,0:T(8,128)(2,1)S(1)}, bf16[96,3072]{1,0:T(8,128)(2,1)S(1)}, u32[]{:S(2)}, u32[]{:S(2)}) collective-permute-start(bf16[96,3072]{1,0:T(8,128)(2,1)S(1)} %pad_maximum_fusion.7), channel_id=1, source_target_pairs={{0,8},{4,12},{8,0},{12,4},{16,24},{20,28},{24,16},{28,20},{1,9},{5... | collective-permute-start | bytes 1769480 | tf_op jit(solution)/shard_map/ppermute | solution.py:232
  481.4 18.8 %collective-permute-start.104 = (bf16[384,768]{1,0:T(8,128)(2,1)}, bf16[384,768]{1,0:T(8,128)(2,1)}, u32[]{:S(2)}, u32[]{:S(2)}) collective-permute-start(bf16[384,768]{1,0:T(8,128)(2,1)} %pad_maximum_fusion.10), channel_id=1, source_target_pairs={{0,16},{4,20},{8,24},{12,28},{16,0},{20,4},{24,8},{28,12},{1,17},{... | collective-permute-start | bytes 1769480 | tf_op jit(solution)/shard_map/ppermute | solution.py:232
  493.7 53.2 %collective-permute-start.83 = (bf16[384,3072]{1,0:T(8,128)(2,1)}, bf16[384,3072]{1,0:T(8,128)(2,1)}, u32[]{:S(2)}, u32[]{:S(2)}) collective-permute-start(bf16[384,3072]{1,0:T(8,128)(2,1)} %pad_maximum_fusion), channel_id=1, source_target_pairs={{0,4},{4,0},{8,12},{12,8},{16,20},{20,16},{24,28},{28,24},{1,5},{5... | collective-permute-start | bytes 7077896 | tf_op jit(solution)/shard_map/ppermute | solution.py:232
  494.5 16.1 %collective-permute-start.94 = (bf16[384,768]{1,0:T(8,128)(2,1)}, bf16[384,768]{1,0:T(8,128)(2,1)}, u32[]{:S(2)}, u32[]{:S(2)}) collective-permute-start(bf16[384,768]{1,0:T(8,128)(2,1)} %pad_maximum_fusion.9), channel_id=1, source_target_pairs={{0,8},{4,12},{8,0},{12,4},{16,24},{20,28},{24,16},{28,20},{1,9},{5... | collective-permute-start | bytes 1769480 | tf_op jit(solution)/shard_map/ppermute | solution.py:232
  513.5 40.8 %collective-permute-start.105 = (bf16[1536,768]{1,0:T(8,128)(2,1)}, bf16[1536,768]{1,0:T(8,128)(2,1)}, u32[]{:S(2)}, u32[]{:S(2)}) collective-permute-start(bf16[1536,768]{1,0:T(8,128)(2,1)} %pad_maximum_fusion.1), channel_id=1, source_target_pairs={{0,4},{4,0},{8,12},{12,8},{16,20},{20,16},{24,28},{28,24},{1,5},{5... | collective-permute-start | bytes 7077896 | tf_op jit(solution)/shard_map/ppermute | solution.py:232
  514.3 12.1 %collective-permute-start.54 = (bf16[192,768]{1,0:T(8,128)(2,1)}, bf16[192,768]{1,0:T(8,128)(2,1)}, u32[]{:S(2)}, u32[]{:S(2)}) collective-permute-start(bf16[192,768]{1,0:T(8,128)(2,1)} %pad_maximum_fusion.11), channel_id=1, source_target_pairs={{0,3},{1,2},{2,1},{3,0},{4,7},{5,6},{6,5},{7,4},{8,11},{9,10},{10,... | collective-permute-start | bytes 884744 | tf_op jit(solution)/shard_map/ppermute | solution.py:232
  516.2 27.5 %collective-permute-start.55 = (bf16[192,768]{1,0:T(8,128)(2,1)}, bf16[192,768]{1,0:T(8,128)(2,1)}, u32[]{:S(2)}, u32[]{:S(2)}) collective-permute-start(bf16[192,768]{1,0:T(8,128)(2,1)} %pad_maximum_fusion.11), channel_id=1, source_target_pairs={{0,2},{1,3},{2,0},{3,1},{4,6},{5,7},{6,4},{7,5},{8,10},{9,11},{10,... | collective-permute-start | bytes 884744 | tf_op jit(solution)/shard_map/ppermute | solution.py:232
  517.1 26.7 %collective-permute-start.56 = (bf16[192,768]{1,0:T(8,128)(2,1)}, bf16[192,768]{1,0:T(8,128)(2,1)}, u32[]{:S(2)}, u32[]{:S(2)}) collective-permute-start(bf16[192,768]{1,0:T(8,128)(2,1)} %pad_maximum_fusion.11), channel_id=1, source_target_pairs={{0,1},{1,0},{2,3},{3,2},{4,5},{5,4},{6,7},{7,6},{8,9},{9,8},{10,11... | collective-permute-start | bytes 884744 | tf_op jit(solution)/shard_map/ppermute | solution.py:232
  (145 other events, 974.3 us)

commit v2 on v1

--- a/solution.py
+++ b/solution.py
@@ -228,6 +228,831 @@
     )(x, w, ow, q, k, v, ctx, lse, ga, acc)
 
 
+MESH = pl.DeviceIdType.MESH
+
+
+class Place:
+    def __init__(self):
+        self.dp = lax.axis_index("dp")
+        self.h = lax.axis_index("head")
+        self.c = self.dp & 1
+        self.x = (self.dp >> 1) & 1
+        self.y = (self.dp >> 2) & 1
+
+    def core(self):
+        return (self.dp ^ 1, self.h)
+
+    def side(self, axis):
+        return (self.dp ^ (2 if axis == "x" else 4), self.h)
+
+    def up(self, offset):
+        return (self.dp, self.h ^ offset)
+
+
+def remote(src, dst, send, recv, where):
+    return pltpu.make_async_remote_copy(
+        src_ref=src,
+        dst_ref=dst,
+        send_sem=send,
+        recv_sem=recv,
+        device_id=where,
+        device_id_type=MESH,
+    )
+
+
+def greet(friends):
+    barrier = pltpu.get_barrier_semaphore()
+    for friend in friends:
+        pl.semaphore_signal(barrier, inc=1, device_id=friend, device_id_type=MESH)
+    pl.semaphore_wait(barrier, len(friends))
+
+
+def early_kernel(
+    x_ref,
+    own_ref,
+    bias_ref,
+    ow_ref,
+    ob_ref,
+    q_ref,
+    k_ref,
+    v_ref,
+    ctx_ref,
+    lse_ref,
+    out_ref,
+    w_out,
+    w_all,
+    b_all,
+    send,
+    recv,
+    local,
+):
+    step = pl.program_id(0)
+    group, row = step // 2, step % 2
+    place = Place()
+    features = w_all.shape[2]
+    width = w_all.shape[3]
+    heads = width // HEAD_DIM
+    half = features // 2
+    rows = pl.ds(pl.multiple_of(place.c * half, half), half)
+
+    load = pltpu.make_async_copy(own_ref, w_all.at[0], local.at[0])
+
+    def part(g):
+        return w_all.at[g, :, rows, :]
+
+    def direct(g):
+        return remote(own_ref.at[:, rows, :], part(g), send.at[0, g], recv.at[0, g], place.up(g))
+
+    relay = remote(part(2), part(3), send.at[0, 3], recv.at[0, 3], place.up(1))
+
+    def cross(g):
+        return remote(part(g), part(g), send.at[1, g], recv.at[1, g], place.core())
+
+    def bias(g):
+        return remote(bias_ref, b_all.at[g], send.at[2, g], recv.at[2, g], place.up(g))
+
+    def store(g):
+        return pltpu.make_async_copy(w_all.at[g], w_out.at[g], local.at[2 + g])
+
+    @pl.when(step == 0)
+    def _():
+        greet([place.core()] + [place.up(o) for o in range(1, 4)])
+        load.start()
+        bias_load = pltpu.make_async_copy(bias_ref, b_all.at[0], local.at[1])
+        bias_load.start()
+        for g in range(1, 4):
+            bias(g).start()
+        direct(1).start()
+        direct(2).start()
+        load.wait()
+        bias_load.wait()
+        store(0).start()
+
+    for g in range(1, 4):
+
+        @pl.when(step == 2 * g)
+        def _():
+            cross(g).wait()
+            bias(g).wait()
+            store(g).start()
+
+    x = x_ref[...]
+    q = (dot_nn(x, w_all[group, 0]) + b_all[group, 0:1, :]).astype(BF)
+    k = dot_nn(x, w_all[group, 1]).astype(BF)
+    v = (dot_nn(x, w_all[group, 2]) + b_all[group, 1:2, :]).astype(BF)
+    q_ref[0] = q
+    k_ref[0] = k
+    v_ref[0] = v
+    v_t = v.T
+    q_scaled = q * jnp.asarray(0.125, BF)
+    pieces = []
+    for head in range(heads):
+        k_head = jnp.where(head_lanes(width, head), k, jnp.zeros_like(k))
+        scores = dot_nt(k_head, q_scaled)
+        highest = jnp.max(scores, axis=0, keepdims=True)
+        exponent = jnp.exp(scores - highest)
+        totals = jnp.sum(exponent, axis=0, keepdims=True)
+        probs = (exponent * (1.0 / totals)).astype(BF)
+        pieces.append(dot_nn(v_t[head * HEAD_DIM : (head + 1) * HEAD_DIM], probs))
+        lse_ref[0, 0, head : head + 1, :] = highest + jnp.log(totals)
+    ctx = jnp.concatenate(pieces, axis=0).T.astype(BF)
+    ctx_ref[0] = ctx
+    result = dot_nn(ctx, ow_ref[place.h ^ group])
+    spot = pl.ds(pl.multiple_of(row * LEN, LEN), LEN)
+
+    @pl.when(group == 0)
+    def _():
+        out_ref[spot, :] = result + ob_ref[...]
+
+    @pl.when(group > 0)
+    def _():
+        out_ref[spot, :] = out_ref[spot, :] + result
+
+    @pl.when(step == 1)
+    def _():
+        direct(1).wait()
+        cross(1).start()
+
+    @pl.when(step == 3)
+    def _():
+        direct(2).wait()
+        cross(2).start()
+        relay.start()
+
+    @pl.when(step == 5)
+    def _():
+        relay.wait()
+        cross(3).start()
+
+    @pl.when(step == 7)
+    def _():
+        for g in range(4):
+            store(g).wait()
+
+
+def early_call(x, own, bias, ow, ob):
+    tokens, features = x.shape
+    width = own.shape[2]
+    groups = features // width
+    rows = tokens // LEN
+    hbm = pl.BlockSpec(memory_space=pl.ANY)
+    per_head = pl.BlockSpec((1, LEN, width), lambda s: (s // 2, s % 2, 0))
+    stacked = jax.ShapeDtypeStruct((groups, tokens, width), BF)
+    dma = pltpu.SemaphoreType.DMA
+    return pl.pallas_call(
+        early_kernel,
+        grid=(groups * rows,),
+        in_specs=[
+            pl.BlockSpec((LEN, features), lambda s: (s % 2, 0)),
+            hbm,
+            hbm,
+            pl.BlockSpec((groups, width, features), lambda s: (0, 0, 0)),
+            pl.BlockSpec((1, features), lambda s: (0, 0)),
+        ],
+        out_specs=[
+            per_head,
+            per_head,
+            per_head,
+            per_head,
+            pl.BlockSpec((1, 1, 8, LEN), lambda s: (s // 2, s % 2, 0, 0)),
+            pl.BlockSpec((tokens, features), lambda s: (0, 0)),
+            hbm,
+        ],
+        out_shape=[
+            stacked,
+            stacked,
+            stacked,
+            stacked,
+            jax.ShapeDtypeStruct((groups, rows, 8, LEN), F32),
+            jax.ShapeDtypeStruct((tokens, features), F32),
+            jax.ShapeDtypeStruct((groups,) + own.shape, BF),
+        ],
+        scratch_shapes=[
+            pltpu.VMEM((groups,) + own.shape, BF),
+            pltpu.VMEM((groups, 8, width), F32),
+            dma((3, 4)),
+            dma((3, 4)),
+            dma((6,)),
+        ],
+        compiler_params=pltpu.CompilerParams(
+            dimension_semantics=("arbitrary",),
+            vmem_limit_bytes=56 << 20,
+            collective_id=0,
+            has_side_effects=True,
+        ),
+        name="early_kernel",
+    )(x, own, bias, ow, ob)
+
+
+LANES = 384
+CHUNK = 512
+TICKS = 3
+SPACING = 2
+
+
+def add_into(target, source):
+    target[...] = (target[...].astype(F32) + source[...].astype(F32)).astype(BF)
+
+
+class MatrixSum:
+    COPIES = 17
+
+    def __init__(self, place, parts, keep, first, second, third, fourth, full, send, recv, local):
+        self.place = place
+        self.parts = parts
+        self.keep, self.first, self.second = keep, first, second
+        self.third, self.fourth, self.full = third, fourth, full
+        self.send, self.recv, self.local = send, recv, local
+
+    def copy(self, i, slot, src, dst, where):
+        return remote(src, dst, self.send.at[i, slot], self.recv.at[i, slot], where)
+
+    def fetches(self, i, source, index):
+        p = self.place
+        out = []
+        for zl in range(2):
+            lanes = pl.ds(zl * LANES, LANES)
+            out.append(
+                pltpu.make_async_copy(
+                    source.at[index, p.c, :, :, :, :, :, lanes],
+                    self.keep.at[i, :, :, :, :, zl],
+                    self.local.at[i, zl],
+                )
+            )
+        return out
+
+    def copies(self, phase, i, source=None, index=None):
+        p = self.place
+        keep, full = self.keep, self.full
+        if phase == 1:
+            return [
+                self.copy(
+                    i,
+                    zl,
+                    source.at[index, 1 - p.c, :, :, :, :, :, pl.ds(zl * LANES, LANES)],
+                    self.first.at[i, :, :, :, :, zl],
+                    p.core(),
+                )
+                for zl in range(2)
+            ]
+        if phase == 2:
+            out = [
+                self.copy(i, 2, keep.at[i, 0, 1 - p.x], self.second.at[i, 0], p.side("x")),
+                self.copy(i, 3, keep.at[i, 1, :, 1 - p.y], self.second.at[i, 1], p.side("y"))
+                if self.parts == 2
+                else None,
+            ]
+        if phase == 3:
+            out = [
+                self.copy(i, 4, keep.at[i, 0, p.x, 1 - p.y], self.third.at[i, 0], p.side("y")),
+                self.copy(i, 5, keep.at[i, 1, 1 - p.x, p.y], self.third.at[i, 1], p.side("x"))
+                if self.parts == 2
+                else None,
+            ]
+        if phase == 4:
+            out = []
+            for o in range(1, 4):
+                t = p.h ^ o
+                out.append(
+                    self.copy(
+                        i,
+                        5 + o,
+                        keep.at[i, :, p.x, p.y, t >> 1, t & 1],
+                        self.fourth.at[i, o - 1],
+                        p.up(o),
+                    )
+                )
+        if phase == 5:
+            spot = full.at[i, p.c, :, p.x, p.y, p.h >> 1, p.h & 1]
+            out = [self.copy(i, 8 + o, spot, spot, p.up(o)) for o in range(1, 4)]
+        if phase == 6:
+            spot = full.at[i, p.c, 0, p.x, p.y]
+            out = [self.copy(i, 12, spot, spot, p.side("y"))]
+            if self.parts == 2:
+                spot = full.at[i, p.c, 1, p.x, p.y]
+                out.append(self.copy(i, 13, spot, spot, p.side("x")))
+        if phase == 7:
+            spot = full.at[i, p.c, 0, p.x]
+            out = [self.copy(i, 14, spot, spot, p.side("x"))]
+            if self.parts == 2:
+                spot = full.at[i, p.c, 1, :, p.y]
+                out.append(self.copy(i, 15, spot, spot, p.side("y")))
+        if phase == 8:
+            spot = full.at[i, p.c]
+            out = [self.copy(i, 16, spot, spot, p.core())]
+        return [one for one in out if one is not None]
+
+    def begin(self, i, source, index):
+        for one in self.fetches(i, source, index) + self.copies(1, i, source, index):
+            one.start()
+
+    def advance(self, phase, i, source=None, index=None):
+        p = self.place
+        if phase == 2:
+            for one in self.fetches(i, source, index):
+                one.wait()
+        for one in self.copies(phase - 1, i, source, index):
+            one.wait()
+        if phase == 2:
+            add_into(self.keep.at[i], self.first.at[i])
+        if phase == 3:
+            add_into(self.keep.at[i, 0, p.x], self.second.at[i, 0])
+            if self.parts == 2:
+                add_into(self.keep.at[i, 1, :, p.y], self.second.at[i, 1])
+        if phase == 4:
+            for part in range(self.parts):
+                add_into(self.keep.at[i, part, p.x, p.y], self.third.at[i, part])
+        if phase == 5:
+            total = self.keep[i, :, p.x, p.y, p.h >> 1, p.h & 1].astype(F32)
+            for o in range(3):
+                total = total + self.fourth[i, o].astype(F32)
+            self.full[i, p.c, :, p.x, p.y, p.h >> 1, p.h & 1] = total.astype(BF)
+        if phase <= 8:
+            for one in self.copies(phase, i):
+                one.start()
+
+
+class GroupSum:
+    def __init__(self, place, own, first, second, third, fourth, full, send, recv):
+        self.place = place
+        self.own, self.first, self.second = own, first, second
+        self.third, self.fourth, self.full = third, fourth, full
+        self.send, self.recv = send, recv
+
+    def copy(self, g, slot, src, dst, where):
+        return remote(src, dst, self.send.at[g, slot], self.recv.at[g, slot], where)
+
+    def copies(self, phase, g):
+        p, own, full = self.place, self.own, self.full
+        if phase == 1:
+            return [self.copy(g, 0, own.at[g, 1 - p.c], self.first.at[g], p.core())]
+        even = g % 2 == 0
+        if phase == 2:
+            src = own.at[g, p.c, 1 - p.x] if even else own.at[g, p.c, :, 1 - p.y]
+            return [self.copy(g, 1, src, self.second.at[g], p.side("x" if even else "y"))]
+        if phase == 3:
+            src = own.at[g, p.c, p.x, 1 - p.y] if even else own.at[g, p.c, 1 - p.x, p.y]
+            return [self.copy(g, 2, src, self.third.at[g], p.side("y" if even else "x"))]
+        if phase == 4:
+            if g == 0:
+                return []
+            src = own.at[g, p.c, p.x, p.y]
+            return [self.copy(g, 3, src, self.fourth.at[g - 1], p.up(g))]
+        if phase == 6:
+            spot = full.at[p.c, p.x, p.y]
+            return [self.copy(0, 4, spot, spot, p.side("y"))]
+        if phase == 7:
+            spot = full.at[p.c, p.x]
+            return [self.copy(0, 5, spot, spot, p.side("x"))]
+        if phase == 8:
+            spot = full.at[p.c]
+            return [self.copy(0, 6, spot, spot, p.core())]
+        return []
+
+    def begin(self, g):
+        for one in self.copies(1, g):
+            one.start()
+
+    def advance(self, phase, g):
+        p, own = self.place, self.own
+        if phase == 6:
+            for group in range(own.shape[0]):
+                for one in self.copies(4, group):
+                    one.wait()
+            total = own[0, p.c, p.x, p.y].astype(F32)
+            for o in range(3):
+                total = total + self.fourth[o].astype(F32)
+            self.full[p.c, p.x, p.y] = total.astype(BF)
+        else:
+            for one in self.copies(phase - 1, g):
+                one.wait()
+        if phase == 2:
+            add_into(own.at[g, p.c], self.first.at[g])
+        if phase == 3:
+            if g % 2 == 0:
+                add_into(own.at[g, p.c, p.x], self.second.at[g])
+            else:
+                add_into(own.at[g, p.c, :, p.y], self.second.at[g])
+        if phase == 4:
+            add_into(own.at[g, p.c, p.x, p.y], self.third.at[g])
+        for one in self.copies(phase, g):
+            one.start()
+
+
+def late_kernel(
+    chunks,
+    x_ref,
+    w_ref,
+    ow_ref,
+    q_ref,
+    k_ref,
+    v_ref,
+    lse_ref,
+    ga_ref,
+    gf_ref,
+    mask_ref,
+    early_0,
+    early_1,
+    early_2,
+    early_3,
+    early_4,
+    early_5,
+    early_up,
+    early_squares,
+    down_ref,
+    up_ref,
+    outw_ref,
+    dx_ref,
+    wg_ref,
+    vec_ref,
+    down_out,
+    up_out,
+    outw_out,
+    wg_acc,
+    k_t,
+    dq_t,
+    dk_acc,
+    dv_acc,
+    stage_up,
+    vec,
+    vec_in,
+    ff_keep,
+    ff_1,
+    ff_2,
+    ff_3,
+    ff_4,
+    ff_full,
+    ow_keep,
+    ow_1,
+    ow_2,
+    ow_3,
+    ow_4,
+    ow_full,
+    qk_own,
+    qk_1,
+    qk_2,
+    qk_3,
+    qk_4,
+    qk_full,
+    ff_send,
+    ff_recv,
+    ff_local,
+    ow_send,
+    ow_recv,
+    ow_local,
+    qk_send,
+    qk_recv,
+    vec_send,
+    vec_recv,
+    store_sem,
+):
+    step = pl.program_id(0)
+    group, row = step // 2, step % 2
+    place = Place()
+    half = chunks // 2
+    count = qk_own.shape[0]
+    feed = MatrixSum(
+        place, 2, ff_keep, ff_1, ff_2, ff_3, ff_4, ff_full, ff_send, ff_recv, ff_local
+    )
+    outer = MatrixSum(
+        place, 1, ow_keep, ow_1, ow_2, ow_3, ow_4, ow_full, ow_send, ow_recv, ow_local
+    )
+    groups = GroupSum(place, qk_own, qk_1, qk_2, qk_3, qk_4, qk_full, qk_send, qk_recv)
+    tail = 2 * count * TICKS
+
+    @pl.when(step == 0)
+    def _():
+        greet(
+            [place.core(), place.side("x"), place.side("y")] + [place.up(o) for o in range(1, 4)]
+        )
+        vec[...] = jnp.zeros_like(vec)
+        for index, ref in enumerate((early_0, early_1, early_2, early_3, early_4, early_5)):
+            vec[0, index : index + 1, :] = ref[...]
+        vec[0, 6:10, :] = early_up[...]
+        vec[0, 10:11, :] = early_squares[...]
+
+    def lanes(zl):
+        return pl.ds(zl * LANES, LANES)
+
+    def down_store(i):
+        return [
+            pltpu.make_async_copy(
+                ff_full.at[i, :, :, :, :, :, zl],
+                down_out.at[i, :, :, :, :, :, :, lanes(zl)],
+                store_sem.at[i, zl],
+            )
+            for zl in range(2)
+        ]
+
+    def up_store(i):
+        spot = pl.ds(pl.multiple_of(i * CHUNK, CHUNK), CHUNK)
+        return pltpu.make_async_copy(
+            stage_up.at[i % 2], up_out.at[:, spot], store_sem.at[half + i, 0]
+        )
+
+    def outw_store():
+        return [
+            pltpu.make_async_copy(
+                ow_full.at[0, :, :, :, :, :, zl],
+                outw_out.at[0, :, :, :, :, :, :, lanes(zl)],
+                store_sem.at[chunks, zl],
+            )
+            for zl in range(2)
+        ]
+
+    def tick(t, start, stop):
+        for phase in range(9, 1, -1):
+            behind = SPACING * (phase - 1)
+            if stop - behind <= 0 or start - behind > chunks:
+                continue
+            i = t - behind
+
+            @pl.when((i >= 0) & (i < half))
+            def _():
+                feed.advance(phase, i, down_ref, i)
+                if phase == 9:
+                    for one in down_store(i):
+                        one.start()
+
+            @pl.when((i >= half) & (i < chunks))
+            def _():
+                feed.advance(phase, i, up_ref, i - half)
+                if phase == 9:
+
+                    @pl.when(i > half + 1)
+                    def _():
+                        up_store(i - half - 2).wait()
+
+                    for zl in range(2):
+                        block = ff_full[i, :, :, :, :, :, zl].reshape(CHUNK, LANES)
+                        stage_up[(i - half) % 2, zl * LANES : (zl + 1) * LANES, :] = block.T
+                    up_store(i - half).start()
+
+            @pl.when(i == chunks)
+            def _():
+                outer.advance(phase, 0, outw_ref, 0)
+                if phase == 9:
+                    for one in outw_store():
+                        one.start()
+
+        if start <= chunks:
+
+            @pl.when(t < half)
+            def _():
+                feed.begin(t, down_ref, t)
+
+            @pl.when((t >= half) & (t < chunks))
+            def _():
+                feed.begin(t, up_ref, t - half)
+
+            @pl.when(t == chunks)
+            def _():
+                outer.begin(0, outw_ref, 0)
+
+        for g in range(count):
+            base = 2 * TICKS * (g + 1)
+            if base < start or base >= stop:
+                continue
+            phases = (9, 8, 7, 6, 4, 3, 2) if g == count - 1 else (4, 3, 2)
+            for phase in phases:
+                when = phase - 1 if phase < 5 else phase - 2
+
+                @pl.when(t == base + when)
+                def _():
+                    groups.advance(phase, g)
+
+            @pl.when(t == base)
+            def _():
+                groups.begin(g)
+
+    width = q_ref.shape[2]
+    heads = width // HEAD_DIM
+    x = x_ref[...]
+    ga = ga_ref[...]
+    dctx = dot_nt(ga, ow_ref[place.h ^ group]).astype(BF)
+    q = q_ref[0]
+    k = k_ref[0]
+    v = v_ref[0]
+    k_t[...] = k.T
+    q_scaled = q * jnp.asarray(0.125, BF)
+
+    @pl.loop(0, heads)
+    def _(head):
+        tick(step * TICKS + head, 0, tail)
+        mask = head_lanes(width, head)
+        spot = pl.ds(pl.multiple_of(head * HEAD_DIM, HEAD_DIM), HEAD_DIM)
+        scores = dot_nt(jnp.where(mask, k, jnp.zeros_like(k)), q_scaled)
+        probs = jnp.exp(scores - lse_ref[0, 0, pl.ds(head, 1), :])
+        dprobs = dot_nt(jnp.where(mask, v, jnp.zeros_like(v)), dctx)
+        delta = jnp.sum(probs * dprobs, axis=0, keepdims=True)
+        dscores = (probs * (dprobs - delta)).astype(BF)
+        dv_acc[...] = jnp.where(mask, dot_nn(probs.astype(BF), dctx), dv_acc[...])
+        dk_acc[...] = jnp.where(mask, dot_nn(dscores, q_scaled), dk_acc[...])
+        dq_t[spot, :] = dot_nn(k_t[spot, :], dscores)
+
+    dq = (dq_t[...] * 0.125).T.astype(BF)
+    dk = dk_acc[...].astype(BF)
+    dv = dv_acc[...].astype(BF)
+    part = dot_nt(dq, w_ref[0, 0]) + dot_nt(dk, w_ref[0, 1]) + dot_nt(dv, w_ref[0, 2])
+    mine = pl.ds(pl.multiple_of(row * LEN, LEN), LEN)
+
+    @pl.when(group == 0)
+    def _():
+        dx_ref[mine, :] = gf_ref[...] + part
+
+    @pl.when(group > 0)
+    def _():
+        dx_ref[mine, :] = dx_ref[mine, :] + part
+
+    @pl.when(row == 0)
+    def _():
+        wg_acc[...] = jnp.zeros_like(wg_acc)
+
+    for index, grad in enumerate((dq, dk, dv)):
+        wg_acc[index * width : (index + 1) * width] += dot_tn(grad, x)
+    spot = place.h ^ group
+    vec[0, pl.ds(16 + spot, 1), 0:width] += jnp.sum(dq.astype(F32), axis=0, keepdims=True)
+    vec[0, pl.ds(20 + spot, 1), 0:width] += jnp.sum(dv.astype(F32), axis=0, keepdims=True)
+
+    @pl.when(row == 1)
+    def _():
+        shape = qk_own.shape[2:]
+        for zl in range(2):
+            block = wg_acc[:, zl * LANES : (zl + 1) * LANES].astype(BF)
+            qk_own[group, zl] = block.reshape(shape)
+
+    @pl.when(group == count - 1)
+    def _():
+        total = jnp.where(mask_ref[...] == 1.0, dx_ref[mine, :], 0.0)
+        vec[0, 15:16, :] += jnp.sum(total, axis=0, keepdims=True)
+
+    @pl.when(step == 2 * count - 1)
+    def _():
+        def vec_copy(k):
+            if k < 3:
+                where = (place.dp ^ (1 << k), place.h)
+            else:
+                where = (place.dp, place.h ^ (1 << (k - 3)))
+            return remote(vec.at[k], vec_in.at[k], vec_send.at[k], vec_recv.at[k], where)
+
+        @pl.loop(tail, tail + 8)
+        def _(t):
+            tick(t, tail, tail + 8)
+            for k in range(6):
+
+                @pl.when(t == tail + k)
+                def _():
+                    if k > 0:
+                        vec_copy(k - 1).wait()
+                        vec[k] = vec[k - 1] + vec_in[k - 1]
+                    if k < 5:
+                        vec_copy(k).start()
+
+        vec_ref[...] = vec[5]
+        for c in range(2):
+            block = qk_full[c].reshape(wg_ref.shape[0], LANES)
+            wg_ref[:, c * LANES : (c + 1) * LANES] = block.astype(F32)
+        for i in range(half):
+            for one in down_store(i):
+                one.wait()
+        for i in (half - 2, half - 1):
+            up_store(i).wait()
+        for one in outw_store():
+            one.wait()
+
+
+def late_call(x, w, ow, q, k, v, lse, ga, gf, mask, early, down, up, outw):
+    tokens, features = x.shape
+    count, _, _, width = w.shape
+    ff = down.shape[0]
+    chunks = 2 * ff // CHUNK
+    chunked = (ff // CHUNK, 2, 2, 2, 2, 2, 16, features)
+    squared = (1, 2, 1, 2, 2, 2, features // 16, features)
+    hbm = pl.BlockSpec(memory_space=pl.ANY)
+
+    def whole(shape):
+        return pl.BlockSpec(shape, lambda s: (0,) * len(shape))
+
+    per_head = pl.BlockSpec((1, LEN, width), lambda s: (s // 2, s % 2, 0))
+    per_row = pl.BlockSpec((LEN, features), lambda s: (s % 2, 0))
+    in_specs = [
+        per_row,
+        pl.BlockSpec((1, 3, features, width), lambda s: (s // 2, 0, 0, 0)),
+        whole(ow.shape),
+        per_head,
+        per_head,
+        per_head,
+        pl.BlockSpec((1, 1, 8, LEN), lambda s: (s // 2, s % 2, 0, 0)),
+        per_row,
+        pl.BlockSpec((LEN, features), lambda s: (jnp.minimum(s, 1), 0)),
+        pl.BlockSpec((LEN, 1), lambda s: (s % 2, 0)),
+    ]
+    in_specs += [whole(one.shape) for one in early]
+    in_specs += [hbm, hbm, hbm]
+    out_specs = [
+        whole((tokens, features)),
+        whole((3 * width, features)),
+        whole((24, features)),
+        hbm,
+        hbm,
+        hbm,
+    ]
+    out_shape = [
+        jax.ShapeDtypeStruct((tokens, features), F32),
+        jax.ShapeDtypeStruct((3 * width, features), F32),
+        jax.ShapeDtypeStruct((24, features), F32),
+        jax.ShapeDtypeStruct(chunked, BF),
+        jax.ShapeDtypeStruct((features, ff), BF),
+        jax.ShapeDtypeStruct(squared, BF),
+    ]
+
+    def sum_buffers(n, parts, rows):
+        block = (rows, LANES)
+        return [
+            pltpu.VMEM((n, parts, 2, 2, 2, 2) + block, BF),
+            pltpu.VMEM((n, parts, 2, 2, 2, 2) + block, BF),
+            pltpu.VMEM((n, parts, 2, 2, 2) + block, BF),
+            pltpu.VMEM((n, parts, 2, 2) + block, BF),
+            pltpu.VMEM((n, 3, parts) + block, BF),
+            pltpu.VMEM((n, 2, parts, 2, 2, 2, 2) + block, BF),
+        ]
+
+    qrows = 3 * width // 4
+    scratch = [
+        pltpu.VMEM((3 * width, features), F32),
+        pltpu.VMEM((width, LEN), BF),
+        pltpu.VMEM((width, LEN), F32),
+        pltpu.VMEM((LEN, width), F32),
+        pltpu.VMEM((LEN, width), F32),
+        pltpu.VMEM((2, features, CHUNK), BF),
+        pltpu.VMEM((6, 24, features), F32),
+        pltpu.VMEM((5, 24, features), F32),
+    ]
+    scratch += sum_buffers(chunks, 2, 16)
+    scratch += sum_buffers(1, 1, features // 16)
+    scratch += [
+        pltpu.VMEM((count, 2, 2, 2, qrows, LANES), BF),
+        pltpu.VMEM((count, 2, 2, qrows, LANES), BF),
+        pltpu.VMEM((count, 2, qrows, LANES), BF),
+        pltpu.VMEM((count, qrows, LANES), BF),
+        pltpu.VMEM((3, qrows, LANES), BF),
+        pltpu.VMEM((2, 2, 2, qrows, LANES), BF),
+    ]
+    dma = pltpu.SemaphoreType.DMA
+    scratch += [
+        dma((chunks, MatrixSum.COPIES)),
+        dma((chunks, MatrixSum.COPIES)),
+        dma((chunks, 2)),
+        dma((1, MatrixSum.COPIES)),
+        dma((1, MatrixSum.COPIES)),
+        dma((1, 2)),
+        dma((count, 7)),
+        dma((count, 7)),
+        dma((5,)),
+        dma((5,)),
+        dma((chunks + 1, 2)),
+    ]
+    results = pl.pallas_call(
+        functools.partial(late_kernel, chunks),
+        grid=(2 * count,),
+        in_specs=in_specs,
+        out_specs=out_specs,
+        out_shape=out_shape,
+        scratch_shapes=scratch,
+        compiler_params=pltpu.CompilerParams(
+            dimension_semantics=("arbitrary",),
+            vmem_limit_bytes=67043328,
+            collective_id=1,
+            has_side_effects=True,
+        ),
+        name="late_kernel",
+    )(
+        x,
+        w,
+        ow,
+        q,
+        k,
+        v,
+        lse,
+        ga,
+        gf,
+        mask,
+        *early,
+        down.reshape(chunked),
+        up.reshape(chunked),
+        outw.reshape(squared),
+    )
+    dx, wg, sums, down_sum, up_sum, outw_sum = results
+    return (
+        dx,
+        wg,
+        sums,
+        down_sum.reshape(ff, features),
+        up_sum,
+        outw_sum.reshape(features, features),
+    )
+
+
 def swap(value, axis, mask, size):
     return lax.ppermute(value, axis, [(i, i ^ mask) for i in range(size)])
 
@@ -389,31 +1214,39 @@
     inputs_wide = inputs.astype(F32)
     validity = valid_mask.astype(F32)[:, None]
 
+    direct = dp == 8 and head == 4 and features == 2 * LANES and tokens.shape[0] == 2 * LEN
     own = jnp.transpose(qkv_weight, (1, 0, 2))
-    core = bit_of("dp", 0)
-    half = lax.dynamic_slice_in_dim(own, core * (features // 2), features // 2, 1)
-    halves = [half]
-    for bit in range(head.bit_length() - 1):
-        halves = halves + [swap(part, "head", 1 << bit, head) for part in halves]
-    weights = [own] + [double(part, 0, dp, 1) for part in halves[1:]]
-    biases = jnp.stack([query_bias, value_bias]).astype(F32)
-    bias_parts = [biases]
-    for bit in range(head.bit_length() - 1):
-        bias_parts = bias_parts + [swap(part, "head", 1 << bit, head) for part in bias_parts]
-    out_parts = own_pieces(out_weight, head, 0)
-
-    attended = jnp.broadcast_to(out_bias[None, :], tokens.shape)
-    saved = []
-    for group in range(head):
-        q, k, v, ctx, lse, attended = attention_forward(
-            inputs,
-            weights[group],
-            bias_parts[group][0:1],
-            bias_parts[group][1:2],
-            out_parts[group],
-            attended,
+    if direct:
+        bias_block = jnp.pad(jnp.stack([query_bias, value_bias]).astype(F32), ((0, 6), (0, 0)))
+        out_parts = out_weight.reshape(head, width, features)
+        q, k, v, ctx, lse, attended, weights = early_call(
+            inputs, own, bias_block, out_parts, out_bias[None, :]
         )
-        saved.append((q, k, v, ctx, lse))
+    else:
+        core = bit_of("dp", 0)
+        half = lax.dynamic_slice_in_dim(own, core * (features // 2), features // 2, 1)
+        halves = [half]
+        for bit in range(head.bit_length() - 1):
+            halves = halves + [swap(part, "head", 1 << bit, head) for part in halves]
+        weights = [own] + [double(part, 0, dp, 1) for part in halves[1:]]
+        biases = jnp.stack([query_bias, value_bias]).astype(F32)
+        bias_parts = [biases]
+        for bit in range(head.bit_length() - 1):
+            bias_parts = bias_parts + [swap(part, "head", 1 << bit, head) for part in bias_parts]
+        out_parts = own_pieces(out_weight, head, 0)
+
+        attended = jnp.broadcast_to(out_bias[None, :], tokens.shape)
+        saved = []
+        for group in range(head):
+            q, k, v, ctx, lse, attended = attention_forward(
+                inputs,
+                weights[group],
+                bias_parts[group][0:1],
+                bias_parts[group][1:2],
+                out_parts[group],
+                attended,
+            )
+            saved.append((q, k, v, ctx, lse))
 
     normed, normal_first, inverse_first = norm_forward(
         inputs_wide + attended, norm1_gain, norm1_bias
@@ -430,14 +1263,11 @@
     grad_feed = grad_second.astype(BF)
     down_bias_grad = jnp.sum(grad_feed, axis=0, dtype=F32)
     down_local = dot_tn(activated, grad_feed).astype(BF)
-    down_weight_grad = all_reduce_matrix(down_local, dp, head, 0)
     slope = phi(preact) + preact * jnp.exp(-0.5 * preact * preact) * (
         1.0 / math.sqrt(2.0 * math.pi)
     )
     grad_preact = (dot_nt(grad_feed, down_weight) * slope).astype(BF)
     up_bias_grad = jnp.sum(grad_preact, axis=0, dtype=F32)
-    up_local = dot_tn(normed_low, grad_preact).astype(BF)
-    up_weight_grad = all_reduce_matrix(up_local, dp, head, 1)
     grad_normed = dot_nt(grad_preact, up_weight) + grad_second
     grad_first, gain_first_grad, bias_first_grad = norm_backward(
         grad_normed, normal_first, inverse_first, norm1_gain
@@ -462,6 +1292,65 @@
         up_bias_grad,
         squares,
     ]
+    if direct:
+        up_local = dot_tn(grad_preact, normed_low).astype(BF)
+        outw = lax.dot_general(
+            ctx, grad_attended, (((1,), (0,)), ((), ())), preferred_element_type=F32
+        ).astype(BF)
+        outw_local = absolute([outw[g] for g in range(head)], 0)
+        vectors = [one[None, :] for one in early[:6]]
+        vectors.append(up_bias_grad.reshape(-1, features))
+        vectors.append(jnp.pad(squares, (0, features - 4))[None, :])
+        dx, weight_sum, sums, down_sum, up_sum, outw_sum = late_call(
+            inputs,
+            weights,
+            out_parts,
+            q,
+            k,
+            v,
+            lse,
+            grad_attended,
+            grad_first,
+            (span_mask == 1).astype(F32)[:, None],
+            vectors,
+            down_local,
+            up_local,
+            outw_local,
+        )
+        tokens_grad = jnp.where(masked, 0.0, dx)
+        down_weight_grad = down_sum.astype(F32)
+        up_weight_grad = up_sum.astype(F32)
+        out_weight_grad = outw_sum.astype(F32)
+        weight_grad = jnp.transpose(weight_sum.reshape(3, width, features), (2, 0, 1))
+        me = lax.axis_index("head")
+        first_grad = lax.dynamic_slice(sums, (16 + me, 0), (1, width))[0]
+        third_grad = lax.dynamic_slice(sums, (20 + me, 0), (1, width))[0]
+        squares = sums[10, :4]
+        count = jnp.maximum(squares[3], 1.0)
+        stream_rms = jnp.sqrt(squares[:3] / (count * features))
+        return (
+            result.astype(BF),
+            tokens_grad,
+            sums[15],
+            weight_grad,
+            first_grad,
+            third_grad,
+            out_weight_grad,
+            sums[5],
+            sums[3],
+            sums[4],
+            up_weight_grad,
+            sums[6:10].reshape(-1),
+            down_weight_grad,
+            sums[0],
+            sums[1],
+            sums[2],
+            stream_rms,
+        )
+
+    up_local = dot_tn(normed_low, grad_preact).astype(BF)
+    down_weight_grad = all_reduce_matrix(down_local, dp, head, 0)
+    up_weight_grad = all_reduce_matrix(up_local, dp, head, 1)
     early_sum = all_reduce_small(jnp.concatenate(early), dp, head)
 
     grad_inputs = grad_first

time: 571 us -> 331 us (0.58); the launches traced: 562 us -> 330 us
  waiting for transfers between devices: 145 us -> 0 us
  Pallas kernels: 87.7 us -> 217 us
  starting transfers between devices: 114 us -> 0 us
  local copies, waits for them, and re-layouts: 77 us -> 16.2 us
  other arithmetic: 72.7 us -> 40.2 us
  matrix products: 61.5 us -> 54.7 us
    ppermute x106 -> x0, waiting for transfers between devices: 145 us -> none  [swap(): return lax.ppermute(value, axis, [(i, i ^ mask) for i in range(size)])]
    pallas_call x8 -> x2, Pallas kernels: 87.7 us -> 217 us  [the longest x1 153 us: late_call(): pl.pallas_call(functools.partial(late_kernel, chunks), grid=(2 * count,),...]
    ppermute x106 -> x0, starting transfers between devices: 114 us -> none  [swap(): return lax.ppermute(value, axis, [(i, i ^ mask) for i in range(size)])]
    dynamic_slice x44 -> x1, local copies, waits for them, and re-layouts: 25.7 us -> 1.34 us  [body(): third_grad = lax.dynamic_slice(sums, (20 + me, 0), (1, width))[0]]
    ppermute x11 -> x0, local copies, waits for them, and re-layouts: 18.7 us -> none  [swap(): return lax.ppermute(value, axis, [(i, i ^ mask) for i in range(size)])]
    concatenate x17 -> x0, other arithmetic: 17.3 us -> none  [the longest x14 14 us: joined(): return jnp.concatenate([low, high], axis=dim)]
    unnamed x208 -> x68, local copies, waits for them, and re-layouts: 18.7 us -> 4.3 us
    select_n x21 -> x1, other arithmetic: 13.2 us -> 1.95 us  [body(): tokens_grad = jnp.where(masked, 0.0, dx)]
  transfers between devices with their start and end apart: 106 -> 0, of which waited for: 53 -> 0; matrix products, arithmetic and copies ran while one was open for 18% -> 0% of each run, Pallas kernels for 4% -> 0%
where the time goes in v2:
time: 331 us; the launch traced here: 330 us
  Pallas kernels  217 us (66%)
  matrix products  54.7 us (17%)
  other arithmetic  40.2 us (12%)
  local copies, waits for them, and re-layouts  16.2 us (5%)
    pallas_call x1, Pallas kernels, late_call(): pl.pallas_call(functools.partial(late_kernel, chunks), grid=(2 * count,),...  153 us
    pallas_call x1, Pallas kernels, early_call(): pl.pallas_call(early_kernel, grid=(groups * rows,), in_specs=[pl.BlockSpe...  64.6 us
    dot_general x2, matrix products, dot_nt(): lax.dot_general(left, right, (((1,), (1,)), ((), ())), preferred_element_...  18.8 us
    dot_general x2, matrix products, dot_tn(): lax.dot_general(left, right, (((0,), (0,)), ((), ())), preferred_element_...  18.5 us
    dot_general x2, matrix products, dot_nn(): lax.dot_general(left, right, (((1,), (0,)), ((), ())), preferred_element_...  14.8 us
    convert_element_type x1, other arithmetic, body(): down_weight_grad = down_sum.astype(F32)  6.97 us

profile of v2, /device:TPU:0, one launch (start us, length us, event | category | flops | bytes accessed | tf_op | source)
XLA Modules:
  0.0 330.1 jit_solution(4461763183636188022)
XLA Ops:
  0.7 0.8 fusion.27
  1.5 2.8 broadcast_select_fusion.1.x_ref
  4.2 1.4 copy.37
  5.7 0.6 fusion.21.bias_ref
  6.3 0.0 copy-done.19
  6.3 0.6 broadcast_in_dim.76.ob_ref
  6.9 64.6 %early_kernel.1 = (bf16[4,1024,192]{2,1,0:T(8,128)(2,1)}, bf16[4,1024,192]{2,1,0:T(8,128)(2,1)}, bf16[4,1024,192]{2,1,0:T(8,128)(2,1)}, bf16[4,1024,192]{2,1,0:T...) custom-call(bf16[1024,768]{1,0:T(8,128)(2,1)} %broadcast_select_fusion.1.x_ref, ...), custom_call_target="tpu_custom_call" | custom-call | tf_op jit(solution)/shard_map/early_kernel/pallas_call | solution.py:402
  71.5 0.0 slice-start.2
  71.5 0.0 copy-done.13
  71.5 0.0 slice-start.3
  71.5 3.2 fusion.29
  74.7 0.0 copy-start.18
  74.7 0.0 copy-start.21
  74.8 0.0 copy-start.22
  74.8 0.0 slice-start
  74.8 0.5 multiply_reduce_fusion.5
  75.3 0.0 slice-done.2
  75.3 0.2 copy-done.18
  75.5 0.0 copy-done.21
  75.6 9.4 %multiply_convert_fusion = (bf16[1024,3072]{1,0:T(8,128)(2,1)S(1)}, f32[1024,3072]{1,0:T(8,128)}) fusion(f32[3072]{0:T(1024)S(1)} %copy-done.21, bf16[768,3072]{1,0:T(8,128)(2,1)S(1)} %bitcast.59, f32[1024,768]{1,0:T(8,128)S(1)} %get-tuple-element.75, f32[768]{0:T(1024)S(1)} %copy-done.22, f32[768]{0:T(1024)S(1)} %copy-done.18, ...), kind=kOutput, calls=%fused_computation.8 | convolution fusion | flops 4854644736 | bytes 26765312 | tf_op jit(solution)/shard_map/dot_general | solution.py:19
  85.0 5.5 %fusion.28 = (f32[1024]{0:T(1024)S(1)}, f32[1024,768]{1,0:T(8,128)S(1)}, f32[1024,768]{1,0:T(8,128)S(1)}) fusion(f32[768]{0:T(1024)S(1)} %copy-done.16, f32[768]{0:T(1024)S(1)} %copy-done.22, f32[768]{0:T(1024)S(1)} %copy-done.18, f32[1024]{0:T(1024)S(1)} %add_rsqrt_fusion.1, f32[1024,768]{1,0:T(8,128)S(1)} %get-tuple-element.75, ...), kind=kOutput, calls=%fused_computation.90 | convolution fusion | flops 4837342208 | bytes 20468736 | tf_op jit(solution)/shard_map/dot_general | solution.py:19
  90.5 0.0 copy-start.15
  90.5 0.0 copy-start
  90.5 0.0 copy-start.2
  90.5 0.0 copy-start.14
  90.5 0.5 multiply_reduce_fusion.4
  91.1 0.1 copy-done.15
  91.2 0.7 copy-done
  91.9 0.5 copy-done.2
  92.4 4.2 %fusion.6 = (f32[]{:T(128)}, f32[]{:T(128)}, f32[]{:T(128)}, f32[768]{0:T(1024)S(1)}, f32[1024]{0:T(1024)S(1)}, /*index=5*/f32[1024]{0:T(1024)S(1)}, f32[768]{0:T(1024)S(1)}) fusion(f32[1024]{0:T(1024)S(1)} %convert_element_type.71, f32[1024,768]{1,0:T(8,128)S(1)} %copy-done.1, f32[1024,768]{1,0:T(8,128)S(1)} %get-tuple-element.85, f32[768]{0:T(1024)S(1)} %copy-done.16, ...), kind=kLoop, calls=%fused_computation.17 | loop fusion | flops 18084348 | bytes 12618252 | tf_op jit(solution)/shard_map/reduce_sum | solution.py:1279
  96.6 2.8 convert_reduce_fusion.2
  99.4 12.8 %convert_reduce_fusion = (f32[3072]{0:T(1024)S(1)}, bf16[1024,3072]{1,0:T(8,128)(2,1)S(1)}) fusion(f32[1024,3072]{1,0:T(8,128)} %get-tuple-element.84, f32[3072]{0:T(1024)S(1)} %copy-done.21, bf16[3072,768]{1,0:T(8,128)(2,1)S(1)} %bitcast.57, f32[1024,768]{1,0:T(8,128)S(1)} %get-tuple-element.69), kind=kOutput, calls=%fused_computation.7 | convolution fusion | flops 4873516032 | bytes 26763264 | tf_op jit(solution)/shard_map/dot_general | solution.py:23
  112.2 0.0 copy-start.26
  112.2 6.1 %multiply_reduce_fusion = (f32[768]{0:T(1024)S(1)}, f32[1024]{0:T(1024)S(1)}, f32[1024]{0:T(1024)S(1)}, f32[768]{0:T(1024)S(1)}, f32[1024,768]{1,0:T(8,128)S(1)}) fusion(f32[1024,768]{1,0:T(8,128)S(1)} %get-tuple-element.75, f32[1024]{0:T(1024)S(1)} %add_rsqrt_fusion.1, f32[1024]{0:T(1024)S(1)} %broadcast_multiply_fusion.5, f32[768]{0:T(1024)S(1)} %copy-done.18, ...), kind=kOutput, calls=%fused_computation.21 | convolution fusion | flops 4839698432 | bytes 20472832 | tf_op jit(solution)/shard_map/dot_general | solution.py:23
  118.3 2.3 convert_reduce_fusion.1
  120.6 2.6 fusion.15
  123.2 1.3 select_bitcast_fusion.3
  124.5 0.0 slice-start.4
  124.5 1.1 pad_maximum_fusion
  125.6 11.3 %convolution_convert_fusion = bf16[3072,768]{1,0:T(8,128)(2,1)} fusion(bf16[1024,3072]{1,0:T(8,128)(2,1)} %copy-done.26, f32[1024,768]{1,0:T(8,128)S(1)} %get-tuple-element.75, f32[768]{0:T(1024)S(1)} %copy-done.22, f32[768]{0:T(1024)S(1)} %copy-done.18, f32[1024]{0:T(1024)S(1)} %add_rsqrt_fusion.1, f32[1024]{0:T(1024)S(1)} %broadcast_multiply_fusion.5), kind=kOutput, calls=%fused_computation.10 | convolution fusion | flops 4838129664 | bytes 14170112 | tf_op jit(solution)/shard_map/dot_general | solution.py:27
  137.0 7.2 %convolution_convert_fusion.1 = bf16[3072,768]{1,0:T(8,128)(2,1)} fusion(bf16[1024,3072]{1,0:T(8,128)(2,1)S(1)} %bitcast.61, f32[1024,768]{1,0:T(8,128)S(1)} %copy-done.6), kind=kOutput, calls=%fused_computation.11 | convolution fusion | flops 4834983936 | bytes 14155776 | tf_op jit(solution)/shard_map/dot_general | solution.py:27
  144.2 0.6 convert_reduce_fusion.3
  144.8 2.7 select_maximum_fusion
  147.4 0.6 broadcast_in_dim.86.early_squares
  148.0 0.6 broadcast_in_dim.85.early_5
  148.6 0.6 broadcast_in_dim.83.early_3
  149.2 0.6 broadcast_in_dim.84.early_4
  149.8 0.6 reshape.137.early_up
  150.4 0.6 broadcast_in_dim.80.early_0
  150.9 0.6 broadcast_in_dim.81.early_1
  151.5 0.6 broadcast_in_dim.82.early_2
  152.1 1.0 copy.39.mask_ref
  153.1 152.6 %late_kernel.1 = (f32[1024,768]{1,0:T(8,128)}, f32[576,768]{1,0:T(8,128)}, f32[24,768]{1,0:T(8,128)}, bf16[6,2,2,2,2,2,16,768]{7,6,5,4,3,2,1,0:T(8,128)(2,1)}, b...) custom-call(bf16[1024,768]{1,0:T(8,128)(2,1)} %broadcast_select_fusion.1.x_ref, ...), custom_call_target="tpu_custom_call" | custom-call | tf_op jit(solution)/shard_map/late_kernel/pallas_call | solution.py:1015
  305.8 1.3 slice.60
  307.7 1.2 sqrt_bitcast_fusion
  308.9 7.0 %bitcast_convert_fusion = f32[3072,768]{1,0:T(8,128)} fusion(bf16[6,2,2,2,2,2,16,768]{7,6,5,4,3,2,1,0:T(8,128)(2,1)} %get-tuple-element.42), kind=kLoop, calls=%fused_computation.15 | loop fusion | flops 2359296 | bytes 14155776 | tf_op jit(solution)/shard_map/convert_element_type | solution.py:1321
  315.9 5.0 %convert_element_type.83 = f32[768,3072]{1,0:T(8,128)} convert(bf16[768,3072]{1,0:T(8,128)(2,1)S(1)} %copy-done.4) | non-fusion elementwise | flops 2359296 | bytes 14155776 | tf_op jit(solution)/shard_map/convert_element_type | solution.py:1322
  320.9 2.0 broadcast_select_fusion
  322.9 1.7 bitcast_convert_fusion.1
  324.5 1.6 slice_reduce_fusion
  326.2 0.8 slice.55
  327.0 0.6 reshape.142
  327.6 1.3 constant_dynamic-slice_fusion
  328.9 1.2 copy.42
  (59 shorter events, 0.1 us)
Async XLA Ops:
  0.7 3.6 %copy-start.10 = (bf16[768,3,192]{0,2,1:T(8,128)(2,1)S(1)}, bf16[768,3,192]{0,2,1:T(8,128)(2,1)}, u32[]{:S(2)}) copy-start(bf16[768,3,192]{0,2,1:T(8,128)(2,1)} %param.22) | copy-start | bytes 2654212
  0.7 5.0 %copy-start.23 = (bf16[192]{0:T(256)(128)(2,1)S(1)}, bf16[192]{0:T(256)(128)(2,1)}, u32[]{:S(2)}) copy-start(bf16[192]{0:T(256)(128)(2,1)} %param.23) | copy-start | bytes 1156
  0.7 5.0 %copy-start.24 = (bf16[192]{0:T(256)(128)(2,1)S(1)}, bf16[192]{0:T(256)(128)(2,1)}, u32[]{:S(2)}) copy-start(bf16[192]{0:T(256)(128)(2,1)} %param.24) | copy-start | bytes 1156
  0.7 5.6 %copy-start.19 = (f32[768]{0:T(1024)S(1)}, f32[768]{0:T(1024)}, u32[]{:S(2)}) copy-start(f32[768]{0:T(1024)} %param.26) | copy-start | bytes 9220
  1.5 89.7 %copy-start.11 = (pred[1024]{0:T(1024)(128)(4,1)}, pred[1024]{0:T(1024)(128)(4,1)S(1)}, u32[]{:S(2)}) copy-start(pred[1024]{0:T(1024)(128)(4,1)S(1)} %get-tuple-element.71) | copy-start | bytes 3076
  4.2 67.3 %copy-start.13 = (bf16[768]{0:T(1024)(128)(2,1)S(1)}, bf16[768]{0:T(1024)(128)(2,1)}, u32[]{:S(2)}) copy-start(bf16[768]{0:T(1024)(128)(2,1)} %param.21) | copy-start | bytes 4612
  71.5 3.8 %slice-start.2 = ((s8[4718592]{0:T(1024)(128)(4,1)}), s8[4194304]{0:T(1024)(128)(4,1)S(1)}, s32[]{:S(2)}) async-start(s8[4718592]{0:T(1024)(128)(4,1)} %bitcast.58), calls=%async_computation.2 | async-start | bytes 8388608
  71.5 3.8 %slice-start.3 = ((s8[4718592]{0:T(1024)(128)(4,1)}), s8[524288]{0:T(1024)(128)(4,1)S(1)}, s32[]{:S(2)}) async-start(s8[4718592]{0:T(1024)(128)(4,1)} %bitcast.58), calls=%async_computation.3 | async-start | bytes 1048576
  74.7 0.8 copy-start.18
  74.7 0.8 copy-start.21
  74.8 0.8 copy-start.22
  74.8 10.2 %slice-start = ((s8[4718592]{0:T(1024)(128)(4,1)}), s8[4194304]{0:T(1024)(128)(4,1)S(1)}, s32[]{:S(2)}) async-start(s8[4718592]{0:T(1024)(128)(4,1)} %bitcast.56), calls=%async_computation | async-start | bytes 8388608
  75.6 9.4 %copy-start.16 = (f32[768]{0:T(1024)S(1)}, f32[768]{0:T(1024)}, u32[]{:S(2)}) copy-start(f32[768]{0:T(1024)} %param.32) | copy-start | bytes 9220
  75.6 9.4 %slice-start.1 = ((s8[4718592]{0:T(1024)(128)(4,1)}), s8[524288]{0:T(1024)(128)(4,1)S(1)}, s32[]{:S(2)}) async-start(s8[4718592]{0:T(1024)(128)(4,1)} %bitcast.56), calls=%async_computation.1 | async-start | bytes 1048576
  85.0 5.5 %copy-start.25 = (bf16[1024,3072]{1,0:T(8,128)(2,1)}, bf16[1024,3072]{1,0:T(8,128)(2,1)S(1)}, u32[]{:S(2)}) copy-start(bf16[1024,3072]{1,0:T(8,128)(2,1)S(1)} %get-tuple-element.83) | copy-start | bytes 18874372
  85.0 6.2 %copy-start.1 = (f32[1024,768]{1,0:T(8,128)S(1)}, f32[1024,768]{1,0:T(8,128)}, u32[]{:S(2)}) copy-start(f32[1024,768]{1,0:T(8,128)} %get-tuple-element.30) | copy-start | bytes 9437188
  90.5 0.7 copy-start.15
  90.5 1.4 copy-start
  90.5 1.9 copy-start.2
  90.5 1.9 copy-start.14
  92.4 4.2 %copy-start.17 = (f32[768]{0:T(1024)S(1)}, f32[768]{0:T(1024)}, u32[]{:S(2)}) copy-start(f32[768]{0:T(1024)} %param.34) | copy-start | bytes 9220
  99.4 12.8 %copy-start.5 = (f32[1024,768]{1,0:T(8,128)}, f32[1024,768]{1,0:T(8,128)S(1)}, u32[]{:S(2)}) copy-start(f32[1024,768]{1,0:T(8,128)S(1)} %get-tuple-element.69) | copy-start | bytes 9437188
  112.2 6.1 %copy-start.26 = (bf16[1024,3072]{1,0:T(8,128)(2,1)}, bf16[1024,3072]{1,0:T(8,128)(2,1)S(1)}, u32[]{:S(2)}) copy-start(bf16[1024,3072]{1,0:T(8,128)(2,1)S(1)} %get-tuple-element.88) | copy-start | bytes 18874372
  118.3 2.3 copy-start.20
  120.6 2.6 copy-start.3
  124.5 12.4 %slice-start.4 = ((s8[6291456]{0:T(1024)(128)(4,1)}), s8[4194304]{0:T(1024)(128)(4,1)S(1)}, s32[]{:S(2)}) async-start(s8[6291456]{0:T(1024)(128)(4,1)} %bitcast.60), calls=%async_computation.4 | async-start | bytes 8388608
  125.6 11.3 %copy-start.6 = (f32[1024,768]{1,0:T(8,128)S(1)}, f32[1024,768]{1,0:T(8,128)}, u32[]{:S(2)}) copy-start(f32[1024,768]{1,0:T(8,128)} %copy-done.5) | copy-start | bytes 9437188
  125.6 11.3 %slice-start.5 = ((s8[6291456]{0:T(1024)(128)(4,1)}), s8[2097152]{0:T(1024)(128)(4,1)S(1)}, s32[]{:S(2)}) async-start(s8[6291456]{0:T(1024)(128)(4,1)} %bitcast.60), calls=%async_computation.5 | async-start | bytes 4194304
  308.9 7.0 %copy-start.4 = (bf16[768,3072]{1,0:T(8,128)(2,1)S(1)}, bf16[768,3072]{1,0:T(8,128)(2,1)}, u32[]{:S(2)}) copy-start(bf16[768,3072]{1,0:T(8,128)(2,1)} %get-tuple-element.41) | copy-start | bytes 14155780
  315.8 5.1 %copy-start.7 = (f32[1024,768]{1,0:T(8,128)S(1)}, f32[1024,768]{1,0:T(8,128)}, u32[]{:S(2)}) copy-start(f32[1024,768]{1,0:T(8,128)} %get-tuple-element.37) | copy-start | bytes 9437188
  315.9 5.1 %copy-start.12 = (pred[1024]{0:T(1024)(128)(4,1)S(1)}, pred[1024]{0:T(1024)(128)(4,1)}, u32[]{:S(2)}) copy-start(pred[1024]{0:T(1024)(128)(4,1)} %copy-done.11) | copy-start | bytes 3076
  320.9 2.0 copy-start.9
  322.9 6.1 %copy-start.8 = (f32[576,768]{1,0:T(8,128)S(1)}, f32[576,768]{1,0:T(8,128)}, u32[]{:S(2)}) copy-start(f32[576,768]{1,0:T(8,128)} %get-tuple-element.39) | copy-start | bytes 5308420

commit v3 on v2

--- a/solution.py
+++ b/solution.py
@@ -268,7 +268,9 @@
 
 
 def early_kernel(
-    x_ref,
+    tokens_ref,
+    mask_ref,
+    embed_ref,
     own_ref,
     bias_ref,
     ow_ref,
@@ -279,6 +281,7 @@
     ctx_ref,
     lse_ref,
     out_ref,
+    x_out,
     w_out,
     w_all,
     b_all,
@@ -289,24 +292,34 @@
     step = pl.program_id(0)
     group, row = step // 2, step % 2
     place = Place()
-    features = w_all.shape[2]
-    width = w_all.shape[3]
+    width = w_all.shape[2]
     heads = width // HEAD_DIM
-    half = features // 2
-    rows = pl.ds(pl.multiple_of(place.c * half, half), half)
+    half, quarter = width // 2, width // 4
+
+    def half_of(g):
+        return w_all.at[g, :, pl.ds(pl.multiple_of(place.c * half, half), half), :]
+
+    def quarter_rows(g):
+        side = place.x if g == 1 else place.y
+        return pl.ds(pl.multiple_of(place.c * half + side * quarter, quarter), quarter)
+
+    def quarter_of(g):
+        return w_all.at[g, :, quarter_rows(g), :]
 
     load = pltpu.make_async_copy(own_ref, w_all.at[0], local.at[0])
 
-    def part(g):
-        return w_all.at[g, :, rows, :]
-
     def direct(g):
-        return remote(own_ref.at[:, rows, :], part(g), send.at[0, g], recv.at[0, g], place.up(g))
-
-    relay = remote(part(2), part(3), send.at[0, 3], recv.at[0, 3], place.up(1))
+        src = own_ref.at[:, quarter_rows(g), :]
+        return remote(src, quarter_of(g), send.at[0, g], recv.at[0, g], place.up(g))
+
+    relay = remote(quarter_of(2), quarter_of(3), send.at[0, 3], recv.at[0, 3], place.up(1))
+
+    def beside(g):
+        where = place.side("x" if g == 1 else "y")
+        return remote(quarter_of(g), quarter_of(g), send.at[3, g], recv.at[3, g], where)
 
     def cross(g):
-        return remote(part(g), part(g), send.at[1, g], recv.at[1, g], place.core())
+        return remote(half_of(g), half_of(g), send.at[1, g], recv.at[1, g], place.core())
 
     def bias(g):
         return remote(bias_ref, b_all.at[g], send.at[2, g], recv.at[2, g], place.up(g))
@@ -316,14 +329,16 @@
 
     @pl.when(step == 0)
     def _():
-        greet([place.core()] + [place.up(o) for o in range(1, 4)])
+        greet(
+            [place.core(), place.side("x"), place.side("y")] + [place.up(o) for o in range(1, 4)]
+        )
+        direct(1).start()
+        direct(2).start()
         load.start()
         bias_load = pltpu.make_async_copy(bias_ref, b_all.at[0], local.at[1])
         bias_load.start()
         for g in range(1, 4):
             bias(g).start()
-        direct(1).start()
-        direct(2).start()
         load.wait()
         bias_load.wait()
         store(0).start()
@@ -336,10 +351,16 @@
             bias(g).wait()
             store(g).start()
 
-    x = x_ref[...]
-    q = (dot_nn(x, w_all[group, 0]) + b_all[group, 0:1, :]).astype(BF)
-    k = dot_nn(x, w_all[group, 1]).astype(BF)
-    v = (dot_nn(x, w_all[group, 2]) + b_all[group, 1:2, :]).astype(BF)
+    x = jnp.where(mask_ref[...] == 1.0, embed_ref[...].astype(F32), tokens_ref[...].astype(F32))
+    x = x.astype(BF)
+
+    @pl.when(step < 2)
+    def _():
+        x_out[...] = x
+
+    q = (dot_nt(x, w_all[group, 0]) + b_all[group, 0:1, :]).astype(BF)
+    k = dot_nt(x, w_all[group, 1]).astype(BF)
+    v = (dot_nt(x, w_all[group, 2]) + b_all[group, 1:2, :]).astype(BF)
     q_ref[0] = q
     k_ref[0] = k
     v_ref[0] = v
@@ -371,17 +392,23 @@
     @pl.when(step == 1)
     def _():
         direct(1).wait()
+        beside(1).start()
+        direct(2).wait()
+        relay.start()
+        beside(2).start()
+        beside(1).wait()
         cross(1).start()
 
-    @pl.when(step == 3)
-    def _():
-        direct(2).wait()
-        cross(2).start()
-        relay.start()
-
-    @pl.when(step == 5)
+    @pl.when(step == 2)
     def _():
         relay.wait()
+        beside(3).start()
+        beside(2).wait()
+        cross(2).start()
+
+    @pl.when(step == 4)
+    def _():
+        beside(3).wait()
         cross(3).start()
 
     @pl.when(step == 7)
@@ -390,9 +417,9 @@
             store(g).wait()
 
 
-def early_call(x, own, bias, ow, ob):
+def early_call(x, mask, embed, own, bias, ow, ob):
     tokens, features = x.shape
-    width = own.shape[2]
+    width = own.shape[1]
     groups = features // width
     rows = tokens // LEN
     hbm = pl.BlockSpec(memory_space=pl.ANY)
@@ -404,6 +431,8 @@
         grid=(groups * rows,),
         in_specs=[
             pl.BlockSpec((LEN, features), lambda s: (s % 2, 0)),
+            pl.BlockSpec((LEN, 1), lambda s: (s % 2, 0)),
+            pl.BlockSpec((1, features), lambda s: (0, 0)),
             hbm,
             hbm,
             pl.BlockSpec((groups, width, features), lambda s: (0, 0, 0)),
@@ -416,6 +445,7 @@
             per_head,
             pl.BlockSpec((1, 1, 8, LEN), lambda s: (s // 2, s % 2, 0, 0)),
             pl.BlockSpec((tokens, features), lambda s: (0, 0)),
+            pl.BlockSpec((LEN, features), lambda s: (jnp.minimum(s, 1), 0)),
             hbm,
         ],
         out_shape=[
@@ -425,13 +455,14 @@
             stacked,
             jax.ShapeDtypeStruct((groups, rows, 8, LEN), F32),
             jax.ShapeDtypeStruct((tokens, features), F32),
+            jax.ShapeDtypeStruct((tokens, features), BF),
             jax.ShapeDtypeStruct((groups,) + own.shape, BF),
         ],
         scratch_shapes=[
             pltpu.VMEM((groups,) + own.shape, BF),
             pltpu.VMEM((groups, 8, width), F32),
-            dma((3, 4)),
-            dma((3, 4)),
+            dma((4, 4)),
+            dma((4, 4)),
             dma((6,)),
         ],
         compiler_params=pltpu.CompilerParams(
@@ -441,13 +472,17 @@
             has_side_effects=True,
         ),
         name="early_kernel",
-    )(x, own, bias, ow, ob)
+    )(x, mask, embed, own, bias, ow, ob)
 
 
 LANES = 384
-CHUNK = 512
-TICKS = 3
-SPACING = 2
+CHUNK = 1024
+PIECE = CHUNK // 64
+SPACING = 3
+DOWN_EVERY = 1
+UP_EVERY = 4
+UP_FIRST = 6
+BLOCK = 256
 
 
 def add_into(target, source):
@@ -455,7 +490,7 @@
 
 
 class MatrixSum:
-    COPIES = 17
+    COPIES = 16
 
     def __init__(self, place, parts, keep, first, second, third, fourth, full, send, recv, local):
         self.place = place
@@ -467,90 +502,64 @@
     def copy(self, i, slot, src, dst, where):
         return remote(src, dst, self.send.at[i, slot], self.recv.at[i, slot], where)
 
-    def fetches(self, i, source, index):
-        p = self.place
-        out = []
-        for zl in range(2):
-            lanes = pl.ds(zl * LANES, LANES)
-            out.append(
-                pltpu.make_async_copy(
-                    source.at[index, p.c, :, :, :, :, :, lanes],
-                    self.keep.at[i, :, :, :, :, zl],
-                    self.local.at[i, zl],
-                )
-            )
-        return out
+    def fetch(self, i, source, index):
+        return pltpu.make_async_copy(
+            source.at[index, self.place.c], self.keep.at[i], self.local.at[i]
+        )
 
     def copies(self, phase, i, source=None, index=None):
         p = self.place
         keep, full = self.keep, self.full
+        both = self.parts == 2
+        out = []
         if phase == 1:
-            return [
-                self.copy(
-                    i,
-                    zl,
-                    source.at[index, 1 - p.c, :, :, :, :, :, pl.ds(zl * LANES, LANES)],
-                    self.first.at[i, :, :, :, :, zl],
-                    p.core(),
-                )
-                for zl in range(2)
-            ]
+            out.append(self.copy(i, 0, source.at[index, 1 - p.c], self.first.at[i], p.core()))
         if phase == 2:
-            out = [
-                self.copy(i, 2, keep.at[i, 0, 1 - p.x], self.second.at[i, 0], p.side("x")),
-                self.copy(i, 3, keep.at[i, 1, :, 1 - p.y], self.second.at[i, 1], p.side("y"))
-                if self.parts == 2
-                else None,
-            ]
+            src = keep.at[i, 0, 1 - p.x]
+            out.append(self.copy(i, 1, src, self.second.at[i, 0], p.side("x")))
+            if both:
+                src = keep.at[i, 1, :, 1 - p.y]
+                out.append(self.copy(i, 2, src, self.second.at[i, 1], p.side("y")))
         if phase == 3:
-            out = [
-                self.copy(i, 4, keep.at[i, 0, p.x, 1 - p.y], self.third.at[i, 0], p.side("y")),
-                self.copy(i, 5, keep.at[i, 1, 1 - p.x, p.y], self.third.at[i, 1], p.side("x"))
-                if self.parts == 2
-                else None,
-            ]
+            src = keep.at[i, 0, p.x, 1 - p.y]
+            out.append(self.copy(i, 3, src, self.third.at[i, 0], p.side("y")))
+            if both:
+                src = keep.at[i, 1, 1 - p.x, p.y]
+                out.append(self.copy(i, 4, src, self.third.at[i, 1], p.side("x")))
         if phase == 4:
-            out = []
             for o in range(1, 4):
-                t = p.h ^ o
-                out.append(
-                    self.copy(
-                        i,
-                        5 + o,
-                        keep.at[i, :, p.x, p.y, t >> 1, t & 1],
-                        self.fourth.at[i, o - 1],
-                        p.up(o),
-                    )
-                )
+                src = keep.at[i, :, p.x, p.y, p.h ^ o]
+                out.append(self.copy(i, 4 + o, src, self.fourth.at[i, o - 1], p.up(o)))
         if phase == 5:
-            spot = full.at[i, p.c, :, p.x, p.y, p.h >> 1, p.h & 1]
-            out = [self.copy(i, 8 + o, spot, spot, p.up(o)) for o in range(1, 4)]
+            spot = full.at[i, p.c, :, p.x, p.y, p.h]
+            for o in range(1, 4):
+                out.append(self.copy(i, 7 + o, spot, spot, p.up(o)))
         if phase == 6:
             spot = full.at[i, p.c, 0, p.x, p.y]
-            out = [self.copy(i, 12, spot, spot, p.side("y"))]
-            if self.parts == 2:
+            out.append(self.copy(i, 11, spot, spot, p.side("y")))
+            if both:
                 spot = full.at[i, p.c, 1, p.x, p.y]
-                out.append(self.copy(i, 13, spot, spot, p.side("x")))
+                out.append(self.copy(i, 12, spot, spot, p.side("x")))
         if phase == 7:
             spot = full.at[i, p.c, 0, p.x]
-            out = [self.copy(i, 14, spot, spot, p.side("x"))]
-            if self.parts == 2:
+            out.append(self.copy(i, 13, spot, spot, p.side("x")))
+            if both:
                 spot = full.at[i, p.c, 1, :, p.y]
-                out.append(self.copy(i, 15, spot, spot, p.side("y")))
+                out.append(self.copy(i, 14, spot, spot, p.side("y")))
         if phase == 8:
             spot = full.at[i, p.c]
-            out = [self.copy(i, 16, spot, spot, p.core())]
-        return [one for one in out if one is not None]
+            out.append(self.copy(i, 15, spot, spot, p.core()))
+        return out
 
     def begin(self, i, source, index):
-        for one in self.fetches(i, source, index) + self.copies(1, i, source, index):
+        self.fetch(i, source, index).start()
+        for one in self.copies(1, i, source, index):
             one.start()
 
     def advance(self, phase, i, source=None, index=None):
         p = self.place
         if phase == 2:
-            for one in self.fetches(i, source, index):
-                one.wait()
+            self.fetch(i, source, index).wait()
         for one in self.copies(phase - 1, i, source, index):
             one.wait()
         if phase == 2:
@@ -563,16 +572,18 @@
             for part in range(self.parts):
                 add_into(self.keep.at[i, part, p.x, p.y], self.third.at[i, part])
         if phase == 5:
-            total = self.keep[i, :, p.x, p.y, p.h >> 1, p.h & 1].astype(F32)
+            total = self.keep[i, :, p.x, p.y, p.h].astype(F32)
             for o in range(3):
                 total = total + self.fourth[i, o].astype(F32)
-            self.full[i, p.c, :, p.x, p.y, p.h >> 1, p.h & 1] = total.astype(BF)
+            self.full[i, p.c, :, p.x, p.y, p.h] = total.astype(BF)
         if phase <= 8:
             for one in self.copies(phase, i):
                 one.start()
 
 
 class GroupSum:
+    COPIES = 11
+
     def __init__(self, place, own, first, second, third, fourth, full, send, recv):
         self.place = place
         self.own, self.first, self.second = own, first, second
@@ -584,29 +595,32 @@
 
     def copies(self, phase, g):
         p, own, full = self.place, self.own, self.full
+        x, y = p.side("x"), p.side("y")
         if phase == 1:
             return [self.copy(g, 0, own.at[g, 1 - p.c], self.first.at[g], p.core())]
-        even = g % 2 == 0
         if phase == 2:
-            src = own.at[g, p.c, 1 - p.x] if even else own.at[g, p.c, :, 1 - p.y]
-            return [self.copy(g, 1, src, self.second.at[g], p.side("x" if even else "y"))]
+            return [
+                self.copy(g, 1, own.at[g, p.c, 0, 1 - p.x], self.second.at[g, 0], x),
+                self.copy(g, 2, own.at[g, p.c, 1, :, 1 - p.y], self.second.at[g, 1], y),
+            ]
         if phase == 3:
-            src = own.at[g, p.c, p.x, 1 - p.y] if even else own.at[g, p.c, 1 - p.x, p.y]
-            return [self.copy(g, 2, src, self.third.at[g], p.side("y" if even else "x"))]
-        if phase == 4:
-            if g == 0:
-                return []
-            src = own.at[g, p.c, p.x, p.y]
-            return [self.copy(g, 3, src, self.fourth.at[g - 1], p.up(g))]
+            return [
+                self.copy(g, 3, own.at[g, p.c, 0, p.x, 1 - p.y], self.third.at[g, 0], y),
+                self.copy(g, 4, own.at[g, p.c, 1, 1 - p.x, p.y], self.third.at[g, 1], x),
+            ]
+        if phase == 4 and g > 0:
+            return [
+                self.copy(g, 5, own.at[g, p.c, :, p.x, p.y], self.fourth.at[g - 1], p.up(g))
+            ]
         if phase == 6:
-            spot = full.at[p.c, p.x, p.y]
-            return [self.copy(0, 4, spot, spot, p.side("y"))]
+            spots = full.at[p.c, 0, p.x, p.y], full.at[p.c, 1, p.x, p.y]
+            return [self.copy(0, 6, spots[0], spots[0], y), self.copy(0, 7, spots[1], spots[1], x)]
         if phase == 7:
-            spot = full.at[p.c, p.x]
-            return [self.copy(0, 5, spot, spot, p.side("x"))]
+            spots = full.at[p.c, 0, p.x], full.at[p.c, 1, :, p.y]
+            return [self.copy(0, 8, spots[0], spots[0], x), self.copy(0, 9, spots[1], spots[1], y)]
         if phase == 8:
             spot = full.at[p.c]
-            return [self.copy(0, 6, spot, spot, p.core())]
+            return [self.copy(0, 10, spot, spot, p.core())]
         return []
 
     def begin(self, g):
@@ -619,56 +633,78 @@
             for group in range(own.shape[0]):
                 for one in self.copies(4, group):
                     one.wait()
-            total = own[0, p.c, p.x, p.y].astype(F32)
+            total = own[0, p.c, :, p.x, p.y].astype(F32)
             for o in range(3):
                 total = total + self.fourth[o].astype(F32)
-            self.full[p.c, p.x, p.y] = total.astype(BF)
+            self.full[p.c, :, p.x, p.y] = total.astype(BF)
         else:
             for one in self.copies(phase - 1, g):
                 one.wait()
         if phase == 2:
             add_into(own.at[g, p.c], self.first.at[g])
         if phase == 3:
-            if g % 2 == 0:
-                add_into(own.at[g, p.c, p.x], self.second.at[g])
-            else:
-                add_into(own.at[g, p.c, :, p.y], self.second.at[g])
+            add_into(own.at[g, p.c, 0, p.x], self.second.at[g, 0])
+            add_into(own.at[g, p.c, 1, :, p.y], self.second.at[g, 1])
         if phase == 4:
-            add_into(own.at[g, p.c, p.x, p.y], self.third.at[g])
+            add_into(own.at[g, p.c, 0, p.x, p.y], self.third.at[g, 0])
+            add_into(own.at[g, p.c, 1, p.x, p.y], self.third.at[g, 1])
         for one in self.copies(phase, g):
             one.start()
 
 
+class Stages:
+    def __init__(self, tokens, ff, count, heads):
+        rows = tokens // LEN
+        self.blocks = ff // BLOCK
+        self.norms = self.blocks + tokens // BLOCK
+        self.outer = self.norms + count
+        self.per_group = 2 * rows
+        self.end = self.outer + count * self.per_group
+        self.half = ff // CHUNK
+        self.outw_first = self.outer + 1
+
+
 def late_kernel(
-    chunks,
-    x_ref,
+    plan,
+    gf_ref,
+    nl_hbm,
+    slope_ref,
+    dw_ref,
+    uw_ref,
+    xh_ref,
+    inv_ref,
+    gs_ref,
+    gain_ref,
+    x_hbm,
     w_ref,
     ow_ref,
+    ctx_ref,
     q_ref,
     k_ref,
     v_ref,
     lse_ref,
-    ga_ref,
-    gf_ref,
     mask_ref,
     early_0,
     early_1,
     early_2,
-    early_3,
-    early_4,
-    early_5,
-    early_up,
     early_squares,
     down_ref,
-    up_ref,
-    outw_ref,
-    dx_ref,
-    wg_ref,
     vec_ref,
+    dx_out,
+    wg_out,
     down_out,
     up_out,
     outw_out,
+    up_ref,
+    outw_ref,
+    dx,
+    rows_ref,
+    ga_all,
+    dpre,
+    stage_w,
+    stage_o,
     wg_acc,
+    dctx,
     k_t,
     dq_t,
     dk_acc,
@@ -705,12 +741,18 @@
     vec_send,
     vec_recv,
     store_sem,
+    block_sem,
+    outer_sem,
+    last_sem,
+    rows_sem,
 ):
     step = pl.program_id(0)
-    group, row = step // 2, step % 2
     place = Place()
-    half = chunks // 2
+    half = plan.half
+    chunks = 2 * half
     count = qk_own.shape[0]
+    width = q_ref.shape[2]
+    heads = width // HEAD_DIM
     feed = MatrixSum(
         place, 2, ff_keep, ff_1, ff_2, ff_3, ff_4, ff_full, ff_send, ff_recv, ff_local
     )
@@ -718,175 +760,278 @@
         place, 1, ow_keep, ow_1, ow_2, ow_3, ow_4, ow_full, ow_send, ow_recv, ow_local
     )
     groups = GroupSum(place, qk_own, qk_1, qk_2, qk_3, qk_4, qk_full, qk_send, qk_recv)
-    tail = 2 * count * TICKS
+    tail = plan.end
+    end = max(
+        tail + 8,
+        plan.outw_first + 8 * SPACING + 1,
+        UP_FIRST + UP_EVERY * (half - 1) + 8 * SPACING + 1,
+    )
+
+    nl_load = pltpu.make_async_copy(nl_hbm, rows_ref, rows_sem.at[0])
+    x_load = pltpu.make_async_copy(x_hbm, rows_ref, rows_sem.at[1])
 
     @pl.when(step == 0)
     def _():
+        nl_load.start()
         greet(
             [place.core(), place.side("x"), place.side("y")] + [place.up(o) for o in range(1, 4)]
         )
+        nl_load.wait()
         vec[...] = jnp.zeros_like(vec)
-        for index, ref in enumerate((early_0, early_1, early_2, early_3, early_4, early_5)):
+        for index, ref in enumerate((early_0, early_1, early_2)):
             vec[0, index : index + 1, :] = ref[...]
-        vec[0, 6:10, :] = early_up[...]
         vec[0, 10:11, :] = early_squares[...]
 
-    def lanes(zl):
-        return pl.ds(zl * LANES, LANES)
-
     def down_store(i):
-        return [
-            pltpu.make_async_copy(
-                ff_full.at[i, :, :, :, :, :, zl],
-                down_out.at[i, :, :, :, :, :, :, lanes(zl)],
-                store_sem.at[i, zl],
+        return pltpu.make_async_copy(ff_full.at[i], down_out.at[i], store_sem.at[i, 0])
+
+    def up_store(i, part):
+        spot = pl.ds(pl.multiple_of((2 * i + part) * (CHUNK // 2), CHUNK // 2), CHUNK // 2)
+        return pltpu.make_async_copy(stage_up, up_out.at[:, spot], store_sem.at[half + i, part])
+
+    def outw_store():
+        return pltpu.make_async_copy(ow_full.at[0], outw_out.at[0], store_sem.at[chunks, 0])
+
+    def tick(t, start, stop):
+        span = 8 * SPACING
+
+        def window(first, last, run):
+            if start <= last and stop > first:
+
+                @pl.when((t >= first) & (t <= last))
+                def _():
+                    run()
+
+        def each(first, every, number, run):
+            for phase in range(9, 0, -1):
+                behind = SPACING * (phase - 1)
+                if stop - behind <= first or start - behind > first + every * (number - 1):
+                    continue
+                at = t - behind - first
+                index = at // every
+
+                @pl.when((at >= 0) & (index < number) & (at % every == 0))
+                def _():
+                    run(phase, index)
+
+        def down_step(phase, i):
+            if phase == 1:
+                feed.begin(i, down_ref, i)
+                return
+            feed.advance(phase, i, down_ref, i)
+            if phase == 9:
+                down_store(i).start()
+
+        def up_step(phase, i):
+            if phase == 1:
+                feed.begin(half + i, up_ref, i)
+                return
+            feed.advance(phase, half + i, up_ref, i)
+            if phase == 9:
+
+                @pl.when(i > 0)
+                def _():
+                    up_store(i - 1, 1).wait()
+
+                for c in range(2):
+                    if c == 1:
+                        up_store(i, 0).wait()
+                    block = ff_full[half + i, c].reshape(CHUNK // 2, 2 * LANES)
+                    stage_up[...] = block.T
+                    up_store(i, c).start()
+
+        def outw_step(phase, i):
+            if phase == 1:
+                outer.begin(0, outw_ref, 0)
+                return
+            outer.advance(phase, 0, outw_ref, 0)
+            if phase == 9:
+                outw_store().start()
+
+        def group_steps():
+            for g in range(count):
+                base = plan.outer + plan.per_group * (g + 1)
+                if base < start or base >= stop:
+                    continue
+                phases = (9, 8, 7, 6, 4, 3, 2) if g == count - 1 else (4, 3, 2)
+                for phase in phases:
+                    when = phase - 1 if phase < 5 else phase - 2
+
+                    @pl.when(t == base + when)
+                    def _():
+                        groups.advance(phase, g)
+
+                @pl.when(t == base)
+                def _():
+                    groups.begin(g)
+
+        first, last = 0, DOWN_EVERY * (half - 1) + span
+        window(first, last, lambda: each(0, DOWN_EVERY, half, down_step))
+        first, last = UP_FIRST, UP_FIRST + UP_EVERY * (half - 1) + span
+        window(first, last, lambda: each(UP_FIRST, UP_EVERY, half, up_step))
+        first, last = plan.outw_first, plan.outw_first + span
+        window(first, last, lambda: each(plan.outw_first, 1, 1, outw_step))
+        window(plan.outer + plan.per_group, tail + 8, group_steps)
+
+    tick(step, 0, tail)
+
+
+    def block_copy(b):
+        per_chunk = CHUNK // BLOCK
+        spot = up_ref.at[b // per_chunk, (b % per_chunk) // 2, b % 2]
+        return pltpu.make_async_copy(stage_w.at[b % 2], spot, block_sem.at[b])
+
+    @pl.when(step < plan.blocks)
+    def _():
+        grad = dot_nt(gf_ref[...], dw_ref[...]) * slope_ref[...]
+        dpre[...] = grad.astype(BF)
+
+        @pl.when(step > 1)
+        def _():
+            block_copy(step - 2).wait()
+
+        part = dot_tn(dpre[...], rows_ref[...]).astype(BF)
+        stage_w[step % 2] = part.reshape(stage_w.shape[1:])
+        block_copy(step).start()
+        per_row = rows_ref.shape[1] // BLOCK
+        spot = pl.ds(pl.multiple_of((step % per_row) * BLOCK, BLOCK), BLOCK)
+        vec[0, pl.ds(6 + step // per_row, 1), spot] = jnp.sum(
+            dpre[...].astype(F32), axis=0, keepdims=True
+        )
+        for r in range(0, dx.shape[0], BLOCK):
+            part = dot_nt(dpre[r : r + BLOCK], uw_ref[...])
+
+            @pl.when(step == 0)
+            def _():
+                dx[r : r + BLOCK] = part
+
+            @pl.when(step > 0)
+            def _():
+                dx[r : r + BLOCK] = dx[r : r + BLOCK] + part
+
+
+    @pl.when((step >= plan.blocks) & (step < plan.norms))
+    def _():
+        @pl.when(step == plan.blocks)
+        def _():
+            block_copy(plan.blocks - 2).wait()
+            block_copy(plan.blocks - 1).wait()
+            x_load.start()
+
+        rows = pl.ds(pl.multiple_of((step - plan.blocks) * BLOCK, BLOCK), BLOCK)
+        upstream = dx[rows, :] + gs_ref[...]
+        normal = xh_ref[...]
+        scaled = upstream * gain_ref[...]
+        mean = jnp.mean(scaled, axis=1, keepdims=True)
+        along = jnp.mean(scaled * normal, axis=1, keepdims=True)
+        hidden = inv_ref[...] * (scaled - mean - normal * along)
+        low = hidden.astype(BF)
+        dx[rows, :] = hidden
+        ga_all[rows, :] = low
+        vec[0, 3:4, :] += jnp.sum(upstream * normal, axis=0, keepdims=True)
+        vec[0, 4:5, :] += jnp.sum(upstream, axis=0, keepdims=True)
+        vec[0, 5:6, :] += jnp.sum(low.astype(F32), axis=0, keepdims=True)
+
+
+    def outer_copy(g):
+        spot = place.h ^ g
+        return pltpu.make_async_copy(
+            stage_o, outw_ref.at[0, spot >> 1, 0, spot & 1], outer_sem.at[g]
+        )
+
+    @pl.when((step >= plan.norms) & (step < plan.outer))
+    def _():
+        g = step - plan.norms
+
+        @pl.when(g > 0)
+        def _():
+            outer_copy(g - 1).wait()
+
+        part = dot_tn(ctx_ref[0], ga_all[...])
+        stage_o[...] = part.astype(BF).reshape(stage_o.shape)
+        outer_copy(g).start()
+
+    @pl.when(step == plan.outer)
+    def _():
+        outer_copy(count - 1).wait()
+        x_load.wait()
+
+
+    def dx_copy(r):
+        spot = pl.ds(pl.multiple_of(r * LEN, LEN), LEN)
+        return pltpu.make_async_copy(dx.at[spot], dx_out.at[spot], last_sem.at[r])
+
+    @pl.when(step >= plan.outer)
+    def _():
+        at = step - plan.outer
+        part = at % 2
+        row = (at // 2) % 2
+        group = at // plan.per_group
+        mine = pl.ds(pl.multiple_of(row * LEN, LEN), LEN)
+        q = q_ref[0]
+        k = k_ref[0]
+        v = v_ref[0]
+
+        @pl.when(part == 0)
+        def _():
+            dctx[...] = dot_nt(ga_all[mine, :], ow_ref[place.h ^ group]).astype(BF)
+            k_t[...] = k.T
+
+        q_scaled = q * jnp.asarray(0.125, BF)
+
+        def one_head(head, carry):
+            mask = head_lanes(width, head)
+            spot = pl.ds(pl.multiple_of(head * HEAD_DIM, HEAD_DIM), HEAD_DIM)
+            scores = dot_nt(jnp.where(mask, k, jnp.zeros_like(k)), q_scaled)
+            probs = jnp.exp(scores - lse_ref[0, 0, pl.ds(head, 1), :])
+            dprobs = dot_nt(jnp.where(mask, v, jnp.zeros_like(v)), dctx[...])
+            delta = jnp.sum(probs * dprobs, axis=0, keepdims=True)
+            dscores = (probs * (dprobs - delta)).astype(BF)
+            dv_acc[...] = jnp.where(mask, dot_nn(probs.astype(BF), dctx[...]), dv_acc[...])
+            dk_acc[...] = jnp.where(mask, dot_nn(dscores, q_scaled), dk_acc[...])
+            dq_t[spot, :] = dot_nn(k_t[spot, :], dscores)
+            return carry
+
+        split = heads // 2 + 1
+        lax.fori_loop(part * split, split + part * (heads - split), one_head, 0)
+
+        @pl.when(part == 1)
+        def _():
+            x = rows_ref[mine, :]
+            dq = (dq_t[...] * 0.125).T.astype(BF)
+            dk = dk_acc[...].astype(BF)
+            dv = dv_acc[...].astype(BF)
+            delta = dot_nn(dq, w_ref[0, 0]) + dot_nn(dk, w_ref[0, 1]) + dot_nn(dv, w_ref[0, 2])
+            dx[mine, :] = dx[mine, :] + delta
+
+            @pl.when(row == 0)
+            def _():
+                wg_acc[...] = jnp.zeros_like(wg_acc)
+
+            for index, grad in enumerate((dq, dk, dv)):
+                wg_acc[index * width : (index + 1) * width] += dot_tn(grad, x)
+            spot = place.h ^ group
+            vec[0, pl.ds(16 + spot, 1), 0:width] += jnp.sum(
+                dq.astype(F32), axis=0, keepdims=True
             )
-            for zl in range(2)
-        ]
-
-    def up_store(i):
-        spot = pl.ds(pl.multiple_of(i * CHUNK, CHUNK), CHUNK)
-        return pltpu.make_async_copy(
-            stage_up.at[i % 2], up_out.at[:, spot], store_sem.at[half + i, 0]
-        )
-
-    def outw_store():
-        return [
-            pltpu.make_async_copy(
-                ow_full.at[0, :, :, :, :, :, zl],
-                outw_out.at[0, :, :, :, :, :, :, lanes(zl)],
-                store_sem.at[chunks, zl],
+            vec[0, pl.ds(20 + spot, 1), 0:width] += jnp.sum(
+                dv.astype(F32), axis=0, keepdims=True
             )
-            for zl in range(2)
-        ]
-
-    def tick(t, start, stop):
-        for phase in range(9, 1, -1):
-            behind = SPACING * (phase - 1)
-            if stop - behind <= 0 or start - behind > chunks:
-                continue
-            i = t - behind
-
-            @pl.when((i >= 0) & (i < half))
+
+            @pl.when(row == 1)
             def _():
-                feed.advance(phase, i, down_ref, i)
-                if phase == 9:
-                    for one in down_store(i):
-                        one.start()
-
-            @pl.when((i >= half) & (i < chunks))
+                shape = qk_own.shape[2:]
+                for zl in range(2):
+                    block = wg_acc[:, zl * LANES : (zl + 1) * LANES].astype(BF)
+                    qk_own[group, zl] = block.reshape(shape)
+
+            @pl.when(group == count - 1)
             def _():
-                feed.advance(phase, i, up_ref, i - half)
-                if phase == 9:
-
-                    @pl.when(i > half + 1)
-                    def _():
-                        up_store(i - half - 2).wait()
-
-                    for zl in range(2):
-                        block = ff_full[i, :, :, :, :, :, zl].reshape(CHUNK, LANES)
-                        stage_up[(i - half) % 2, zl * LANES : (zl + 1) * LANES, :] = block.T
-                    up_store(i - half).start()
-
-            @pl.when(i == chunks)
-            def _():
-                outer.advance(phase, 0, outw_ref, 0)
-                if phase == 9:
-                    for one in outw_store():
-                        one.start()
-
-        if start <= chunks:
-
-            @pl.when(t < half)
-            def _():
-                feed.begin(t, down_ref, t)
-
-            @pl.when((t >= half) & (t < chunks))
-            def _():
-                feed.begin(t, up_ref, t - half)
-
-            @pl.when(t == chunks)
-            def _():
-                outer.begin(0, outw_ref, 0)
-
-        for g in range(count):
-            base = 2 * TICKS * (g + 1)
-            if base < start or base >= stop:
-                continue
-            phases = (9, 8, 7, 6, 4, 3, 2) if g == count - 1 else (4, 3, 2)
-            for phase in phases:
-                when = phase - 1 if phase < 5 else phase - 2
-
-                @pl.when(t == base + when)
-                def _():
-                    groups.advance(phase, g)
-
-            @pl.when(t == base)
-            def _():
-                groups.begin(g)
-
-    width = q_ref.shape[2]
-    heads = width // HEAD_DIM
-    x = x_ref[...]
-    ga = ga_ref[...]
-    dctx = dot_nt(ga, ow_ref[place.h ^ group]).astype(BF)
-    q = q_ref[0]
-    k = k_ref[0]
-    v = v_ref[0]
-    k_t[...] = k.T
-    q_scaled = q * jnp.asarray(0.125, BF)
-
-    @pl.loop(0, heads)
-    def _(head):
-        tick(step * TICKS + head, 0, tail)
-        mask = head_lanes(width, head)
-        spot = pl.ds(pl.multiple_of(head * HEAD_DIM, HEAD_DIM), HEAD_DIM)
-        scores = dot_nt(jnp.where(mask, k, jnp.zeros_like(k)), q_scaled)
-        probs = jnp.exp(scores - lse_ref[0, 0, pl.ds(head, 1), :])
-        dprobs = dot_nt(jnp.where(mask, v, jnp.zeros_like(v)), dctx)
-        delta = jnp.sum(probs * dprobs, axis=0, keepdims=True)
-        dscores = (probs * (dprobs - delta)).astype(BF)
-        dv_acc[...] = jnp.where(mask, dot_nn(probs.astype(BF), dctx), dv_acc[...])
-        dk_acc[...] = jnp.where(mask, dot_nn(dscores, q_scaled), dk_acc[...])
-        dq_t[spot, :] = dot_nn(k_t[spot, :], dscores)
-
-    dq = (dq_t[...] * 0.125).T.astype(BF)
-    dk = dk_acc[...].astype(BF)
-    dv = dv_acc[...].astype(BF)
-    part = dot_nt(dq, w_ref[0, 0]) + dot_nt(dk, w_ref[0, 1]) + dot_nt(dv, w_ref[0, 2])
-    mine = pl.ds(pl.multiple_of(row * LEN, LEN), LEN)
-
-    @pl.when(group == 0)
-    def _():
-        dx_ref[mine, :] = gf_ref[...] + part
-
-    @pl.when(group > 0)
-    def _():
-        dx_ref[mine, :] = dx_ref[mine, :] + part
-
-    @pl.when(row == 0)
-    def _():
-        wg_acc[...] = jnp.zeros_like(wg_acc)
-
-    for index, grad in enumerate((dq, dk, dv)):
-        wg_acc[index * width : (index + 1) * width] += dot_tn(grad, x)
-    spot = place.h ^ group
-    vec[0, pl.ds(16 + spot, 1), 0:width] += jnp.sum(dq.astype(F32), axis=0, keepdims=True)
-    vec[0, pl.ds(20 + spot, 1), 0:width] += jnp.sum(dv.astype(F32), axis=0, keepdims=True)
-
-    @pl.when(row == 1)
-    def _():
-        shape = qk_own.shape[2:]
-        for zl in range(2):
-            block = wg_acc[:, zl * LANES : (zl + 1) * LANES].astype(BF)
-            qk_own[group, zl] = block.reshape(shape)
-
-    @pl.when(group == count - 1)
-    def _():
-        total = jnp.where(mask_ref[...] == 1.0, dx_ref[mine, :], 0.0)
-        vec[0, 15:16, :] += jnp.sum(total, axis=0, keepdims=True)
-
-    @pl.when(step == 2 * count - 1)
+                total = jnp.where(mask_ref[...] == 1.0, dx[mine, :], 0.0)
+                vec[0, 15:16, :] += jnp.sum(total, axis=0, keepdims=True)
+                dx_copy(row).start()
+
+    @pl.when(step == plan.end - 1)
     def _():
         def vec_copy(k):
             if k < 3:
@@ -895,9 +1040,9 @@
                 where = (place.dp, place.h ^ (1 << (k - 3)))
             return remote(vec.at[k], vec_in.at[k], vec_send.at[k], vec_recv.at[k], where)
 
-        @pl.loop(tail, tail + 8)
+        @pl.loop(tail, end)
         def _(t):
-            tick(t, tail, tail + 8)
+            tick(t, tail, end)
             for k in range(6):
 
                 @pl.when(t == tail + k)
@@ -910,111 +1055,149 @@
 
         vec_ref[...] = vec[5]
         for c in range(2):
-            block = qk_full[c].reshape(wg_ref.shape[0], LANES)
-            wg_ref[:, c * LANES : (c + 1) * LANES] = block.astype(F32)
+            block = qk_full[c].reshape(wg_acc.shape[0], LANES)
+            wg_acc[:, c * LANES : (c + 1) * LANES] = block.astype(F32)
+        wg_copy = pltpu.make_async_copy(wg_acc, wg_out, last_sem.at[2])
+        wg_copy.start()
         for i in range(half):
-            for one in down_store(i):
-                one.wait()
-        for i in (half - 2, half - 1):
-            up_store(i).wait()
-        for one in outw_store():
-            one.wait()
-
-
-def late_call(x, w, ow, q, k, v, lse, ga, gf, mask, early, down, up, outw):
+            down_store(i).wait()
+        up_store(half - 1, 1).wait()
+        outw_store().wait()
+        for r in range(2):
+            dx_copy(r).wait()
+        wg_copy.wait()
+
+
+def late_call(
+    gf, nl, slope, dw, uw, xh, inv, gs, gain, x, w, ow, ctx, q, k, v, lse, mask, early, down
+):
     tokens, features = x.shape
-    count, _, _, width = w.shape
+    count, _, width, _ = w.shape
     ff = down.shape[0]
-    chunks = 2 * ff // CHUNK
-    chunked = (ff // CHUNK, 2, 2, 2, 2, 2, 16, features)
-    squared = (1, 2, 1, 2, 2, 2, features // 16, features)
+    heads = width // HEAD_DIM
+    plan = Stages(tokens, ff, count, heads)
+    chunks = 2 * plan.half
+    chunked = (plan.half, 2, 2, 2, 2, 4, PIECE, features)
+    squared = (1, 2, 1, 2, 2, 4, features // 32, features)
     hbm = pl.BlockSpec(memory_space=pl.ANY)
+    once = pl.Buffered(1)
 
     def whole(shape):
-        return pl.BlockSpec(shape, lambda s: (0,) * len(shape))
-
-    per_head = pl.BlockSpec((1, LEN, width), lambda s: (s // 2, s % 2, 0))
-    per_row = pl.BlockSpec((LEN, features), lambda s: (s % 2, 0))
+        return pl.BlockSpec(shape, lambda s: (0,) * len(shape), pipeline_mode=once)
+
+    def block_at(s):
+        return jnp.minimum(s, plan.blocks - 1)
+
+    def norm_at(s):
+        return jnp.clip(s - plan.blocks, 0, tokens // BLOCK - 1)
+
+    def head_at(s):
+        at = jnp.clip(s - plan.outer, 0, plan.end - plan.outer - 1)
+        return at // plan.per_group, (at // 2) % 2
+
+    def per_head(s):
+        group, row = head_at(s)
+        return group, row, 0
+
     in_specs = [
-        per_row,
-        pl.BlockSpec((1, 3, features, width), lambda s: (s // 2, 0, 0, 0)),
+        whole(gf.shape),
+        hbm,
+        pl.BlockSpec((tokens, BLOCK), lambda s: (0, block_at(s))),
+        pl.BlockSpec((BLOCK, features), lambda s: (block_at(s), 0)),
+        pl.BlockSpec((features, BLOCK), lambda s: (0, block_at(s))),
+        pl.BlockSpec((BLOCK, features), lambda s: (norm_at(s), 0)),
+        pl.BlockSpec((BLOCK, 1), lambda s: (norm_at(s), 0), pipeline_mode=once),
+        pl.BlockSpec((BLOCK, features), lambda s: (norm_at(s), 0)),
+        whole(gain.shape),
+        hbm,
+        pl.BlockSpec((1, 3, width, features), lambda s: (head_at(s)[0], 0, 0, 0)),
         whole(ow.shape),
-        per_head,
-        per_head,
-        per_head,
-        pl.BlockSpec((1, 1, 8, LEN), lambda s: (s // 2, s % 2, 0, 0)),
-        per_row,
-        pl.BlockSpec((LEN, features), lambda s: (jnp.minimum(s, 1), 0)),
-        pl.BlockSpec((LEN, 1), lambda s: (s % 2, 0)),
+        pl.BlockSpec(
+            (1, tokens, width),
+            lambda s: (jnp.clip(s - plan.norms, 0, count - 1), 0, 0),
+            pipeline_mode=once,
+        ),
+        pl.BlockSpec((1, LEN, width), per_head),
+        pl.BlockSpec((1, LEN, width), per_head),
+        pl.BlockSpec((1, LEN, width), per_head),
+        pl.BlockSpec((1, 1, 8, LEN), lambda s: head_at(s) + (0, 0)),
+        pl.BlockSpec((LEN, 1), lambda s: (head_at(s)[1], 0)),
     ]
     in_specs += [whole(one.shape) for one in early]
-    in_specs += [hbm, hbm, hbm]
-    out_specs = [
-        whole((tokens, features)),
-        whole((3 * width, features)),
-        whole((24, features)),
-        hbm,
-        hbm,
-        hbm,
-    ]
+    in_specs += [hbm]
+    out_specs = [pl.BlockSpec((24, features), lambda s: (0, 0))] + [hbm] * 7
     out_shape = [
+        jax.ShapeDtypeStruct((24, features), F32),
         jax.ShapeDtypeStruct((tokens, features), F32),
         jax.ShapeDtypeStruct((3 * width, features), F32),
-        jax.ShapeDtypeStruct((24, features), F32),
         jax.ShapeDtypeStruct(chunked, BF),
         jax.ShapeDtypeStruct((features, ff), BF),
         jax.ShapeDtypeStruct(squared, BF),
+        jax.ShapeDtypeStruct(chunked, BF),
+        jax.ShapeDtypeStruct(squared, BF),
     ]
 
     def sum_buffers(n, parts, rows):
-        block = (rows, LANES)
+        block = (rows, features)
         return [
-            pltpu.VMEM((n, parts, 2, 2, 2, 2) + block, BF),
-            pltpu.VMEM((n, parts, 2, 2, 2, 2) + block, BF),
-            pltpu.VMEM((n, parts, 2, 2, 2) + block, BF),
-            pltpu.VMEM((n, parts, 2, 2) + block, BF),
+            pltpu.VMEM((n, parts, 2, 2, 4) + block, BF),
+            pltpu.VMEM((n, parts, 2, 2, 4) + block, BF),
+            pltpu.VMEM((n, parts, 2, 4) + block, BF),
+            pltpu.VMEM((n, parts, 4) + block, BF),
             pltpu.VMEM((n, 3, parts) + block, BF),
-            pltpu.VMEM((n, 2, parts, 2, 2, 2, 2) + block, BF),
+            pltpu.VMEM((n, 2, parts, 2, 2, 4) + block, BF),
         ]
 
-    qrows = 3 * width // 4
+    qrows = 3 * width // 8
+    quarter = (2, 2, 2, qrows, LANES)
     scratch = [
+        pltpu.VMEM((tokens, features), F32),
+        pltpu.VMEM((tokens, features), BF),
+        pltpu.VMEM((tokens, features), BF),
+        pltpu.VMEM((tokens, BLOCK), BF),
+        pltpu.VMEM((2, 2, 2, 4, PIECE, features), BF),
+        pltpu.VMEM((2, 4, width // 8, features), BF),
         pltpu.VMEM((3 * width, features), F32),
+        pltpu.VMEM((LEN, width), BF),
         pltpu.VMEM((width, LEN), BF),
         pltpu.VMEM((width, LEN), F32),
         pltpu.VMEM((LEN, width), F32),
         pltpu.VMEM((LEN, width), F32),
-        pltpu.VMEM((2, features, CHUNK), BF),
+        pltpu.VMEM((features, CHUNK // 2), BF),
         pltpu.VMEM((6, 24, features), F32),
         pltpu.VMEM((5, 24, features), F32),
     ]
-    scratch += sum_buffers(chunks, 2, 16)
-    scratch += sum_buffers(1, 1, features // 16)
+    scratch += sum_buffers(chunks, 2, PIECE)
+    scratch += sum_buffers(1, 1, features // 32)
     scratch += [
-        pltpu.VMEM((count, 2, 2, 2, qrows, LANES), BF),
+        pltpu.VMEM((count, 2) + quarter, BF),
+        pltpu.VMEM((count,) + quarter, BF),
         pltpu.VMEM((count, 2, 2, qrows, LANES), BF),
         pltpu.VMEM((count, 2, qrows, LANES), BF),
-        pltpu.VMEM((count, qrows, LANES), BF),
-        pltpu.VMEM((3, qrows, LANES), BF),
-        pltpu.VMEM((2, 2, 2, qrows, LANES), BF),
+        pltpu.VMEM((3, 2, qrows, LANES), BF),
+        pltpu.VMEM((2,) + quarter, BF),
     ]
     dma = pltpu.SemaphoreType.DMA
     scratch += [
         dma((chunks, MatrixSum.COPIES)),
         dma((chunks, MatrixSum.COPIES)),
-        dma((chunks, 2)),
+        dma((chunks,)),
         dma((1, MatrixSum.COPIES)),
         dma((1, MatrixSum.COPIES)),
-        dma((1, 2)),
-        dma((count, 7)),
-        dma((count, 7)),
+        dma((1,)),
+        dma((count, GroupSum.COPIES)),
+        dma((count, GroupSum.COPIES)),
         dma((5,)),
         dma((5,)),
         dma((chunks + 1, 2)),
+        dma((plan.blocks,)),
+        dma((count,)),
+        dma((3,)),
+        dma((2,)),
     ]
     results = pl.pallas_call(
-        functools.partial(late_kernel, chunks),
-        grid=(2 * count,),
+        functools.partial(late_kernel, plan),
+        grid=(plan.end,),
         in_specs=in_specs,
         out_specs=out_specs,
         out_shape=out_shape,
@@ -1027,22 +1210,28 @@
         ),
         name="late_kernel",
     )(
+        gf,
+        nl,
+        slope,
+        dw,
+        uw,
+        xh,
+        inv,
+        gs,
+        gain,
         x,
         w,
         ow,
+        ctx,
         q,
         k,
         v,
         lse,
-        ga,
-        gf,
         mask,
         *early,
         down.reshape(chunked),
-        up.reshape(chunked),
-        outw.reshape(squared),
     )
-    dx, wg, sums, down_sum, up_sum, outw_sum = results
+    sums, dx, wg, down_sum, up_sum, outw_sum = results[:6]
     return (
         dx,
         wg,
@@ -1210,19 +1399,24 @@
     features = tokens.shape[1]
     width = qkv_weight.shape[2]
     masked = (span_mask == 1)[:, None]
-    inputs = jnp.where(masked, mask_embedding[None, :], tokens)
-    inputs_wide = inputs.astype(F32)
     validity = valid_mask.astype(F32)[:, None]
-
     direct = dp == 8 and head == 4 and features == 2 * LANES and tokens.shape[0] == 2 * LEN
-    own = jnp.transpose(qkv_weight, (1, 0, 2))
     if direct:
+        mask_column = (span_mask == 1).astype(F32)[:, None]
         bias_block = jnp.pad(jnp.stack([query_bias, value_bias]).astype(F32), ((0, 6), (0, 0)))
         out_parts = out_weight.reshape(head, width, features)
-        q, k, v, ctx, lse, attended, weights = early_call(
-            inputs, own, bias_block, out_parts, out_bias[None, :]
+        q, k, v, ctx, lse, attended, inputs, weights = early_call(
+            tokens,
+            mask_column,
+            mask_embedding[None, :],
+            jnp.transpose(qkv_weight, (1, 2, 0)),
+            bias_block,
+            out_parts,
+            out_bias[None, :],
         )
     else:
+        inputs = jnp.where(masked, mask_embedding[None, :], tokens)
+        own = jnp.transpose(qkv_weight, (1, 0, 2))
         core = bit_of("dp", 0)
         half = lax.dynamic_slice_in_dim(own, core * (features // 2), features // 2, 1)
         halves = [half]
@@ -1248,12 +1442,15 @@
             )
             saved.append((q, k, v, ctx, lse))
 
+    inputs_wide = inputs.astype(F32)
     normed, normal_first, inverse_first = norm_forward(
         inputs_wide + attended, norm1_gain, norm1_bias
     )
     normed_low = normed.astype(BF)
     preact = dot_nn(normed_low, up_weight) + up_bias
-    activated = (preact * phi(preact)).astype(BF)
+    share = phi(preact)
+    activated = (preact * share).astype(BF)
+    slope = share + preact * jnp.exp(-0.5 * preact * preact) * (1.0 / math.sqrt(2.0 * math.pi))
     feedout = dot_nn(activated, down_weight) + down_bias
     result, normal_second, inverse_second = norm_forward(normed + feedout, norm2_gain, norm2_bias)
     grad_output = out_grad.astype(F32) * validity
@@ -1263,17 +1460,6 @@
     grad_feed = grad_second.astype(BF)
     down_bias_grad = jnp.sum(grad_feed, axis=0, dtype=F32)
     down_local = dot_tn(activated, grad_feed).astype(BF)
-    slope = phi(preact) + preact * jnp.exp(-0.5 * preact * preact) * (
-        1.0 / math.sqrt(2.0 * math.pi)
-    )
-    grad_preact = (dot_nt(grad_feed, down_weight) * slope).astype(BF)
-    up_bias_grad = jnp.sum(grad_preact, axis=0, dtype=F32)
-    grad_normed = dot_nt(grad_preact, up_weight) + grad_second
-    grad_first, gain_first_grad, bias_first_grad = norm_backward(
-        grad_normed, normal_first, inverse_first, norm1_gain
-    )
-    grad_attended = grad_first.astype(BF)
-    out_bias_grad = jnp.sum(grad_attended, axis=0, dtype=F32)
     squares = jnp.stack(
         [
             jnp.sum(validity * inputs_wide * inputs_wide),
@@ -1282,40 +1468,30 @@
             jnp.sum(validity),
         ]
     )
-    early = [
-        down_bias_grad,
-        gain_second_grad,
-        bias_second_grad,
-        gain_first_grad,
-        bias_first_grad,
-        out_bias_grad,
-        up_bias_grad,
-        squares,
-    ]
     if direct:
-        up_local = dot_tn(grad_preact, normed_low).astype(BF)
-        outw = lax.dot_general(
-            ctx, grad_attended, (((1,), (0,)), ((), ())), preferred_element_type=F32
-        ).astype(BF)
-        outw_local = absolute([outw[g] for g in range(head)], 0)
-        vectors = [one[None, :] for one in early[:6]]
-        vectors.append(up_bias_grad.reshape(-1, features))
+        vectors = [one[None, :] for one in (down_bias_grad, gain_second_grad, bias_second_grad)]
         vectors.append(jnp.pad(squares, (0, features - 4))[None, :])
         dx, weight_sum, sums, down_sum, up_sum, outw_sum = late_call(
+            grad_feed,
+            normed_low,
+            slope,
+            down_weight,
+            up_weight,
+            normal_first,
+            inverse_first,
+            grad_second,
+            norm1_gain[None, :],
             inputs,
             weights,
             out_parts,
+            ctx,
             q,
             k,
             v,
             lse,
-            grad_attended,
-            grad_first,
-            (span_mask == 1).astype(F32)[:, None],
+            mask_column,
             vectors,
             down_local,
-            up_local,
-            outw_local,
         )
         tokens_grad = jnp.where(masked, 0.0, dx)
         down_weight_grad = down_sum.astype(F32)
@@ -1348,7 +1524,25 @@
             stream_rms,
         )
 
+    grad_preact = (dot_nt(grad_feed, down_weight) * slope).astype(BF)
+    up_bias_grad = jnp.sum(grad_preact, axis=0, dtype=F32)
     up_local = dot_tn(normed_low, grad_preact).astype(BF)
+    grad_normed = dot_nt(grad_preact, up_weight) + grad_second
+    grad_first, gain_first_grad, bias_first_grad = norm_backward(
+        grad_normed, normal_first, inverse_first, norm1_gain
+    )
+    grad_attended = grad_first.astype(BF)
+    out_bias_grad = jnp.sum(grad_attended, axis=0, dtype=F32)
+    early = [
+        down_bias_grad,
+        gain_second_grad,
+        bias_second_grad,
+        gain_first_grad,
+        bias_first_grad,
+        out_bias_grad,
+        up_bias_grad,
+        squares,
+    ]
     down_weight_grad = all_reduce_matrix(down_local, dp, head, 0)
     up_weight_grad = all_reduce_matrix(up_local, dp, head, 1)
     early_sum = all_reduce_small(jnp.concatenate(early), dp, head)

time: 331 us -> 314 us (0.949)
  matrix products: 54.7 us -> 27.9 us
  Pallas kernels: 217 us -> 230 us
    pallas_call x1, Pallas kernels: 153 us -> 181 us  [late_call(): pl.pallas_call(functools.partial(late_kernel, plan), grid=(plan.end,), in...]
    dot_general x3 -> x0, matrix products: 21.4 us -> none  [the longest x2 18.8 us: dot_nt(): lax.dot_general(left, right, (((1,), (1,)), ((), ())), preferred_element_...]
    pallas_call x1, Pallas kernels: 64.6 us -> 49.5 us  [early_call(): pl.pallas_call(early_kernel, grid=(groups * rows,), in_specs=[pl.BlockSpe...]
    dot_general x2 -> x1, matrix products: 18.5 us -> 9.66 us  [dot_tn(): lax.dot_general(left, right, (((0,), (0,)), ((), ())), preferred_element_...]
    select_n x2 -> x0, other arithmetic: 4.09 us -> none  [the longest x1 2.76 us: body(): inputs = jnp.where(masked, mask_embedding[None, :], tokens)]
    dot_general x2, matrix products: 14.8 us -> 18.2 us  [dot_nn(): lax.dot_general(left, right, (((1,), (0,)), ((), ())), preferred_element_...]
where the time goes in v3:
time: 314 us; the launch traced here: 313 us
  Pallas kernels  230 us (73%)
  other arithmetic  39.1 us (12%)
  matrix products  27.9 us (9%)
  local copies, waits for them, and re-layouts  14.6 us (5%)
    pallas_call x1, Pallas kernels, late_call(): pl.pallas_call(functools.partial(late_kernel, plan), grid=(plan.end,), in...  181 us
    pallas_call x1, Pallas kernels, early_call(): pl.pallas_call(early_kernel, grid=(groups * rows,), in_specs=[pl.BlockSpe...  49.5 us
    dot_general x2, matrix products, dot_nn(): lax.dot_general(left, right, (((1,), (0,)), ((), ())), preferred_element_...  18.2 us
    dot_general x1, matrix products, dot_tn(): lax.dot_general(left, right, (((0,), (0,)), ((), ())), preferred_element_...  9.66 us
    convert_element_type x1, other arithmetic, body(): up_weight_grad = up_sum.astype(F32)  7.37 us
    convert_element_type x1, other arithmetic, body(): down_weight_grad = down_sum.astype(F32)  6.95 us

profile of v3, /device:TPU:0, one launch (start us, length us, event | category | flops | bytes accessed | tf_op | source)
XLA Modules:
  0.0 313.3 jit_solution(9672101917212538094)
XLA Ops:
  0.7 0.0 copy-start.11
  0.7 1.3 fusion.17
  1.9 1.0 copy.36.mask_ref
  2.9 1.3 broadcast_in_dim.55.embed_ref
  4.2 0.7 stack.25
  4.9 0.7 stack.24
  5.5 0.6 fusion.15.bias_ref
  6.1 1.3 broadcast_in_dim.56.ob_ref
  7.4 49.5 %early_kernel.1 = (bf16[4,1024,192]{2,1,0:T(8,128)(2,1)}, bf16[4,1024,192]{2,1,0:T(8,128)(2,1)}, bf16[4,1024,192]{2,1,0:T(8,128)(2,1)}, bf16[4,1024,192]{2,1,0:T...) custom-call(bf16[1024,768]{1,0:T(8,128)(2,1)} %tokens_ref.1, ...), custom_call_target="tpu_custom_call" | custom-call | tf_op jit(solution)/shard_map/early_kernel/pallas_call | solution.py:429
  56.9 0.0 copy-start
  56.9 0.0 copy-start.1
  56.9 0.0 copy-done.11
  57.0 2.9 fusion.11
  59.8 0.0 copy-start.10
  59.9 0.0 copy-start.13
  59.9 0.3 copy-done
  60.2 0.5 copy-done.1
  60.7 3.0 fusion.5
  63.7 0.0 copy-done.10
  63.7 0.0 copy-done.13
  63.7 0.0 slice-start.1
  63.7 0.0 copy-start.15
  63.7 0.0 slice-start.2
  63.8 0.8 fusion.10
  64.5 0.0 copy-start.4
  64.5 0.0 copy-start.2
  64.6 0.0 slice-done
  64.6 0.2 slice-done.1
  64.8 0.0 copy-done.15
  64.8 12.8 %fusion.3 = (f32[1024,3072]{1,0:T(8,128)}, bf16[1024,3072]{1,0:T(8,128)(2,1)S(1)}) fusion(f32[3072]{0:T(1024)S(1)} %copy-done.15, bf16[1024,768]{1,0:T(8,128)(2,1)S(1)} %get-tuple-element.65.nl_hbm, bf16[768,3072]{1,0:T(8,128)(2,1)S(1)} %bitcast.30), kind=kOutput, calls=%fused_computation.4 | convolution fusion | flops 4866441216 | bytes 25178112 | tf_op jit(solution)/shard_map/dot_general | solution.py:19
  77.6 0.0 copy-done.4
  77.6 0.0 copy-done.2
  77.6 0.0 slice-done.2
  77.6 0.0 slice-done.3
  77.6 0.0 copy-done.12
  77.6 5.4 %fusion.16 = (f32[1024]{0:T(1024)S(1)}, f32[1024,768]{1,0:T(8,128)S(1)}, f32[1024,768]{1,0:T(8,128)S(1)}) fusion(f32[768]{0:T(1024)S(1)} %copy-done.12, f32[768]{0:T(1024)S(1)} %copy-done.13, f32[1024,768]{1,0:T(8,128)S(1)} %get-tuple-element.66.xh_ref, f32[768]{0:T(1024)S(1)} %copy-done.10, bf16[1024,3072]{1,0:T(8,128)(2,1)S(1)} %get-tuple-element.70, ...), kind=kOutput, calls=%fused_computation.62 | convolution fusion | flops 4835769344 | bytes 20460544 | tf_op jit(solution)/shard_map/dot_general | solution.py:19
  83.0 0.0 copy-done.16
  83.0 0.0 copy-start.3
  83.0 0.0 copy-start.9
  83.1 0.5 multiply_reduce_fusion.2
  83.6 0.8 copy-done.3
  84.4 0.0 copy-done.9
  84.5 3.4 %multiply_reduce_fusion = (f32[768]{0:T(1024)S(1)}, f32[1024]{0:T(1024)S(1)}, f32[1024]{0:T(1024)S(1)}, f32[768]{0:T(1024)S(1)}, f32[]{:T(128)}) fusion(bf16[1024,768]{1,0:T(8,128)(2,1)S(1)} %copy-done.3, f32[1024,768]{1,0:T(8,128)S(1)} %get-tuple-element.64, f32[1024]{0:T(1024)S(1)} %convert_element_type.53, f32[1024]{0:T(1024)S(1)} %add_rsqrt_fusion, ...), kind=kLoop, calls=%fused_computation.16 | loop fusion | flops 11792895 | bytes 7897092 | tf_op jit(solution)/shard_map/reduce_sum | solution.py:1362
  87.8 3.0 convert_reduce_fusion
  90.8 1.3 copy.38.inv_ref
  92.1 0.6 broadcast_in_dim.59.gain_ref
  92.7 0.6 broadcast_in_dim.60.early_0
  93.3 0.6 broadcast_in_dim.61.early_1
  93.9 0.6 broadcast_in_dim.62.early_2
  94.5 0.6 convert_reduce_fusion.1
  95.1 2.7 select_maximum_fusion
  97.7 0.6 broadcast_in_dim.63.early_squares
  98.3 9.7 %convolution_convert_fusion = bf16[3072,768]{1,0:T(8,128)(2,1)} fusion(bf16[1024,3072]{1,0:T(8,128)(2,1)} %copy-done.16, bf16[1024,768]{1,0:T(8,128)(2,1)S(1)} %get-tuple-element.61.gf_ref), kind=kOutput, calls=%fused_computation.7 | convolution fusion | flops 4834197504 | bytes 12582912 | tf_op jit(solution)/shard_map/dot_general | solution.py:27
  108.0 180.6 %late_kernel.1 = (f32[24,768]{1,0:T(8,128)}, f32[1024,768]{1,0:T(8,128)}, f32[576,768]{1,0:T(8,128)}, bf16[3,2,2,2,2,4,16,768]{7,6,5,4,3,2,1,0:T(8,128)(2,1)}, b...) custom-call(bf16[1024,768]{1,0:T(8,128)(2,1)} %copy-done.5, ...), custom_call_target="tpu_custom_call" | custom-call | tf_op jit(solution)/shard_map/late_kernel/pallas_call | solution.py:1198
  288.6 3.9 %broadcast_select_fusion = f32[1024,768]{1,0:T(8,128)} fusion(f32[1024,768]{1,0:T(8,128)} %get-tuple-element.39, pred[1024]{0:T(1024)(128)(4,1)} %get-tuple-element.68), kind=kLoop, calls=%fused_computation.32 | loop fusion | flops 786432 | bytes 6292480 | tf_op jit(solution)/shard_map/jit(_where)/select_n | solution.py:1496
  292.5 0.7 slice_reduce_fusion
  293.2 0.6 constant_dynamic-slice_fusion
  293.7 1.7 bitcast_convert_fusion.1
  295.4 7.4 %convert_element_type.59 = f32[768,3072]{1,0:T(8,128)} convert(bf16[768,3072]{1,0:T(8,128)(2,1)} %get-tuple-element.43) | non-fusion elementwise | flops 2359296 | bytes 14155776 | tf_op jit(solution)/shard_map/convert_element_type | solution.py:1498
  302.8 0.6 reshape.118
  303.4 6.9 %bitcast_convert_fusion = f32[3072,768]{1,0:T(8,128)} fusion(bf16[3,2,2,2,2,4,16,768]{7,6,5,4,3,2,1,0:T(8,128)(2,1)} %get-tuple-element.44), kind=kLoop, calls=%fused_computation.11 | loop fusion | flops 2359296 | bytes 14155776 | tf_op jit(solution)/shard_map/convert_element_type | solution.py:1497
  310.3 0.6 slice.44
  311.6 0.5 sqrt_bitcast_fusion
  312.1 1.2 copy.42
  (23 shorter events, 0.1 us)
Async XLA Ops:
  0.7 56.3 %copy-start.11 = (s32[1024]{0:T(1024)S(1)}, s32[1024]{0:T(1024)}, u32[]{:S(2)}) copy-start(s32[1024]{0:T(1024)} %param.20) | copy-start | bytes 12292
  56.9 3.3 %copy-start = (f32[1024,768]{1,0:T(8,128)S(1)}, f32[1024,768]{1,0:T(8,128)}, u32[]{:S(2)}) copy-start(f32[1024,768]{1,0:T(8,128)} %get-tuple-element.32) | copy-start | bytes 9437188
  56.9 3.8 %copy-start.1 = (bf16[1024,768]{1,0:T(8,128)(2,1)S(1)}, bf16[1024,768]{1,0:T(8,128)(2,1)}, u32[]{:S(2)}) copy-start(bf16[1024,768]{1,0:T(8,128)(2,1)} %get-tuple-element.31.x_hbm) | copy-start | bytes 4718596
  59.8 3.9 %copy-start.10 = (f32[768]{0:T(1024)S(1)}, f32[768]{0:T(1024)}, u32[]{:S(2)}) copy-start(f32[768]{0:T(1024)} %param.27) | copy-start | bytes 9220
  59.9 3.9 %copy-start.13 = (f32[768]{0:T(1024)S(1)}, f32[768]{0:T(1024)}, u32[]{:S(2)}) copy-start(f32[768]{0:T(1024)} %param.28) | copy-start | bytes 9220
  60.7 3.9 %slice-start = ((s8[4718592]{0:T(1024)(128)(4,1)}), s8[4194304]{0:T(1024)(128)(4,1)S(1)}, s32[]{:S(2)}) async-start(s8[4718592]{0:T(1024)(128)(4,1)} %bitcast.29), calls=%async_computation | async-start | bytes 8388608
  63.7 1.0 slice-start.1
  63.7 1.0 copy-start.15
  63.7 13.9 %slice-start.2 = ((s8[4718592]{0:T(1024)(128)(4,1)}), s8[4194304]{0:T(1024)(128)(4,1)S(1)}, s32[]{:S(2)}) async-start(s8[4718592]{0:T(1024)(128)(4,1)} %bitcast.31), calls=%async_computation.2 | async-start | bytes 8388608
  64.5 13.1 %copy-start.4 = (bf16[1024,768]{1,0:T(8,128)(2,1)}, bf16[1024,768]{1,0:T(8,128)(2,1)S(1)}, u32[]{:S(2)}) copy-start(bf16[1024,768]{1,0:T(8,128)(2,1)S(1)} %get-tuple-element.65.nl_hbm) | copy-start | bytes 4718596
  64.5 13.0 %copy-start.2 = (f32[1024,768]{1,0:T(8,128)}, f32[1024,768]{1,0:T(8,128)S(1)}, u32[]{:S(2)}) copy-start(f32[1024,768]{1,0:T(8,128)S(1)} %get-tuple-element.66.xh_ref) | copy-start | bytes 9437188
  64.8 12.8 %slice-start.3 = ((s8[4718592]{0:T(1024)(128)(4,1)}), s8[524288]{0:T(1024)(128)(4,1)S(1)}, s32[]{:S(2)}) async-start(s8[4718592]{0:T(1024)(128)(4,1)} %bitcast.31), calls=%async_computation.3 | async-start | bytes 1048576
  64.8 12.8 %copy-start.12 = (f32[768]{0:T(1024)S(1)}, f32[768]{0:T(1024)}, u32[]{:S(2)}) copy-start(f32[768]{0:T(1024)} %param.32) | copy-start | bytes 9220
  77.6 5.4 %copy-start.16 = (bf16[1024,3072]{1,0:T(8,128)(2,1)}, bf16[1024,3072]{1,0:T(8,128)(2,1)S(1)}, u32[]{:S(2)}) copy-start(bf16[1024,3072]{1,0:T(8,128)(2,1)S(1)} %get-tuple-element.70) | copy-start | bytes 18874372
  83.0 1.4 copy-start.3
  83.0 1.4 copy-start.9
  84.5 3.4 %copy-start.14 = (f32[768]{0:T(1024)S(1)}, f32[768]{0:T(1024)}, u32[]{:S(2)}) copy-start(f32[768]{0:T(1024)} %param.34) | copy-start | bytes 9220
  90.8 17.1 %copy-start.5 = (bf16[1024,768]{1,0:T(8,128)(2,1)}, bf16[1024,768]{1,0:T(8,128)(2,1)S(1)}, u32[]{:S(2)}) copy-start(bf16[1024,768]{1,0:T(8,128)(2,1)S(1)} %get-tuple-element.61.gf_ref) | copy-start | bytes 4718596
  288.6 4.0 %copy-start.8 = (f32[24,768]{1,0:T(8,128)S(1)}, f32[24,768]{1,0:T(8,128)}, u32[]{:S(2)}) copy-start(f32[24,768]{1,0:T(8,128)} %get-tuple-element.40) | copy-start | bytes 221188
  288.6 5.2 %copy-start.7 = (bf16[1,2,1,2,2,4,24,768]{7,6,5,4,3,2,1,0:T(8,128)(2,1)S(1)}, bf16[1,2,1,2,2,4,24,768]{7,6,5,4,3,2,1,0:T(8,128)(2,1)}, u32[]{:S(2)}) copy-start(bf16[1,2,1,2,2,4,24,768]{7,6,5,4,3,2,1,0:T(8,128)(2,1)} %get-tuple-element.42) | copy-start | bytes 3538948
  303.4 8.7 %copy-start.6 = (f32[576,768]{1,0:T(8,128)S(1)}, f32[576,768]{1,0:T(8,128)}, u32[]{:S(2)}) copy-start(f32[576,768]{1,0:T(8,128)} %get-tuple-element.41) | copy-start | bytes 5308420

commit v4 on v3

--- a/solution.py
+++ b/solution.py
@@ -272,7 +272,8 @@
     mask_ref,
     embed_ref,
     own_ref,
-    bias_ref,
+    qb_ref,
+    vb_ref,
     ow_ref,
     ob_ref,
     q_ref,
@@ -322,7 +323,7 @@
         return remote(half_of(g), half_of(g), send.at[1, g], recv.at[1, g], place.core())
 
     def bias(g):
-        return remote(bias_ref, b_all.at[g], send.at[2, g], recv.at[2, g], place.up(g))
+        return remote(b_all.at[0], b_all.at[g], send.at[2, g], recv.at[2, g], place.up(g))
 
     def store(g):
         return pltpu.make_async_copy(w_all.at[g], w_out.at[g], local.at[2 + g])
@@ -335,13 +336,16 @@
         direct(1).start()
         direct(2).start()
         load.start()
-        bias_load = pltpu.make_async_copy(bias_ref, b_all.at[0], local.at[1])
-        bias_load.start()
+        b_all[0] = jnp.zeros(b_all.shape[1:], F32)
+        b_all[0, 0:1, :] = qb_ref[...].astype(F32).reshape(1, width)
+        b_all[0, 1:2, :] = vb_ref[...].astype(F32).reshape(1, width)
+        load.wait()
+        store(0).start()
+
+    @pl.when(step == 1)
+    def _():
         for g in range(1, 4):
             bias(g).start()
-        load.wait()
-        bias_load.wait()
-        store(0).start()
 
     for g in range(1, 4):
 
@@ -351,7 +355,8 @@
             bias(g).wait()
             store(g).start()
 
-    x = jnp.where(mask_ref[...] == 1.0, embed_ref[...].astype(F32), tokens_ref[...].astype(F32))
+    embed = embed_ref[...].astype(F32).reshape(1, tokens_ref.shape[1])
+    x = jnp.where(mask_ref[...] == 1.0, embed, tokens_ref[...].astype(F32))
     x = x.astype(BF)
 
     @pl.when(step < 2)
@@ -383,7 +388,7 @@
 
     @pl.when(group == 0)
     def _():
-        out_ref[spot, :] = result + ob_ref[...]
+        out_ref[spot, :] = result + ob_ref[...].reshape(1, result.shape[1])
 
     @pl.when(group > 0)
     def _():
@@ -417,7 +422,7 @@
             store(g).wait()
 
 
-def early_call(x, mask, embed, own, bias, ow, ob):
+def early_call(x, mask, embed, own, qb, vb, ow, ob):
     tokens, features = x.shape
     width = own.shape[1]
     groups = features // width
@@ -432,11 +437,12 @@
         in_specs=[
             pl.BlockSpec((LEN, features), lambda s: (s % 2, 0)),
             pl.BlockSpec((LEN, 1), lambda s: (s % 2, 0)),
-            pl.BlockSpec((1, features), lambda s: (0, 0)),
+            pl.BlockSpec((features,), lambda s: (0,)),
             hbm,
-            hbm,
+            pl.BlockSpec((width,), lambda s: (0,)),
+            pl.BlockSpec((width,), lambda s: (0,)),
             pl.BlockSpec((groups, width, features), lambda s: (0, 0, 0)),
-            pl.BlockSpec((1, features), lambda s: (0, 0)),
+            pl.BlockSpec((features,), lambda s: (0,)),
         ],
         out_specs=[
             per_head,
@@ -472,7 +478,7 @@
             has_side_effects=True,
         ),
         name="early_kernel",
-    )(x, mask, embed, own, bias, ow, ob)
+    )(x, mask, embed, own, qb, vb, ow, ob)
 
 
 LANES = 384
@@ -687,7 +693,10 @@
     early_0,
     early_1,
     early_2,
-    early_squares,
+    early_3,
+    early_4,
+    early_5,
+    early_6,
     down_ref,
     vec_ref,
     dx_out,
@@ -778,9 +787,10 @@
         )
         nl_load.wait()
         vec[...] = jnp.zeros_like(vec)
-        for index, ref in enumerate((early_0, early_1, early_2)):
-            vec[0, index : index + 1, :] = ref[...]
-        vec[0, 10:11, :] = early_squares[...]
+        rows = (early_0, 0), (early_1, 1), (early_2, 2)
+        rows += (early_3, 10), (early_4, 11), (early_5, 12), (early_6, 13)
+        for ref, index in rows:
+            vec[0, index : index + 1, :] = ref[...].reshape(1, vec.shape[2])
 
     def down_store(i):
         return pltpu.make_async_copy(ff_full.at[i], down_out.at[i], store_sem.at[i, 0])
@@ -921,7 +931,7 @@
         rows = pl.ds(pl.multiple_of((step - plan.blocks) * BLOCK, BLOCK), BLOCK)
         upstream = dx[rows, :] + gs_ref[...]
         normal = xh_ref[...]
-        scaled = upstream * gain_ref[...]
+        scaled = upstream * gain_ref[...].reshape(1, upstream.shape[1])
         mean = jnp.mean(scaled, axis=1, keepdims=True)
         along = jnp.mean(scaled * normal, axis=1, keepdims=True)
         hidden = inv_ref[...] * (scaled - mean - normal * along)
@@ -1242,6 +1252,33 @@
     )
 
 
+def final_kernel(down_ref, up_ref, outw_ref, dx_ref, mask_ref, down_out, up_out, outw_out, dx_out):
+    down_out[...] = down_ref[...].astype(F32)
+    up_out[...] = up_ref[...].astype(F32)
+    outw_out[...] = outw_ref[...].astype(F32)
+    dx_out[...] = jnp.where(mask_ref[...] == 1.0, 0.0, dx_ref[...])
+
+
+def final_call(down, up, outw, dx, mask):
+    steps = 8
+    arrays = (down, up, outw, dx)
+
+    def spec(shape):
+        return pl.BlockSpec((shape[0] // steps, shape[1]), lambda s: (s, 0))
+
+    return pl.pallas_call(
+        final_kernel,
+        grid=(steps,),
+        in_specs=[spec(one.shape) for one in arrays + (mask,)],
+        out_specs=[spec(one.shape) for one in arrays],
+        out_shape=[jax.ShapeDtypeStruct(one.shape, F32) for one in arrays],
+        compiler_params=pltpu.CompilerParams(
+            dimension_semantics=("arbitrary",), vmem_limit_bytes=63 << 20
+        ),
+        name="final_kernel",
+    )(down, up, outw, dx, mask)
+
+
 def swap(value, axis, mask, size):
     return lax.ppermute(value, axis, [(i, i ^ mask) for i in range(size)])
 
@@ -1403,16 +1440,16 @@
     direct = dp == 8 and head == 4 and features == 2 * LANES and tokens.shape[0] == 2 * LEN
     if direct:
         mask_column = (span_mask == 1).astype(F32)[:, None]
-        bias_block = jnp.pad(jnp.stack([query_bias, value_bias]).astype(F32), ((0, 6), (0, 0)))
         out_parts = out_weight.reshape(head, width, features)
         q, k, v, ctx, lse, attended, inputs, weights = early_call(
             tokens,
             mask_column,
-            mask_embedding[None, :],
+            mask_embedding,
             jnp.transpose(qkv_weight, (1, 2, 0)),
-            bias_block,
+            query_bias,
+            value_bias,
             out_parts,
-            out_bias[None, :],
+            out_bias,
         )
     else:
         inputs = jnp.where(masked, mask_embedding[None, :], tokens)
@@ -1469,8 +1506,13 @@
         ]
     )
     if direct:
-        vectors = [one[None, :] for one in (down_bias_grad, gain_second_grad, bias_second_grad)]
-        vectors.append(jnp.pad(squares, (0, features - 4))[None, :])
+        vectors = [down_bias_grad, gain_second_grad, bias_second_grad]
+        vectors += [
+            jnp.sum(validity * inputs_wide * inputs_wide, axis=0),
+            jnp.sum(validity * attended * attended, axis=0),
+            jnp.sum(validity * feedout * feedout, axis=0),
+            jnp.broadcast_to(jnp.sum(validity), (features,)),
+        ]
         dx, weight_sum, sums, down_sum, up_sum, outw_sum = late_call(
             grad_feed,
             normed_low,
@@ -1480,7 +1522,7 @@
             normal_first,
             inverse_first,
             grad_second,
-            norm1_gain[None, :],
+            norm1_gain,
             inputs,
             weights,
             out_parts,
@@ -1493,17 +1535,15 @@
             vectors,
             down_local,
         )
-        tokens_grad = jnp.where(masked, 0.0, dx)
-        down_weight_grad = down_sum.astype(F32)
-        up_weight_grad = up_sum.astype(F32)
-        out_weight_grad = outw_sum.astype(F32)
+        down_weight_grad, up_weight_grad, out_weight_grad, tokens_grad = final_call(
+            down_sum, up_sum, outw_sum, dx, mask_column
+        )
         weight_grad = jnp.transpose(weight_sum.reshape(3, width, features), (2, 0, 1))
         me = lax.axis_index("head")
         first_grad = lax.dynamic_slice(sums, (16 + me, 0), (1, width))[0]
         third_grad = lax.dynamic_slice(sums, (20 + me, 0), (1, width))[0]
-        squares = sums[10, :4]
-        count = jnp.maximum(squares[3], 1.0)
-        stream_rms = jnp.sqrt(squares[:3] / (count * features))
+        count = jnp.maximum(sums[13, 0], 1.0)
+        stream_rms = jnp.sqrt(jnp.sum(sums[10:13], axis=1) / (count * features))
         return (
             result.astype(BF),
             tokens_grad,

time: 314 us -> 300 us (0.955)
  other arithmetic: 39.1 us -> 14.9 us
  Pallas kernels: 230 us -> 244 us
  local copies, waits for them, and re-layouts: 14.6 us -> 10.7 us
    convert_element_type x3 -> x0, other arithmetic: 16 us -> none  [the longest x1 7.37 us: body(): up_weight_grad = up_sum.astype(F32)]
    pallas_call x0 -> x1, Pallas kernels: none -> 14.3 us  [final_call(): pl.pallas_call(final_kernel, grid=(steps,), in_specs=[spec(one.shape) for...]
    broadcast_in_dim x7 -> x1, local copies, waits for them, and re-layouts: 5.43 us -> 1.24 us  [body(): jnp.broadcast_to(jnp.sum(validity), (features,))]
    select_n x1 -> x0, other arithmetic: 3.94 us -> none  [body(): tokens_grad = jnp.where(masked, 0.0, dx)]
where the time goes in v4:
time: 300 us
  Pallas kernels  244 us (81%)
  matrix products  27.9 us (9%)
  other arithmetic  14.9 us (5%)
  local copies, waits for them, and re-layouts  10.7 us (4%)
    pallas_call x1, Pallas kernels, late_call(): pl.pallas_call(functools.partial(late_kernel, plan), grid=(plan.end,), in...  181 us
    pallas_call x1, Pallas kernels, early_call(): pl.pallas_call(early_kernel, grid=(groups * rows,), in_specs=[pl.BlockSpe...  49.6 us
    dot_general x2, matrix products, dot_nn(): lax.dot_general(left, right, (((1,), (0,)), ((), ())), preferred_element_...  18.2 us
    pallas_call x1, Pallas kernels, final_call(): pl.pallas_call(final_kernel, grid=(steps,), in_specs=[spec(one.shape) for...  14.3 us
    dot_general x1, matrix products, dot_tn(): lax.dot_general(left, right, (((0,), (0,)), ((), ())), preferred_element_...  9.65 us

profile of v4, /device:TPU:0, one launch (start us, length us, event | category | flops | bytes accessed | tf_op | source)
XLA Modules:
  0.0 299.5 jit_solution(8963990339533389567)
XLA Ops:
  0.7 0.0 copy-start.9
  0.7 0.7 compare_convert_fusion
  1.4 1.0 copy.35.mask_ref
  2.4 49.6 %early_kernel.1 = (bf16[4,1024,192]{2,1,0:T(8,128)(2,1)}, bf16[4,1024,192]{2,1,0:T(8,128)(2,1)}, bf16[4,1024,192]{2,1,0:T(8,128)(2,1)}, bf16[4,1024,192]{2,1,0:T...) custom-call(bf16[1024,768]{1,0:T(8,128)(2,1)} %tokens_ref.1, ...), custom_call_target="tpu_custom_call" | custom-call | tf_op jit(solution)/shard_map/early_kernel/pallas_call | solution.py:434
  51.9 0.0 copy-start
  52.0 0.0 copy-start.1
  52.0 0.0 copy-done.9
  52.0 2.9 fusion.11
  54.9 0.0 copy-start.8
  54.9 0.0 copy-start.10
  54.9 0.3 copy-done
  55.3 0.5 copy-done.1
  55.7 0.0 slice-start
  55.7 2.3 fusion.5
  58.1 0.0 copy-done.8
  58.1 0.0 copy-done.10
  58.1 0.0 slice-start.1
  58.1 0.0 copy-start.13
  58.1 0.0 slice-start.2
  58.1 0.7 fusion.10
  58.8 0.0 copy-start.3
  58.8 0.0 copy-start.2
  58.9 0.0 slice-done
  58.9 0.2 slice-done.1
  59.1 0.0 copy-done.13
  59.1 0.0 slice-start.3
  59.1 0.0 copy-start.11
  59.1 12.8 %fusion.3 = (f32[1024,3072]{1,0:T(8,128)}, bf16[1024,3072]{1,0:T(8,128)(2,1)S(1)}) fusion(f32[3072]{0:T(1024)S(1)} %copy-done.13, bf16[1024,768]{1,0:T(8,128)(2,1)S(1)} %get-tuple-element.73.nl_hbm, bf16[768,3072]{1,0:T(8,128)(2,1)S(1)} %bitcast.23), kind=kOutput, calls=%fused_computation.4 | convolution fusion | flops 4866441216 | bytes 25178112 | tf_op jit(solution)/shard_map/dot_general | solution.py:19
  71.9 0.0 copy-done.3
  71.9 0.0 copy-start.14
  71.9 0.0 copy-done.2
  71.9 0.0 slice-done.2
  72.0 0.0 slice-done.3
  72.0 0.0 copy-done.11
  72.0 5.4 %fusion.12 = (f32[1024]{0:T(1024)S(1)}, f32[1024,768]{1,0:T(8,128)S(1)}, f32[1024,768]{1,0:T(8,128)S(1)}) fusion(f32[768]{0:T(1024)S(1)} %copy-done.11, f32[768]{0:T(1024)S(1)} %copy-done.10, f32[1024,768]{1,0:T(8,128)S(1)} %get-tuple-element.74.xh_ref, f32[768]{0:T(1024)S(1)} %copy-done.8, bf16[1024,3072]{1,0:T(8,128)(2,1)S(1)} %get-tuple-element.76, ...), kind=kOutput, calls=%fused_computation.51 | convolution fusion | flops 4835769344 | bytes 20460544 | tf_op jit(solution)/shard_map/dot_general | solution.py:19
  77.4 0.0 copy-done.14
  77.4 0.0 copy-start.5
  77.4 0.0 copy-start.7
  77.4 0.5 multiply_reduce_fusion.2
  78.0 0.8 copy-done.5
  78.8 0.0 copy-done.7
  78.8 0.0 copy-start.12
  78.8 2.9 multiply_reduce_fusion
  81.7 0.0 copy-done.12
  81.7 3.6 %convert_reduce_fusion = (f32[768]{0:T(1024)}, bf16[1024,768]{1,0:T(8,128)(2,1)S(1)}, f32[1024,768]{1,0:T(8,128)}, bf16[1024,768]{1,0:T(8,128)(2,1)}) fusion(f32[1024]{0:T(1024)S(1)} %get-tuple-element.81, f32[1024,768]{1,0:T(8,128)S(1)} %get-tuple-element.72, f32[1024]{0:T(1024)S(1)} %broadcast_multiply_fusion.2, f32[1024]{0:T(1024)S(1)} %get-tuple-element.82, ...), kind=kLoop, calls=%fused_computation.16 | loop fusion | flops 11795712 | bytes 11039744 | tf_op jit(solution)/shard_map/reduce_sum | solution.py:1498
  85.3 0.0 copy-start.4
  85.3 1.3 copy.36.inv_ref
  86.6 0.6 convert_reduce_fusion.1
  87.2 1.2 broadcast_in_dim.8.early_6
  88.5 9.7 %convolution_convert_fusion = bf16[3072,768]{1,0:T(8,128)(2,1)} fusion(bf16[1024,3072]{1,0:T(8,128)(2,1)} %copy-done.14, bf16[1024,768]{1,0:T(8,128)(2,1)S(1)} %get-tuple-element.69.gf_ref), kind=kOutput, calls=%fused_computation.7 | convolution fusion | flops 4834197504 | bytes 12582912 | tf_op jit(solution)/shard_map/dot_general | solution.py:27
  98.1 0.0 copy-done.4
  98.1 180.6 %late_kernel.1 = (f32[24,768]{1,0:T(8,128)}, f32[1024,768]{1,0:T(8,128)}, f32[576,768]{1,0:T(8,128)}, bf16[3,2,2,2,2,4,16,768]{7,6,5,4,3,2,1,0:T(8,128)(2,1)}, b...) custom-call(bf16[1024,768]{1,0:T(8,128)(2,1)} %copy-done.4, ...), custom_call_target="tpu_custom_call" | custom-call | tf_op jit(solution)/shard_map/late_kernel/pallas_call | solution.py:1208
  278.8 0.0 copy-start.6
  278.8 14.3 %final_kernel.1 = (f32[3072,768]{1,0:T(8,128)}, f32[768,3072]{1,0:T(8,128)}, f32[768,768]{1,0:T(8,128)}, f32[1024,768]{1,0:T(8,128)}) custom-call(bf16[3072,768]{1,0:T(8,128)(2,1)} %bitcast.21, bf16[768,3072]{1,0:T(8,128)(2,1)} %get-tuple-element.44.up_ref, bf16[768,768]{1,0:T(8,128)(2,1)} %bitcast.28, f32[1024,768]{1,0:T(8,128)} %get-tuple-element.46.dx_ref, ...), custom_call_target="tpu_custom_call" | custom-call | tf_op jit(solution)/shard_map/final_kernel/pallas_call | solution.py:1269
  293.0 0.0 copy-done.6
  293.1 0.7 slice_reduce_fusion.1
  293.7 0.6 constant_dynamic-slice_fusion
  294.3 0.6 reshape.113
  294.9 0.1 slice_reduce_fusion
  295.0 0.5 slice.39
  296.2 0.5 divide_sqrt_fusion
  296.7 2.8 copy.40
  (9 shorter events, 0.0 us)
Async XLA Ops:
  0.7 51.3 %copy-start.9 = (s32[1024]{0:T(1024)S(1)}, s32[1024]{0:T(1024)}, u32[]{:S(2)}) copy-start(s32[1024]{0:T(1024)} %param.20) | copy-start | bytes 12292
  51.9 3.3 %copy-start = (f32[1024,768]{1,0:T(8,128)S(1)}, f32[1024,768]{1,0:T(8,128)}, u32[]{:S(2)}) copy-start(f32[1024,768]{1,0:T(8,128)} %get-tuple-element.36) | copy-start | bytes 9437188
  52.0 3.8 %copy-start.1 = (bf16[1024,768]{1,0:T(8,128)(2,1)S(1)}, bf16[1024,768]{1,0:T(8,128)(2,1)}, u32[]{:S(2)}) copy-start(bf16[1024,768]{1,0:T(8,128)(2,1)} %get-tuple-element.35.x_hbm) | copy-start | bytes 4718596
  54.9 3.2 %copy-start.8 = (f32[768]{0:T(1024)S(1)}, f32[768]{0:T(1024)}, u32[]{:S(2)}) copy-start(f32[768]{0:T(1024)} %gain_ref.1) | copy-start | bytes 9220
  54.9 3.2 %copy-start.10 = (f32[768]{0:T(1024)S(1)}, f32[768]{0:T(1024)}, u32[]{:S(2)}) copy-start(f32[768]{0:T(1024)} %param.28) | copy-start | bytes 9220
  55.7 3.1 %slice-start = ((s8[4718592]{0:T(1024)(128)(4,1)}), s8[4194304]{0:T(1024)(128)(4,1)S(1)}, s32[]{:S(2)}) async-start(s8[4718592]{0:T(1024)(128)(4,1)} %bitcast.22), calls=%async_computation | async-start | bytes 8388608
  58.1 1.0 slice-start.1
  58.1 1.0 copy-start.13
  58.1 13.9 %slice-start.2 = ((s8[4718592]{0:T(1024)(128)(4,1)}), s8[4194304]{0:T(1024)(128)(4,1)S(1)}, s32[]{:S(2)}) async-start(s8[4718592]{0:T(1024)(128)(4,1)} %bitcast.24), calls=%async_computation.2 | async-start | bytes 8388608
  58.8 13.1 %copy-start.3 = (bf16[1024,768]{1,0:T(8,128)(2,1)}, bf16[1024,768]{1,0:T(8,128)(2,1)S(1)}, u32[]{:S(2)}) copy-start(bf16[1024,768]{1,0:T(8,128)(2,1)S(1)} %get-tuple-element.73.nl_hbm) | copy-start | bytes 4718596
  58.8 13.1 %copy-start.2 = (f32[1024,768]{1,0:T(8,128)}, f32[1024,768]{1,0:T(8,128)S(1)}, u32[]{:S(2)}) copy-start(f32[1024,768]{1,0:T(8,128)S(1)} %get-tuple-element.74.xh_ref) | copy-start | bytes 9437188
  59.1 12.8 %slice-start.3 = ((s8[4718592]{0:T(1024)(128)(4,1)}), s8[524288]{0:T(1024)(128)(4,1)S(1)}, s32[]{:S(2)}) async-start(s8[4718592]{0:T(1024)(128)(4,1)} %bitcast.24), calls=%async_computation.3 | async-start | bytes 1048576
  59.1 12.9 %copy-start.11 = (f32[768]{0:T(1024)S(1)}, f32[768]{0:T(1024)}, u32[]{:S(2)}) copy-start(f32[768]{0:T(1024)} %param.32) | copy-start | bytes 9220
  71.9 5.4 %copy-start.14 = (bf16[1024,3072]{1,0:T(8,128)(2,1)}, bf16[1024,3072]{1,0:T(8,128)(2,1)S(1)}, u32[]{:S(2)}) copy-start(bf16[1024,3072]{1,0:T(8,128)(2,1)S(1)} %get-tuple-element.76) | copy-start | bytes 18874372
  77.4 1.4 copy-start.5
  77.4 1.4 copy-start.7
  78.8 2.9 copy-start.12
  85.3 12.8 %copy-start.4 = (bf16[1024,768]{1,0:T(8,128)(2,1)}, bf16[1024,768]{1,0:T(8,128)(2,1)S(1)}, u32[]{:S(2)}) copy-start(bf16[1024,768]{1,0:T(8,128)(2,1)S(1)} %get-tuple-element.69.gf_ref) | copy-start | bytes 4718596
  278.8 14.3 %copy-start.6 = (f32[24,768]{1,0:T(8,128)S(1)}, f32[24,768]{1,0:T(8,128)}, u32[]{:S(2)}) copy-start(f32[24,768]{1,0:T(8,128)} %get-tuple-element.48) | copy-start | bytes 221188

commit v5 on v4

--- a/solution.py
+++ b/solution.py
@@ -859,21 +859,22 @@
                 outw_store().start()
 
         def group_steps():
-            for g in range(count):
-                base = plan.outer + plan.per_group * (g + 1)
-                if base < start or base >= stop:
-                    continue
-                phases = (9, 8, 7, 6, 4, 3, 2) if g == count - 1 else (4, 3, 2)
-                for phase in phases:
-                    when = phase - 1 if phase < 5 else phase - 2
-
-                    @pl.when(t == base + when)
+            for place_of in range(count):
+                g = (place_of + 1) % count
+                base = plan.outer + plan.per_group * (place_of + 1)
+                steps = ((4, 5), (3, 3), (2, 1), (1, 0))
+                if place_of == count - 1:
+                    steps = ((9, 7), (8, 6), (7, 5), (6, 4), (4, 3), (3, 2), (2, 1), (1, 0))
+                for phase, later in steps:
+                    if not start <= base + later < stop:
+                        continue
+
+                    @pl.when(t == base + later)
                     def _():
-                        groups.advance(phase, g)
-
-                @pl.when(t == base)
-                def _():
-                    groups.begin(g)
+                        if phase == 1:
+                            groups.begin(g)
+                        else:
+                            groups.advance(phase, g)
 
         first, last = 0, DOWN_EVERY * (half - 1) + span
         window(first, last, lambda: each(0, DOWN_EVERY, half, down_step))
@@ -976,7 +977,8 @@
         at = step - plan.outer
         part = at % 2
         row = (at // 2) % 2
-        group = at // plan.per_group
+        turn = at // plan.per_group
+        group = (turn + 1) % count
         mine = pl.ds(pl.multiple_of(row * LEN, LEN), LEN)
         q = q_ref[0]
         k = k_ref[0]
@@ -1035,7 +1037,7 @@
                     block = wg_acc[:, zl * LANES : (zl + 1) * LANES].astype(BF)
                     qk_own[group, zl] = block.reshape(shape)
 
-            @pl.when(group == count - 1)
+            @pl.when(turn == count - 1)
             def _():
                 total = jnp.where(mask_ref[...] == 1.0, dx[mine, :], 0.0)
                 vec[0, 15:16, :] += jnp.sum(total, axis=0, keepdims=True)
@@ -1103,7 +1105,7 @@
 
     def head_at(s):
         at = jnp.clip(s - plan.outer, 0, plan.end - plan.outer - 1)
-        return at // plan.per_group, (at // 2) % 2
+        return (at // plan.per_group + 1) % count, (at // 2) % 2
 
     def per_head(s):
         group, row = head_at(s)

time: 300 us -> 294 us (0.980)
  Pallas kernels: 244 us -> 238 us
    pallas_call x1, Pallas kernels: 181 us -> 174 us  [late_call(): pl.pallas_call(functools.partial(late_kernel, plan), grid=(plan.end,), in...]
where the time goes in v5:
time: 294 us; the launch traced here: 293 us
  Pallas kernels  238 us (81%)
  matrix products  27.9 us (9%)
  other arithmetic  14.9 us (5%)
  local copies, waits for them, and re-layouts  10.7 us (4%)
    pallas_call x1, Pallas kernels, late_call(): pl.pallas_call(functools.partial(late_kernel, plan), grid=(plan.end,), in...  174 us
    pallas_call x1, Pallas kernels, early_call(): pl.pallas_call(early_kernel, grid=(groups * rows,), in_specs=[pl.BlockSpe...  49.6 us
    dot_general x2, matrix products, dot_nn(): lax.dot_general(left, right, (((1,), (0,)), ((), ())), preferred_element_...  18.2 us
    pallas_call x1, Pallas kernels, final_call(): pl.pallas_call(final_kernel, grid=(steps,), in_specs=[spec(one.shape) for...  14.3 us
    dot_general x1, matrix products, dot_tn(): lax.dot_general(left, right, (((0,), (0,)), ((), ())), preferred_element_...  9.65 us

profile of v5, /device:TPU:0, one launch (start us, length us, event | category | flops | bytes accessed | tf_op | source)
XLA Modules:
  0.0 292.9 jit_solution(7285436570488895688)
XLA Ops:
  0.7 0.0 copy-start.9
  0.7 0.7 compare_convert_fusion
  1.4 1.0 copy.35.mask_ref
  2.4 49.6 %early_kernel.1 = (bf16[4,1024,192]{2,1,0:T(8,128)(2,1)}, bf16[4,1024,192]{2,1,0:T(8,128)(2,1)}, bf16[4,1024,192]{2,1,0:T(8,128)(2,1)}, bf16[4,1024,192]{2,1,0:T...) custom-call(bf16[1024,768]{1,0:T(8,128)(2,1)} %tokens_ref.1, ...), custom_call_target="tpu_custom_call" | custom-call | tf_op jit(solution)/shard_map/early_kernel/pallas_call | solution.py:434
  51.9 0.0 copy-start
  52.0 0.0 copy-start.1
  52.0 0.0 copy-done.9
  52.0 2.9 fusion.11
  54.9 0.0 copy-start.8
  54.9 0.0 copy-start.10
  54.9 0.3 copy-done
  55.3 0.5 copy-done.1
  55.7 0.0 slice-start
  55.7 2.3 fusion.5
  58.1 0.0 copy-done.8
  58.1 0.0 copy-done.10
  58.1 0.0 slice-start.1
  58.1 0.0 copy-start.13
  58.1 0.0 slice-start.2
  58.1 0.7 fusion.10
  58.8 0.0 copy-start.3
  58.8 0.0 copy-start.2
  58.9 0.0 slice-done
  58.9 0.2 slice-done.1
  59.1 0.0 copy-done.13
  59.1 0.0 slice-start.3
  59.1 0.0 copy-start.11
  59.1 12.8 %fusion.3 = (f32[1024,3072]{1,0:T(8,128)}, bf16[1024,3072]{1,0:T(8,128)(2,1)S(1)}) fusion(f32[3072]{0:T(1024)S(1)} %copy-done.13, bf16[1024,768]{1,0:T(8,128)(2,1)S(1)} %get-tuple-element.73.nl_hbm, bf16[768,3072]{1,0:T(8,128)(2,1)S(1)} %bitcast.23), kind=kOutput, calls=%fused_computation.4 | convolution fusion | flops 4866441216 | bytes 25178112 | tf_op jit(solution)/shard_map/dot_general | solution.py:19
  71.9 0.0 copy-done.3
  71.9 0.0 copy-start.14
  71.9 0.0 copy-done.2
  71.9 0.0 slice-done.2
  72.0 0.0 slice-done.3
  72.0 0.0 copy-done.11
  72.0 5.4 %fusion.12 = (f32[1024]{0:T(1024)S(1)}, f32[1024,768]{1,0:T(8,128)S(1)}, f32[1024,768]{1,0:T(8,128)S(1)}) fusion(f32[768]{0:T(1024)S(1)} %copy-done.11, f32[768]{0:T(1024)S(1)} %copy-done.10, f32[1024,768]{1,0:T(8,128)S(1)} %get-tuple-element.74.xh_ref, f32[768]{0:T(1024)S(1)} %copy-done.8, bf16[1024,3072]{1,0:T(8,128)(2,1)S(1)} %get-tuple-element.76, ...), kind=kOutput, calls=%fused_computation.51 | convolution fusion | flops 4835769344 | bytes 20460544 | tf_op jit(solution)/shard_map/dot_general | solution.py:19
  77.4 0.0 copy-done.14
  77.4 0.0 copy-start.5
  77.4 0.0 copy-start.7
  77.4 0.5 multiply_reduce_fusion.2
  78.0 0.8 copy-done.5
  78.8 0.0 copy-done.7
  78.8 0.0 copy-start.12
  78.8 2.9 %multiply_reduce_fusion = (f32[768]{0:T(1024)}, f32[1024]{0:T(1024)S(1)}, f32[1024]{0:T(1024)S(1)}, f32[768]{0:T(1024)}, f32[768]{0:T(1024)}) fusion(bf16[1024,768]{1,0:T(8,128)(2,1)S(1)} %copy-done.5, f32[1024,768]{1,0:T(8,128)S(1)} %get-tuple-element.72, f32[1024]{0:T(1024)S(1)} %convert_element_type.33, f32[1024]{0:T(1024)S(1)} %add_rsqrt_fusion, ...), kind=kLoop, calls=%fused_computation.15 | loop fusion | flops 11792128 | bytes 7900160 | tf_op jit(solution)/shard_map/reduce_sum | solution.py:1401
  81.7 0.0 copy-done.12
  81.7 3.6 %convert_reduce_fusion = (f32[768]{0:T(1024)}, bf16[1024,768]{1,0:T(8,128)(2,1)S(1)}, f32[1024,768]{1,0:T(8,128)}, bf16[1024,768]{1,0:T(8,128)(2,1)}) fusion(f32[1024]{0:T(1024)S(1)} %get-tuple-element.81, f32[1024,768]{1,0:T(8,128)S(1)} %get-tuple-element.72, f32[1024]{0:T(1024)S(1)} %broadcast_multiply_fusion.2, f32[1024]{0:T(1024)S(1)} %get-tuple-element.82, ...), kind=kLoop, calls=%fused_computation.16 | loop fusion | flops 11795712 | bytes 11039744 | tf_op jit(solution)/shard_map/reduce_sum | solution.py:1500
  85.3 0.0 copy-start.4
  85.3 1.3 copy.36.inv_ref
  86.6 0.6 convert_reduce_fusion.1
  87.2 1.2 broadcast_in_dim.8.early_6
  88.5 9.7 %convolution_convert_fusion = bf16[3072,768]{1,0:T(8,128)(2,1)} fusion(bf16[1024,3072]{1,0:T(8,128)(2,1)} %copy-done.14, bf16[1024,768]{1,0:T(8,128)(2,1)S(1)} %get-tuple-element.69.gf_ref), kind=kOutput, calls=%fused_computation.7 | convolution fusion | flops 4834197504 | bytes 12582912 | tf_op jit(solution)/shard_map/dot_general | solution.py:27
  98.1 0.0 copy-done.4
  98.1 174.0 %late_kernel.1 = (f32[24,768]{1,0:T(8,128)}, f32[1024,768]{1,0:T(8,128)}, f32[576,768]{1,0:T(8,128)}, bf16[3,2,2,2,2,4,16,768]{7,6,5,4,3,2,1,0:T(8,128)(2,1)}, b...) custom-call(bf16[1024,768]{1,0:T(8,128)(2,1)} %copy-done.4, ...), custom_call_target="tpu_custom_call" | custom-call | tf_op jit(solution)/shard_map/late_kernel/pallas_call | solution.py:1210
  272.1 0.0 copy-start.6
  272.1 14.3 %final_kernel.1 = (f32[3072,768]{1,0:T(8,128)}, f32[768,3072]{1,0:T(8,128)}, f32[768,768]{1,0:T(8,128)}, f32[1024,768]{1,0:T(8,128)}) custom-call(bf16[3072,768]{1,0:T(8,128)(2,1)} %bitcast.21, bf16[768,3072]{1,0:T(8,128)(2,1)} %get-tuple-element.44.up_ref, bf16[768,768]{1,0:T(8,128)(2,1)} %bitcast.28, f32[1024,768]{1,0:T(8,128)} %get-tuple-element.46.dx_ref, ...), custom_call_target="tpu_custom_call" | custom-call | tf_op jit(solution)/shard_map/final_kernel/pallas_call | solution.py:1271
  286.4 0.0 copy-done.6
  286.4 0.7 slice_reduce_fusion.1
  287.1 0.6 constant_dynamic-slice_fusion
  287.6 0.6 reshape.113
  288.2 0.1 slice_reduce_fusion
  288.4 0.5 slice.39
  289.5 0.5 divide_sqrt_fusion
  290.1 2.8 copy.40
  (9 shorter events, 0.0 us)
Async XLA Ops:
  0.7 51.3 %copy-start.9 = (s32[1024]{0:T(1024)S(1)}, s32[1024]{0:T(1024)}, u32[]{:S(2)}) copy-start(s32[1024]{0:T(1024)} %param.20) | copy-start | bytes 12292
  51.9 3.3 %copy-start = (f32[1024,768]{1,0:T(8,128)S(1)}, f32[1024,768]{1,0:T(8,128)}, u32[]{:S(2)}) copy-start(f32[1024,768]{1,0:T(8,128)} %get-tuple-element.36) | copy-start | bytes 9437188
  52.0 3.8 %copy-start.1 = (bf16[1024,768]{1,0:T(8,128)(2,1)S(1)}, bf16[1024,768]{1,0:T(8,128)(2,1)}, u32[]{:S(2)}) copy-start(bf16[1024,768]{1,0:T(8,128)(2,1)} %get-tuple-element.35.x_hbm) | copy-start | bytes 4718596
  54.9 3.2 %copy-start.8 = (f32[768]{0:T(1024)S(1)}, f32[768]{0:T(1024)}, u32[]{:S(2)}) copy-start(f32[768]{0:T(1024)} %gain_ref.1) | copy-start | bytes 9220
  54.9 3.2 %copy-start.10 = (f32[768]{0:T(1024)S(1)}, f32[768]{0:T(1024)}, u32[]{:S(2)}) copy-start(f32[768]{0:T(1024)} %param.28) | copy-start | bytes 9220
  55.7 3.1 %slice-start = ((s8[4718592]{0:T(1024)(128)(4,1)}), s8[4194304]{0:T(1024)(128)(4,1)S(1)}, s32[]{:S(2)}) async-start(s8[4718592]{0:T(1024)(128)(4,1)} %bitcast.22), calls=%async_computation | async-start | bytes 8388608
  58.1 1.0 slice-start.1
  58.1 1.0 copy-start.13
  58.1 13.9 %slice-start.2 = ((s8[4718592]{0:T(1024)(128)(4,1)}), s8[4194304]{0:T(1024)(128)(4,1)S(1)}, s32[]{:S(2)}) async-start(s8[4718592]{0:T(1024)(128)(4,1)} %bitcast.24), calls=%async_computation.2 | async-start | bytes 8388608
  58.8 13.1 %copy-start.3 = (bf16[1024,768]{1,0:T(8,128)(2,1)}, bf16[1024,768]{1,0:T(8,128)(2,1)S(1)}, u32[]{:S(2)}) copy-start(bf16[1024,768]{1,0:T(8,128)(2,1)S(1)} %get-tuple-element.73.nl_hbm) | copy-start | bytes 4718596
  58.8 13.1 %copy-start.2 = (f32[1024,768]{1,0:T(8,128)}, f32[1024,768]{1,0:T(8,128)S(1)}, u32[]{:S(2)}) copy-start(f32[1024,768]{1,0:T(8,128)S(1)} %get-tuple-element.74.xh_ref) | copy-start | bytes 9437188
  59.1 12.8 %slice-start.3 = ((s8[4718592]{0:T(1024)(128)(4,1)}), s8[524288]{0:T(1024)(128)(4,1)S(1)}, s32[]{:S(2)}) async-start(s8[4718592]{0:T(1024)(128)(4,1)} %bitcast.24), calls=%async_computation.3 | async-start | bytes 1048576
  59.1 12.9 %copy-start.11 = (f32[768]{0:T(1024)S(1)}, f32[768]{0:T(1024)}, u32[]{:S(2)}) copy-start(f32[768]{0:T(1024)} %param.32) | copy-start | bytes 9220
  71.9 5.4 %copy-start.14 = (bf16[1024,3072]{1,0:T(8,128)(2,1)}, bf16[1024,3072]{1,0:T(8,128)(2,1)S(1)}, u32[]{:S(2)}) copy-start(bf16[1024,3072]{1,0:T(8,128)(2,1)S(1)} %get-tuple-element.76) | copy-start | bytes 18874372
  77.4 1.4 copy-start.5
  77.4 1.4 copy-start.7
  78.8 2.9 %copy-start.12 = (f32[768]{0:T(1024)S(1)}, f32[768]{0:T(1024)}, u32[]{:S(2)}) copy-start(f32[768]{0:T(1024)} %param.34) | copy-start | bytes 9220
  85.3 12.8 %copy-start.4 = (bf16[1024,768]{1,0:T(8,128)(2,1)}, bf16[1024,768]{1,0:T(8,128)(2,1)S(1)}, u32[]{:S(2)}) copy-start(bf16[1024,768]{1,0:T(8,128)(2,1)S(1)} %get-tuple-element.69.gf_ref) | copy-start | bytes 4718596
  272.1 14.3 %copy-start.6 = (f32[24,768]{1,0:T(8,128)S(1)}, f32[24,768]{1,0:T(8,128)}, u32[]{:S(2)}) copy-start(f32[24,768]{1,0:T(8,128)} %get-tuple-element.48) | copy-start | bytes 221188
